TPU v7x, 32 devices: a whole 2x2x4 slice. The times are simulated.
32 devices in a mesh: py: 2 (over y), px: 4 (over x, core), pz: 4 (over z).
Axes of the slice: x: 2, y: 2, z: 4, core: 2. Of those that a mesh axis runs over, the one named last changes fastest.
Arguments:
- tracer: float32 [32, 512, 32, 128], P('py', 'px', 'pz'), may hold values from 0.2 to 1.8
- conductance: float32 [32, 512, 32, 128], P('py', 'px', 'pz'), may hold values from 0.03 to 0.15
- source: float32 [32, 512, 32, 128], P('py', 'px', 'pz'), may hold values from -0.2 to 0.2
Outputs:
- potential: float32 [32, 512, 32, 128], P('py', 'px', 'pz')
- tracer_end: float32 [32, 512, 32, 128], P('py', 'px', 'pz')
All inputs are finite; a program needn't handle non-finite values.
Results may differ from a plain program's by a relative error of at most 0.00002.
Values sent between devices are 32-bit elements; how exact they have to be, the bound alone decides.
No kernel may reach another device: no remote copies, remote signals or barrier semaphores. Data moves between devices by JAX's collectives and lax.ppermute only.
A program may use at most 320 MiB of HBM per device.

v0:
```python
import jax
import jax.numpy as jnp
from jax import lax
from jax.sharding import PartitionSpec as P

STEPS = 4


def padded_2(block, sides, width):
    for axis, dim in sides:
        count = lax.axis_size(axis)
        forward = [(i, i + 1) for i in range(count - 1)]
        forward.append((count - 1, 0))
        backward = [(target, source) for source, target in forward]
        low = lax.ppermute(
            lax.slice_in_dim(block, block.shape[dim] - width, None, axis=dim), axis, forward
        )
        high = lax.ppermute(lax.slice_in_dim(block, 0, width, axis=dim), axis, backward)
        block = jnp.concatenate([low, block, high], axis=dim)
    return block


def entering(value, axis, join, neutral):
    count, mine = (lax.axis_size(axis), lax.axis_index(axis))
    pieces = lax.all_gather(value, axis)
    so_far = jnp.full_like(value, 0) + jnp.asarray(neutral, value.dtype)

    def hop(position, so_far):
        longer = join(so_far, pieces[position])
        return jnp.where(position < mine, longer, so_far)

    return lax.fori_loop(0, count - 1, hop, so_far)


def strip_edges(values, dims):
    for dim in dims:
        values = lax.slice_in_dim(values, 1, values.shape[dim] - 1, axis=dim)
    return values


def neighbour(values, dim, start, dims):
    others = [other for other in dims if other != dim]
    values = strip_edges(values, others)
    return lax.slice_in_dim(values, start, start + values.shape[dim] - 2, axis=dim)


def one_step(padded, conductance, source):
    middle = strip_edges(padded, (0, 1, 2))
    lower = [neighbour(padded, dim, 0, (0, 1, 2)) for dim in (0, 1, 2)]
    upper = [neighbour(padded, dim, 2, (0, 1, 2)) for dim in (0, 1, 2)]
    spread = lower[0] + upper[0] + lower[1] + upper[1] + lower[2] + upper[2] - 6.0 * middle
    return middle + conductance * spread + source


def on_device(tracer, conductance, source):
    for step in range(STEPS):
        padded = padded_2(tracer, (("py", 0), ("px", 1), ("pz", 2)), 1)
        tracer = one_step(padded, conductance, source)
    here = jnp.cumsum(tracer, axis=2)
    total = lax.slice_in_dim(here, here.shape[2] - 1, here.shape[2], axis=2)

    def add_pair(earlier_total, later_total):
        return earlier_total + later_total

    below = entering(total, "pz", add_pair, jnp.zeros_like(total))
    potential = (here + below) / (tracer.shape[2] * lax.axis_size("pz"))
    return (potential, tracer)


def solution(mesh):
    placed = (P("py", "px", "pz", None), P("py", "px", "pz", None), P("py", "px", "pz", None))
    return jax.shard_map(
        on_device,
        mesh=mesh,
        in_specs=placed,
        out_specs=(P("py", "px", "pz", None), P("py", "px", "pz", None)),
        check_vma=False,
    )
```

profile of v0, /device:TPU:0, one launch (start us, length us, event | category | flops | bytes accessed | tf_op | source)
XLA Modules:
  0.0 1174.0 jit_solution(1236503037858312687)
XLA Ops:
  7.2 1.3 fusion.40
  8.5 3.1 collective-permute-start
  11.6 12.7 %collective-permute-done = f32[1,128,8,128]{3,2,1,0:T(8,128)S(1)} collective-permute-done((f32[1,128,8,128]{3,2,1,0:T(8,128)S(1)}, f32[1,128,8,128]{3,2,1,0:T(8,128)S(1)}, u32[]{:S(2)}, u32[]{:S(2)}) %collective-permute-start) | collective-permute-done | bytes 524320 | tf_op jit(solution)/shard_map/ppermute | solution.py:15
  24.4 4.0 constant_dynamic-update-slice_fusion.1
  28.4 6.3 collective-permute-done.1
  34.8 1.7 collective-permute-start.3
  36.6 2.0 collective-permute-done.2
  38.6 1.9 pad_maximum_fusion.81
  40.6 3.9 collective-permute-start.5
  44.6 27.2 %collective-permute-done.5 = f32[18,130,1,128]{3,1,2,0:T(8,128)S(1)} collective-permute-done((f32[18,130,1,128]{3,1,2,0:T(8,128)S(1)}, f32[18,130,1,128]{3,1,2,0:T(8,128)S(1)}, u32[]{:S(2)}, u32[]{:S(2)}) %collective-permute-start.5) | collective-permute-done | bytes 1198112 | tf_op jit(solution)/shard_map/ppermute | solution.py:18
  71.8 1.2 copy.27
  73.0 26.5 %collective-permute-done.4 = f32[18,130,1,128]{3,1,2,0:T(8,128)S(1)} collective-permute-done((f32[18,130,1,128]{3,1,2,0:T(8,128)S(1)}, f32[18,130,1,128]{3,1,2,0:T(8,128)S(1)}, u32[]{:S(2)}, u32[]{:S(2)}) %collective-permute-start.4) | collective-permute-done | bytes 1198112 | tf_op jit(solution)/shard_map/ppermute | solution.py:15
  99.5 1.2 copy.25
  100.8 26.9 %fusion.31 = f32[16,128,8,128]{3,2,1,0:T(8,128)S(1)} fusion(f32[16,128,8,128]{3,2,1,0:T(8,128)} %param.7, f32[16,128,8,128]{3,2,1,0:T(8,128)} %param.5, f32[16,128,8,128]{3,2,1,0:T(8,128)} %param.6, f32[18,130,1,128]{3,2,1,0:T(1,128)S(1)} %copy.27, f32[18,1,8,128]{3,2,1,0:T(8,128)S(1)} %collective-permute-done.3, f32[18,128,8,128]{3,2,1,0:T(8,128)} %copy-done.2, ...), kind=kLoop, calls=%fused_computation.89 | loop fusion | flops 41943040 | bytes 46583808 | tf_op jit(solution)/shard_map/add | solution.py:52
  127.7 1.6 collective-permute-start.6
  129.8 12.8 %collective-permute-done.6 = f32[1,128,8,128]{3,2,1,0:T(8,128)S(1)} collective-permute-done((f32[1,128,8,128]{3,2,1,0:T(8,128)S(1)}, f32[1,128,8,128]{3,2,1,0:T(8,128)S(1)}, u32[]{:S(2)}, u32[]{:S(2)}) %collective-permute-start.6) | collective-permute-done | bytes 524320 | tf_op jit(solution)/shard_map/ppermute | solution.py:15
  142.6 10.7 collective-permute-done.7
  153.4 1.7 collective-permute-start.9
  155.1 2.0 collective-permute-done.8
  157.1 2.8 pad_maximum_fusion.78
  160.1 2.2 collective-permute-start.11
  162.6 27.7 %collective-permute-done.11 = f32[18,130,1,128]{3,1,2,0:T(8,128)S(1)} collective-permute-done((f32[18,130,1,128]{3,1,2,0:T(8,128)S(1)}, f32[18,130,1,128]{3,1,2,0:T(8,128)S(1)}, u32[]{:S(2)}, u32[]{:S(2)}) %collective-permute-start.11) | collective-permute-done | bytes 1198112 | tf_op jit(solution)/shard_map/ppermute | solution.py:18
  190.3 1.2 copy.31
  191.5 26.3 %collective-permute-done.10 = f32[18,130,1,128]{3,1,2,0:T(8,128)S(1)} collective-permute-done((f32[18,130,1,128]{3,1,2,0:T(8,128)S(1)}, f32[18,130,1,128]{3,1,2,0:T(8,128)S(1)}, u32[]{:S(2)}, u32[]{:S(2)}) %collective-permute-start.10) | collective-permute-done | bytes 1198112 | tf_op jit(solution)/shard_map/ppermute | solution.py:15
  217.8 2.3 copy.29
  220.1 13.7 %fusion.22 = f32[16,128,8,128]{3,2,1,0:T(8,128)} fusion(f32[16,128,8,128]{3,2,1,0:T(8,128)} %param.7, f32[16,128,8,128]{3,2,1,0:T(8,128)S(1)} %fusion.31, f32[16,128,8,128]{3,2,1,0:T(8,128)} %param.6, f32[18,130,1,128]{3,2,1,0:T(1,128)S(1)} %copy.31, f32[18,1,8,128]{3,2,1,0:T(8,128)S(1)} %collective-permute-done.9, ...), kind=kLoop, calls=%fused_computation.62 | loop fusion | flops 58720256 | bytes 37146624 | tf_op jit(solution)/shard_map/add | solution.py:52
  233.8 1.4 fusion.38
  235.2 1.6 collective-permute-start.12
  237.3 12.8 %collective-permute-done.12 = f32[1,128,8,128]{3,2,1,0:T(8,128)S(1)} collective-permute-done((f32[1,128,8,128]{3,2,1,0:T(8,128)S(1)}, f32[1,128,8,128]{3,2,1,0:T(8,128)S(1)}, u32[]{:S(2)}, u32[]{:S(2)}) %collective-permute-start.12) | collective-permute-done | bytes 524320 | tf_op jit(solution)/shard_map/ppermute | solution.py:15
  250.1 10.0 collective-permute-done.13
  260.1 1.0 pad_maximum_fusion.87
  261.2 1.7 collective-permute-start.15
  262.9 2.0 collective-permute-done.14
  265.0 2.8 pad_maximum_fusion.73
  267.9 2.7 collective-permute-start.17
  270.9 27.7 %collective-permute-done.17 = f32[18,130,1,128]{3,1,2,0:T(8,128)S(1)} collective-permute-done((f32[18,130,1,128]{3,1,2,0:T(8,128)S(1)}, f32[18,130,1,128]{3,1,2,0:T(8,128)S(1)}, u32[]{:S(2)}, u32[]{:S(2)}) %collective-permute-start.17) | collective-permute-done | bytes 1198112 | tf_op jit(solution)/shard_map/ppermute | solution.py:18
  298.7 1.2 copy.35
  299.9 27.6 %collective-permute-done.16 = f32[18,130,1,128]{3,1,2,0:T(8,128)S(1)} collective-permute-done((f32[18,130,1,128]{3,1,2,0:T(8,128)S(1)}, f32[18,130,1,128]{3,1,2,0:T(8,128)S(1)}, u32[]{:S(2)}, u32[]{:S(2)}) %collective-permute-start.16) | collective-permute-done | bytes 1198112 | tf_op jit(solution)/shard_map/ppermute | solution.py:15
  327.5 2.3 copy.33
  329.8 13.7 %fusion.13 = f32[16,128,8,128]{3,2,1,0:T(8,128)} fusion(f32[16,128,8,128]{3,2,1,0:T(8,128)} %param.7, f32[16,128,8,128]{3,2,1,0:T(8,128)S(1)} %copy-done, f32[16,128,8,128]{3,2,1,0:T(8,128)} %param.6, f32[18,130,1,128]{3,2,1,0:T(1,128)S(1)} %copy.35, f32[18,1,8,128]{3,2,1,0:T(8,128)S(1)} %collective-permute-done.15, ...), kind=kLoop, calls=%fused_computation.35 | loop fusion | flops 58720256 | bytes 37146624 | tf_op jit(solution)/shard_map/add | solution.py:52
  343.5 1.4 fusion.37
  344.9 1.6 collective-permute-start.18
  347.0 12.8 %collective-permute-done.18 = f32[1,128,8,128]{3,2,1,0:T(8,128)S(1)} collective-permute-done((f32[1,128,8,128]{3,2,1,0:T(8,128)S(1)}, f32[1,128,8,128]{3,2,1,0:T(8,128)S(1)}, u32[]{:S(2)}, u32[]{:S(2)}) %collective-permute-start.18) | collective-permute-done | bytes 524320 | tf_op jit(solution)/shard_map/ppermute | solution.py:15
  359.8 10.3 collective-permute-done.19
  371.1 1.7 collective-permute-start.21
  372.9 2.0 collective-permute-done.20
  374.9 2.8 pad_maximum_fusion.68
  377.9 1.7 collective-permute-start.23
  380.1 27.9 %collective-permute-done.23 = f32[18,130,1,128]{3,1,2,0:T(8,128)S(1)} collective-permute-done((f32[18,130,1,128]{3,1,2,0:T(8,128)S(1)}, f32[18,130,1,128]{3,1,2,0:T(8,128)S(1)}, u32[]{:S(2)}, u32[]{:S(2)}) %collective-permute-start.23) | collective-permute-done | bytes 1198112 | tf_op jit(solution)/shard_map/ppermute | solution.py:18
  408.0 1.2 copy.39
  409.2 26.6 %collective-permute-done.22 = f32[18,130,1,128]{3,1,2,0:T(8,128)S(1)} collective-permute-done((f32[18,130,1,128]{3,1,2,0:T(8,128)S(1)}, f32[18,130,1,128]{3,1,2,0:T(8,128)S(1)}, u32[]{:S(2)}, u32[]{:S(2)}) %collective-permute-start.22) | collective-permute-done | bytes 1198112 | tf_op jit(solution)/shard_map/ppermute | solution.py:15
  435.8 2.3 copy.37
  438.0 13.7 %fusion.4 = f32[16,128,8,128]{3,2,1,0:T(8,128)} fusion(f32[16,128,8,128]{3,2,1,0:T(8,128)} %param.7, f32[16,128,8,128]{3,2,1,0:T(8,128)S(1)} %copy-done.1, f32[16,128,8,128]{3,2,1,0:T(8,128)} %param.6, f32[18,130,1,128]{3,2,1,0:T(1,128)S(1)} %copy.39, f32[18,1,8,128]{3,2,1,0:T(8,128)S(1)} %collective-permute-done.21, ...), kind=kLoop, calls=%fused_computation.8 | loop fusion | flops 58720256 | bytes 37146624 | tf_op jit(solution)/shard_map/add | solution.py:52
  451.7 612.0 %reduce_window_sum.11 = f32[16,128,8,128]{3,2,1,0:T(8,128)} reduce-window(f32[16,128,8,128]{3,2,1,0:T(8,128)} %fusion.4, f32[]{:T(128)} %constant.34.clone.1), window={size=1x1x8x1 pad=0_0x0_0x7_0x0_0}, to_apply=%region_0.0 | reduce-window | flops 14680064 | bytes 16777220 | tf_op jit(solution)/shard_map/jit(cumsum)/reduce_window_sum | solution.py:59
  1063.7 5.6 slice.360
  1069.3 80.4 %all-gather.3.cloned.1.call-done = f32[64,128,1,128]{3,1,2,0:T(8,128)} async-done(((f32[16,128,1,128]{3,1,2,0:T(8,128)}), f32[64,128,1,128]{3,1,2,0:T(8,128)}) %all-gather.3.cloned.1.call-update) | async-done | bytes 4194320 | tf_op jit(solution)/shard_map/all_gather | solution.py:25
  1149.7 9.2 while.14
  1149.7 1.3 constant_dynamic-slice_fusion.2
  1151.0 1.7 broadcast_select_fusion.3
  1152.7 1.3 constant_dynamic-slice_fusion.2
  1154.1 1.7 broadcast_select_fusion.3
  1155.8 1.3 constant_dynamic-slice_fusion.2
  1157.1 1.7 broadcast_select_fusion.3
  1158.9 7.8 add_multiply_fusion
  (51 shorter events, 4.6 us)
Async XLA Ops:
  7.2 1142.5 %all-gather.3.cloned.1.call-start = ((), (), s32[]{:S(2)}) async-start(), calls=%async_computation | async-start | bytes 5242880 | tf_op jit(solution)/shard_map/all_gather | solution.py:25
  8.5 15.8 %collective-permute-start = (f32[1,128,8,128]{3,2,1,0:T(8,128)S(1)}, f32[1,128,8,128]{3,2,1,0:T(8,128)S(1)}, u32[]{:S(2)}, u32[]{:S(2)}) collective-permute-start(f32[1,128,8,128]{3,2,1,0:T(8,128)S(1)} %get-tuple-element.142), channel_id=1, source_target_pairs={{0,16},{16,0},{1,17},{17,1},{2,18},{18,2},{3,19},{19,3},{4,20},{20... | collective-permute-start | bytes 1572872 | tf_op jit(solution)/shard_map/ppermute | solution.py:15
  11.5 23.2 %collective-permute-start.1 = (f32[1,128,8,128]{3,2,1,0:T(8,128)S(1)}, f32[1,128,8,128]{3,2,1,0:T(8,128)S(1)}, u32[]{:S(2)}, u32[]{:S(2)}) collective-permute-start(f32[1,128,8,128]{3,2,1,0:T(8,128)S(1)} %get-tuple-element.141), channel_id=1, source_target_pairs={{16,0},{0,16},{17,1},{1,17},{18,2},{2,18},{19,3},{3,19},{20,4},{4,... | collective-permute-start | bytes 1572872 | tf_op jit(solution)/shard_map/ppermute | solution.py:18
  34.7 9.8 copy-start.2
  34.8 3.8 collective-permute-start.2
  34.8 3.8 collective-permute-start.3
  40.6 31.2 %collective-permute-start.5 = (f32[18,130,1,128]{3,1,2,0:T(8,128)S(1)}, f32[18,130,1,128]{3,1,2,0:T(8,128)S(1)}, u32[]{:S(2)}, u32[]{:S(2)}) collective-permute-start(f32[18,130,1,128]{3,1,2,0:T(8,128)S(1)} %copy.26), channel_id=1, source_target_pairs={{1,0},{2,1},{3,2},{0,3},{5,4},{6,5},{7,6},{4,7},{9,8},{10,9},{11,1... | collective-permute-start | bytes 3594248 | tf_op jit(solution)/shard_map/ppermute | solution.py:18
  44.5 55.0 %collective-permute-start.4 = (f32[18,130,1,128]{3,1,2,0:T(8,128)S(1)}, f32[18,130,1,128]{3,1,2,0:T(8,128)S(1)}, u32[]{:S(2)}, u32[]{:S(2)}) collective-permute-start(f32[18,130,1,128]{3,1,2,0:T(8,128)S(1)} %copy.24), channel_id=1, source_target_pairs={{0,1},{1,2},{2,3},{3,0},{4,5},{5,6},{6,7},{7,4},{8,9},{9,10},{10,1... | collective-permute-start | bytes 3594248 | tf_op jit(solution)/shard_map/ppermute | solution.py:15
  127.7 14.9 %collective-permute-start.6 = (f32[1,128,8,128]{3,2,1,0:T(8,128)S(1)}, f32[1,128,8,128]{3,2,1,0:T(8,128)S(1)}, u32[]{:S(2)}, u32[]{:S(2)}) collective-permute-start(f32[1,128,8,128]{3,2,1,0:T(8,128)S(1)} %get-tuple-element.139), channel_id=1, source_target_pairs={{0,16},{16,0},{1,17},{17,1},{2,18},{18,2},{3,19},{19,3},{4,20},{20... | collective-permute-start | bytes 1572872 | tf_op jit(solution)/shard_map/ppermute | solution.py:15
  129.3 24.0 %collective-permute-start.7 = (f32[1,128,8,128]{3,2,1,0:T(8,128)S(1)}, f32[1,128,8,128]{3,2,1,0:T(8,128)S(1)}, u32[]{:S(2)}, u32[]{:S(2)}) collective-permute-start(f32[1,128,8,128]{3,2,1,0:T(8,128)S(1)} %get-tuple-element.140), channel_id=1, source_target_pairs={{16,0},{0,16},{17,1},{1,17},{18,2},{2,18},{19,3},{3,19},{20,4},{4,... | collective-permute-start | bytes 1572872 | tf_op jit(solution)/shard_map/ppermute | solution.py:18
  142.6 17.4 %copy-start.3 = (f32[1,128,8,128]{3,2,1,0:T(8,128)}, f32[1,128,8,128]{3,2,1,0:T(8,128)S(1)}, u32[]{:S(2)}) copy-start(f32[1,128,8,128]{3,2,1,0:T(8,128)S(1)} %collective-permute-done.6) | copy-start | bytes 1572868
  153.3 6.7 copy-start.6
  153.3 3.8 collective-permute-start.8
  153.4 3.8 collective-permute-start.9
  160.1 30.2 %collective-permute-start.11 = (f32[18,130,1,128]{3,1,2,0:T(8,128)S(1)}, f32[18,130,1,128]{3,1,2,0:T(8,128)S(1)}, u32[]{:S(2)}, u32[]{:S(2)}) collective-permute-start(f32[18,130,1,128]{3,1,2,0:T(8,128)S(1)} %copy.30), channel_id=1, source_target_pairs={{1,0},{2,1},{3,2},{0,3},{5,4},{6,5},{7,6},{4,7},{9,8},{10,9},{11,1... | collective-permute-start | bytes 3594248 | tf_op jit(solution)/shard_map/ppermute | solution.py:18
  162.4 55.4 %collective-permute-start.10 = (f32[18,130,1,128]{3,1,2,0:T(8,128)S(1)}, f32[18,130,1,128]{3,1,2,0:T(8,128)S(1)}, u32[]{:S(2)}, u32[]{:S(2)}) collective-permute-start(f32[18,130,1,128]{3,1,2,0:T(8,128)S(1)} %copy.28), channel_id=1, source_target_pairs={{0,1},{1,2},{2,3},{3,0},{4,5},{5,6},{6,7},{7,4},{8,9},{9,10},{10,1... | collective-permute-start | bytes 3594248 | tf_op jit(solution)/shard_map/ppermute | solution.py:15
  233.8 31.2 %copy-start = (f32[16,128,8,128]{3,2,1,0:T(8,128)S(1)}, f32[16,128,8,128]{3,2,1,0:T(8,128)}, u32[]{:S(2)}) copy-start(f32[16,128,8,128]{3,2,1,0:T(8,128)} %fusion.22) | copy-start | bytes 25165828
  235.2 14.9 %collective-permute-start.12 = (f32[1,128,8,128]{3,2,1,0:T(8,128)S(1)}, f32[1,128,8,128]{3,2,1,0:T(8,128)S(1)}, u32[]{:S(2)}, u32[]{:S(2)}) collective-permute-start(f32[1,128,8,128]{3,2,1,0:T(8,128)S(1)} %get-tuple-element.137), channel_id=1, source_target_pairs={{0,16},{16,0},{1,17},{17,1},{2,18},{18,2},{3,19},{19,3},{4,20},{20... | collective-permute-start | bytes 1572872 | tf_op jit(solution)/shard_map/ppermute | solution.py:15
  236.8 23.3 %collective-permute-start.13 = (f32[1,128,8,128]{3,2,1,0:T(8,128)S(1)}, f32[1,128,8,128]{3,2,1,0:T(8,128)S(1)}, u32[]{:S(2)}, u32[]{:S(2)}) collective-permute-start(f32[1,128,8,128]{3,2,1,0:T(8,128)S(1)} %get-tuple-element.138), channel_id=1, source_target_pairs={{16,0},{0,16},{17,1},{1,17},{18,2},{2,18},{19,3},{3,19},{20,4},{4,... | collective-permute-start | bytes 1572872 | tf_op jit(solution)/shard_map/ppermute | solution.py:18
  250.1 17.7 %copy-start.4 = (f32[1,128,8,128]{3,2,1,0:T(8,128)}, f32[1,128,8,128]{3,2,1,0:T(8,128)S(1)}, u32[]{:S(2)}) copy-start(f32[1,128,8,128]{3,2,1,0:T(8,128)S(1)} %collective-permute-done.12) | copy-start | bytes 1572868
  260.1 7.7 copy-start.7
  261.1 3.8 collective-permute-start.14
  261.2 3.8 collective-permute-start.15
  267.9 30.7 %collective-permute-start.17 = (f32[18,130,1,128]{3,1,2,0:T(8,128)S(1)}, f32[18,130,1,128]{3,1,2,0:T(8,128)S(1)}, u32[]{:S(2)}, u32[]{:S(2)}) collective-permute-start(f32[18,130,1,128]{3,1,2,0:T(8,128)S(1)} %copy.34), channel_id=1, source_target_pairs={{1,0},{2,1},{3,2},{0,3},{5,4},{6,5},{7,6},{4,7},{9,8},{10,9},{11,1... | collective-permute-start | bytes 3594248 | tf_op jit(solution)/shard_map/ppermute | solution.py:18
  270.8 56.7 %collective-permute-start.16 = (f32[18,130,1,128]{3,1,2,0:T(8,128)S(1)}, f32[18,130,1,128]{3,1,2,0:T(8,128)S(1)}, u32[]{:S(2)}, u32[]{:S(2)}) collective-permute-start(f32[18,130,1,128]{3,1,2,0:T(8,128)S(1)} %copy.32), channel_id=1, source_target_pairs={{0,1},{1,2},{2,3},{3,0},{4,5},{5,6},{6,7},{7,4},{8,9},{9,10},{10,1... | collective-permute-start | bytes 3594248 | tf_op jit(solution)/shard_map/ppermute | solution.py:15
  343.5 31.4 %copy-start.1 = (f32[16,128,8,128]{3,2,1,0:T(8,128)S(1)}, f32[16,128,8,128]{3,2,1,0:T(8,128)}, u32[]{:S(2)}) copy-start(f32[16,128,8,128]{3,2,1,0:T(8,128)} %fusion.13) | copy-start | bytes 25165828
  344.9 14.9 %collective-permute-start.18 = (f32[1,128,8,128]{3,2,1,0:T(8,128)S(1)}, f32[1,128,8,128]{3,2,1,0:T(8,128)S(1)}, u32[]{:S(2)}, u32[]{:S(2)}) collective-permute-start(f32[1,128,8,128]{3,2,1,0:T(8,128)S(1)} %get-tuple-element.135), channel_id=1, source_target_pairs={{0,16},{16,0},{1,17},{17,1},{2,18},{18,2},{3,19},{19,3},{4,20},{20... | collective-permute-start | bytes 1572872 | tf_op jit(solution)/shard_map/ppermute | solution.py:15
  346.5 23.6 %collective-permute-start.19 = (f32[1,128,8,128]{3,2,1,0:T(8,128)S(1)}, f32[1,128,8,128]{3,2,1,0:T(8,128)S(1)}, u32[]{:S(2)}, u32[]{:S(2)}) collective-permute-start(f32[1,128,8,128]{3,2,1,0:T(8,128)S(1)} %get-tuple-element.136), channel_id=1, source_target_pairs={{16,0},{0,16},{17,1},{1,17},{18,2},{2,18},{19,3},{3,19},{20,4},{4,... | collective-permute-start | bytes 1572872 | tf_op jit(solution)/shard_map/ppermute | solution.py:18
  359.8 18.0 %copy-start.5 = (f32[1,128,8,128]{3,2,1,0:T(8,128)}, f32[1,128,8,128]{3,2,1,0:T(8,128)S(1)}, u32[]{:S(2)}) copy-start(f32[1,128,8,128]{3,2,1,0:T(8,128)S(1)} %collective-permute-done.18) | copy-start | bytes 1572868
  370.1 7.7 copy-start.8
  371.1 3.8 collective-permute-start.20
  371.1 3.8 collective-permute-start.21
  377.9 30.1 %collective-permute-start.23 = (f32[18,130,1,128]{3,1,2,0:T(8,128)S(1)}, f32[18,130,1,128]{3,1,2,0:T(8,128)S(1)}, u32[]{:S(2)}, u32[]{:S(2)}) collective-permute-start(f32[18,130,1,128]{3,1,2,0:T(8,128)S(1)} %copy.38), channel_id=1, source_target_pairs={{1,0},{2,1},{3,2},{0,3},{5,4},{6,5},{7,6},{4,7},{9,8},{10,9},{11,1... | collective-permute-start | bytes 3594248 | tf_op jit(solution)/shard_map/ppermute | solution.py:18
  379.7 56.1 %collective-permute-start.22 = (f32[18,130,1,128]{3,1,2,0:T(8,128)S(1)}, f32[18,130,1,128]{3,1,2,0:T(8,128)S(1)}, u32[]{:S(2)}, u32[]{:S(2)}) collective-permute-start(f32[18,130,1,128]{3,1,2,0:T(8,128)S(1)} %copy.36), channel_id=1, source_target_pairs={{0,1},{1,2},{2,3},{3,0},{4,5},{5,6},{6,7},{7,4},{8,9},{9,10},{10,1... | collective-permute-start | bytes 3594248 | tf_op jit(solution)/shard_map/ppermute | solution.py:15
Sparse Core Ops, SparseCore 0:
  1069.4 80.2 all-gather.2
where the time goes:
time: 1190 us; the launch traced here: 1170 us
  other arithmetic  705 us (59%)
  waiting for transfers between devices  394 us (33%)
  local copies, waits for them, and re-layouts  31.4 us (3%)
  starting transfers between devices  28 us (2%)
  between operations  14.8 us (1%)
    another operation x1, other arithmetic, on_device(): here = jnp.cumsum(tracer, axis=2)  612 us
    ppermute x12, waiting for transfers between devices, padded_2(): lax.ppermute(lax.slice_in_dim(block, block.shape[dim] - width, None, axis...  166 us
    ppermute x12, waiting for transfers between devices, padded_2(): lax.ppermute(lax.slice_in_dim(block, 0, width, axis=dim), axis, backward)  148 us
    all_gather x1, waiting for transfers between devices, entering(): pieces = lax.all_gather(value, axis)  80.4 us
    add x4, other arithmetic, one_step(): return middle + conductance * spread + source  68 us
  transfers between devices with their start and end apart: 25, of which 21 were waited for; matrix products, arithmetic and copies ran while one was open for 1% of the time, Pallas kernels for 0%

commit v1 on v0

v1 whole, which is shorter than its diff:
```python
import math

import jax
import jax.numpy as jnp
from jax import lax
from jax.experimental import pallas as pl
from jax.experimental.pallas import tpu as pltpu
from jax.sharding import PartitionSpec as P


STEPS = 4
LANES = 8
SHARES = (5, 5, 4, 2)
GROUPS = 4
VMEM_LIMIT = 20 * 1024 * 1024


HBM = pl.BlockSpec(memory_space=pltpu.HBM)
VMEM = pl.BlockSpec(memory_space=pltpu.VMEM)


def pieces_of(width):
    tiles = width // LANES
    total = sum(SHARES)
    ends = [tiles * sum(SHARES[: i + 1]) // total for i in range(len(SHARES))]
    starts = [0] + ends[:-1]
    return [(a * LANES, (b - a) * LANES) for a, b in zip(starts, ends) if b > a]


def groups_of(planes):
    count = math.gcd(planes, GROUPS)
    return count, planes // count


def prepare_kernel(first, width, depth, lead, trail, tracer, *refs):
    refs = refs[len(refs) - (5 + lead + trail) :]
    bottom, top, rows = refs[:3]
    edges = refs[3 : 3 + lead + trail]
    block, sem_in = refs[3 + lead + trail :]
    planes = block.shape[0]
    count, each = groups_of(planes)

    def load(g):
        return pltpu.make_async_copy(
            tracer.at[pl.ds(g * each, each), pl.ds(first * depth, width * depth)],
            block.at[pl.ds(g * each, each)],
            sem_in.at[g],
        )

    for g in range(count):
        load(g).start()
    for g in range(count):
        load(g).wait()
        take_rows(block, bottom, top, g * each, each, width, depth)
    take_sides(block, rows, edges, lead, trail, width, depth)


def take_sides(block, rows, edges, lead, trail, width, depth):
    planes = block.shape[0]
    rows[0] = block[planes - 1]
    rows[1] = block[0]
    columns = ([0] if lead else []) + ([width - 1] if trail else [])
    for column, edge in zip(columns, edges):
        edge[...] = block[:, pl.ds(column * depth, depth), :]


def take_rows(block, low, high, start, planes, width, depth):
    across = width // LANES

    def body(i, carry):
        y = start + i // across
        x = lax.rem(i, across) * LANES
        at = pl.multiple_of(x * depth, LANES * depth)
        low[y, pl.ds(pl.multiple_of(x, LANES), LANES), :] = block[y, pl.ds(at, LANES, stride=depth), :]
        high[y, pl.ds(pl.multiple_of(x, LANES), LANES), :] = block[
            y, pl.ds(at + depth - 1, LANES, stride=depth), :
        ]
        return carry

    lax.fori_loop(0, planes * across, body, 0)


def step_kernel(plan, *refs):
    width, depth, where, first, lead, trail, last, extras = plan
    middle, left, right, lower_y, upper_y, low, high, conductance, source = refs[:9]
    refs = refs[9 + extras :]
    if last:
        field, sums, totals = refs[:3]
        old, coefficient, extra, new, running, sem_in, sem_edge, sem_out = refs[3:]
    else:
        field, bottom, top, rows = refs[:4]
        edges = refs[4 : 4 + lead + trail]
        old, coefficient, extra, new, sem_in, sem_edge, sem_out = refs[4 + lead + trail :]
    planes = new.shape[0]
    count, each = groups_of(planes)
    cells = width * depth
    across = width // LANES

    def load(kind, g):
        span = pl.ds(g * each, each)
        if kind == 0:
            return pltpu.make_async_copy(
                middle.at[span, pl.ds(where[0] * depth, cells)],
                old.at[pl.ds(g * each + 1, each), pl.ds(depth, cells)],
                sem_in.at[0, g],
            )
        from_ref, to_ref = ((conductance, coefficient), (source, extra))[kind - 1]
        return pltpu.make_async_copy(
            from_ref.at[span, pl.ds(first * depth, cells)], to_ref.at[span], sem_in.at[kind, g]
        )

    side_loads = []
    for n, (side, is_outer, column) in enumerate(((left, lead, 0), (right, trail, cells + depth))):
        if not is_outer:
            side_loads.append(
                pltpu.make_async_copy(
                    side.at[:, pl.ds(where[1 + n] * depth, depth)],
                    old.at[pl.ds(1, planes), pl.ds(column, depth)],
                    sem_edge.at[n],
                )
            )
    for copy in side_loads:
        copy.start()
    for g in range(count):
        for kind in range(3):
            load(kind, g).start()
    for side, is_outer, column in ((left, lead, 0), (right, trail, cells + depth)):
        if is_outer:
            old[pl.ds(1, planes), pl.ds(column, depth), :] = side[...]
    old[0, pl.ds(depth, cells), :] = lower_y[where[3]]
    old[planes + 1, pl.ds(depth, cells), :] = upper_y[where[4]]
    for copy in side_loads:
        copy.wait()
    load(0, 0).wait()

    here = lax.broadcasted_iota(jnp.int32, (depth, new.shape[2]), 0)
    at_low = here == 0
    at_high = here == depth - 1

    def column_block(i, start):
        y = start + i // across
        x = pl.multiple_of(lax.rem(i, across) * LANES, LANES)
        at = pl.multiple_of(x * depth, LANES * depth)
        before = old[y + 1, pl.ds(at, depth), :]
        centre = old[y + 1, pl.ds(at + depth, depth), :]
        for j in range(LANES):
            row = at + j * depth
            after = old[y + 1, pl.ds(row + 2 * depth, depth), :]
            below = low[y, pl.ds(x + j, depth, stride=0), :]
            above = high[y, pl.ds(x + j, depth, stride=0), :]
            below = jnp.where(at_low, below, pltpu.roll(centre, 1, 0))
            above = jnp.where(at_high, above, pltpu.roll(centre, depth - 1, 0))
            near = old[y, pl.ds(row + depth, depth), :] + old[y + 2, pl.ds(row + depth, depth), :]
            near = near + (before + after) + (below + above) - 6.0 * centre
            new[y, pl.ds(row, depth), :] = (
                centre + coefficient[y, pl.ds(row, depth), :] * near + extra[y, pl.ds(row, depth), :]
            )
            before, centre = centre, after

    def sum_block(i, start):
        y = start + i // across
        x = pl.multiple_of(lax.rem(i, across) * LANES, LANES)
        at = pl.multiple_of(x * depth, LANES * depth)
        so_far = new[y, pl.ds(at, LANES, stride=depth), :]
        running[y, pl.ds(at, LANES, stride=depth), :] = so_far
        for z in range(1, depth):
            so_far = so_far + new[y, pl.ds(at + z, LANES, stride=depth), :]
            running[y, pl.ds(at + z, LANES, stride=depth), :] = so_far
        totals[y, pl.ds(x, LANES), :] = so_far

    def save(g):
        span = pl.ds(g * each, each)
        target = field.at[span, pl.ds(first * depth, cells)] if last else field.at[span]
        return pltpu.make_async_copy(new.at[span], target, sem_out.at[0, g])

    def save_sums(g):
        span = pl.ds(g * each, each)
        return pltpu.make_async_copy(running.at[span], sums.at[span], sem_out.at[1, g])

    for g in range(count):
        if g + 1 < count:
            load(0, g + 1).wait()
        load(1, g).wait()
        load(2, g).wait()

        def walk(i, carry):
            column_block(i, g * each)
            return carry

        lax.fori_loop(0, each * across, walk, 0)
        save(g).start()
        if last:

            def walk_sums(i, carry):
                sum_block(i, g * each)
                return carry

            lax.fori_loop(0, each * across, walk_sums, 0)
            save_sums(g).start()
        else:
            take_rows(new, bottom, top, g * each, each, width, depth)
    if not last:
        take_sides(new, rows, edges, lead, trail, width, depth)
    for g in range(count):
        save(g).wait()
        if last:
            save_sums(g).wait()


def potential_kernel(plan, *refs):
    width, depth, first, earlier, scale, extras = plan
    sums = refs[0]
    offsets = refs[1 : 1 + earlier]
    potential, here, out, sem_in, sem_out = refs[1 + earlier + extras :]
    planes = here.shape[0]
    count, each = groups_of(planes)
    cells = width * depth
    across = width // LANES

    def load(g):
        span = pl.ds(g * each, each)
        return pltpu.make_async_copy(sums.at[span], here.at[span], sem_in.at[g])

    def save(g):
        span = pl.ds(g * each, each)
        return pltpu.make_async_copy(
            out.at[span], potential.at[span, pl.ds(first * depth, cells)], sem_out.at[g]
        )

    for g in range(count):
        load(g).start()
    for g in range(count):
        load(g).wait()

        def walk(i, carry):
            y = g * each + i // across
            x = pl.multiple_of(lax.rem(i, across) * LANES, LANES)
            for j in range(LANES):
                total = offsets[0][y, pl.ds(x + j, depth, stride=0), :]
                for offset in offsets[1:]:
                    total = total + offset[y, pl.ds(x + j, depth, stride=0), :]
                span = pl.ds(pl.multiple_of(x * depth + j * depth, depth), depth)
                value = here[y, span, :] + total
                out[y, span, :] = value * scale[0] if scale[1] else value / scale[0]
            return carry

        lax.fori_loop(0, each * across, walk, 0)
        save(g).start()
    for g in range(count):
        save(g).wait()


def ring(axis):
    count = lax.axis_size(axis)
    forward = [(i, (i + 1) % count) for i in range(count)]
    return forward, [(target, origin) for origin, target in forward]


def on_device(tracer, conductance, source):
    shape = tracer.shape
    planes, columns, depth, members = shape
    pieces = pieces_of(columns)
    last_piece = len(pieces) - 1
    flat = (planes, columns * depth, members)
    tracer, conductance, source = (v.reshape(flat) for v in (tracer, conductance, source))
    count, _ = groups_of(planes)

    def array(*dims):
        return pltpu.HBM(dims, jnp.float32)

    def near(*dims):
        return pltpu.VMEM(dims, jnp.float32)

    def placed(arrays, specs):
        return [
            pltpu.with_memory_space_constraint(v, pltpu.VMEM if spec is VMEM else pltpu.HBM)
            for v, spec in zip(arrays, specs)
        ]

    def scratch(*dims):
        return pltpu.VMEM(dims, jnp.float32)

    def ends(k):
        return int(k == 0), int(k == last_piece)

    def outer_arrays(k):
        width = pieces[k][1]
        lead, trail = ends(k)
        return [
            near(planes, width, members),
            near(planes, width, members),
            near(2, width * depth, members),
        ] + [near(planes, depth, members)] * (lead + trail)

    def prepare(k, token):
        first, width = pieces[k]
        lead, trail = ends(k)

        def kernel(*refs):
            prepare_kernel(first, width, depth, lead, trail, *refs)

        outs = outer_arrays(k)
        return pl.pallas_call(
            kernel,
            out_shape=outs,
            in_specs=[HBM] + [VMEM] * len(token),
            out_specs=[VMEM] * len(outs),
            scratch_shapes=[
                scratch(planes, width * depth, members),
                pltpu.SemaphoreType.DMA((count,)),
            ],
            compiler_params=pltpu.CompilerParams(vmem_limit_bytes=VMEM_LIMIT),
        )(*placed([tracer] + token, [HBM] + [VMEM] * len(token)))

    def advance(k, last, where, operands, whole, token):
        first, width = pieces[k]
        lead, trail = ends(k)
        specs = [HBM, VMEM if lead else HBM, VMEM if trail else HBM] + [VMEM] * 4 + [HBM] * 2
        aliases = {}
        operands = operands + token
        specs = specs + [HBM] * len(token)
        if last and k > 0:
            aliases = {len(operands): 0}
            operands = operands + [whole]
            specs = specs + [HBM]
        plan = (width, depth, where, first, lead, trail, last, len(operands) - 9)

        def kernel(*refs):
            step_kernel(plan, *refs)

        cells = width * depth
        if last:
            outs = [array(*flat), array(planes, cells, members), near(planes, width, members)]
            out_specs = [HBM, HBM, VMEM]
        else:
            outs = [array(planes, cells, members)] + outer_arrays(k)
            out_specs = [HBM] + [VMEM] * (len(outs) - 1)
        return pl.pallas_call(
            kernel,
            out_shape=outs,
            in_specs=specs,
            out_specs=out_specs,
            input_output_aliases=aliases,
            scratch_shapes=[
                scratch(planes + 2, cells + 2 * depth, members),
                scratch(planes, cells, members),
                scratch(planes, cells, members),
                scratch(planes, cells, members),
            ]
            + [scratch(planes, cells, members)] * last
            + [
                pltpu.SemaphoreType.DMA((3, count)),
                pltpu.SemaphoreType.DMA((2,)),
                pltpu.SemaphoreType.DMA((2, count)),
            ],
            compiler_params=pltpu.CompilerParams(vmem_limit_bytes=VMEM_LIMIT),
        )(*placed(operands, specs))

    def finish(k, sums, offsets, whole, scale):
        first, width = pieces[k]
        cells = width * depth
        operands = [sums] + offsets
        specs = [HBM] + [VMEM] * len(offsets)
        aliases = {}
        if k > 0:
            aliases = {len(operands): 0}
            operands = operands + [whole]
            specs = specs + [HBM]
        plan = (width, depth, first, len(offsets), scale, len(operands) - 1 - len(offsets))

        def kernel(*refs):
            potential_kernel(plan, *refs)

        return pl.pallas_call(
            kernel,
            out_shape=[array(*flat)],
            in_specs=specs,
            out_specs=[HBM],
            input_output_aliases=aliases,
            scratch_shapes=[
                scratch(planes, cells, members),
                scratch(planes, cells, members),
                pltpu.SemaphoreType.DMA((count,)),
                pltpu.SemaphoreType.DMA((count,)),
            ],
            compiler_params=pltpu.CompilerParams(vmem_limit_bytes=VMEM_LIMIT),
        )(*placed(operands, specs))[0]

    z_up, z_down = ring("pz")
    y_up, y_down = ring("py")
    x_up, x_down = ring("px")

    def exchange(k, outer, sides):
        bottom, top, rows = outer[:3]
        edges = list(outer[3:])
        from_below = lax.ppermute(top, "pz", z_up)
        from_above = lax.ppermute(bottom, "pz", z_down)
        if len(y_up) <= 2:
            rows = lax.ppermute(rows, "py", y_up)
            lower_y, upper_y = (rows, 0), (rows, 1)
        else:
            lower_y = (lax.ppermute(rows[0:1], "py", y_up), 0)
            upper_y = (lax.ppermute(rows[1:2], "py", y_down), 0)
        lead, trail = ends(k)
        if lead:
            sides["right"] = lax.ppermute(edges.pop(0), "px", x_down)
        if trail:
            sides["left"] = lax.ppermute(edges.pop(0), "px", x_up)
        return lower_y, upper_y, from_below, from_above

    halos, sides, token = [], {}, []
    for k in range(len(pieces)):
        outer = prepare(k, token)
        token = [outer[0]]
        halos.append(exchange(k, outer, sides))
    token = []
    fields = None
    end, sums, totals = None, [], []
    for step in range(STEPS):
        last = step == STEPS - 1
        next_fields, next_halos, next_sides = [], [], {}
        for k, (first, width) in enumerate(pieces):
            lower_y, upper_y, from_below, from_above = halos[k]
            if step == 0:
                middle = (tracer, first)
                left = (tracer, first - 1)
                right = (tracer, first + width)
            else:
                middle = (fields[k], 0)
                left = (fields[k - 1], pieces[k - 1][1] - 1) if k > 0 else None
                right = (fields[k + 1], 0) if k < last_piece else None
            if k == 0:
                left = (sides["left"], 0)
            if k == last_piece:
                right = (sides["right"], 0)
            where = (middle[1], left[1], right[1], lower_y[1], upper_y[1])
            operands = [
                middle[0], left[0], right[0], lower_y[0], upper_y[0],
                from_below, from_above, conductance, source,
            ]
            results = advance(k, last, where, operands, end, token)
            token = [results[0]] if not last else []
            if last:
                end = results[0]
                sums.append(results[1])
                totals.append(results[2])
            else:
                next_fields.append(results[0])
                next_halos.append(exchange(k, results[1:], next_sides))
        fields, halos, sides = next_fields, next_halos, next_sides

    blocks = lax.axis_size("pz")
    cells_along = depth * blocks
    exact = cells_along & (cells_along - 1) == 0
    scale = (1.0 / cells_along, True) if exact else (float(cells_along), False)
    potential = None
    for k in range(len(pieces)):
        carried, offsets = totals[k], []
        for hop in range(blocks - 1):
            arrived = lax.ppermute(carried, "pz", [(hop, hop + 1)])
            offsets.append(arrived)
            carried = carried + arrived
        potential = finish(k, sums[k], offsets, potential, scale)
    return (potential.reshape(shape), end.reshape(shape))


def solution(mesh):
    placed = P("py", "px", "pz", None)

    return jax.shard_map(
        on_device,
        mesh=mesh,
        in_specs=(placed, placed, placed),
        out_specs=(placed, placed),
        check_vma=False,
    )
```

time: 1190 us -> 276 us (0.23)
  the two profiles are of different devices: /device:TPU:0 before, /device:TPU:24 now
where the time goes in v1:
time: 276 us
  Pallas kernels  109 us (39%)
  waiting for transfers between devices  89.5 us (32%)
  starting transfers between devices  76.3 us (28%)
    pallas_call x16, Pallas kernels, advance(): pl.pallas_call(kernel, out_shape=outs, in_specs=specs, out_specs=out_spec...  87.6 us
    ppermute x16, waiting for transfers between devices, exchange(): from_above = lax.ppermute(bottom, 'pz', z_down)  34.5 us
    ppermute x16, starting transfers between devices, exchange(): from_below = lax.ppermute(top, 'pz', z_up)  29.3 us
    ppermute x16, waiting for transfers between devices, exchange(): from_below = lax.ppermute(top, 'pz', z_up)  24.8 us
    ppermute x16, starting transfers between devices, exchange(): rows = lax.ppermute(rows, 'py', y_up)  19.6 us
    ppermute x16, starting transfers between devices, exchange(): from_above = lax.ppermute(bottom, 'pz', z_down)  14.3 us
    pallas_call x4, Pallas kernels, finish(): pl.pallas_call(kernel, out_shape=[array(*flat)], in_specs=specs, out_spec...  13.1 us
    ppermute x12, waiting for transfers between devices, on_device(): arrived = lax.ppermute(carried, 'pz', [(hop, hop + 1)])  12.9 us
  transfers between devices with their start and end apart: 68, of which 20 were waited for; matrix products, arithmetic and copies ran while one was open for 0% of the time, Pallas kernels for 38%

profile of v1, /device:TPU:24, one launch (start us, length us, event | category | flops | bytes accessed | tf_op | source)
XLA Modules:
  0.0 275.7 jit_solution(1346783475917686195)
XLA Ops:
  0.6 2.3 shard_map.50
  5.4 2.3 shard_map.51
  7.7 1.8 shard_map.52
  11.9 1.8 collective-permute-start.13
  13.7 1.6 collective-permute-done.10.refs_1_
  16.8 4.8 %collective-permute-done.1.refs_3_.refs_4_ = f32[2,128,128]{2,1,0:T(8,128)S(1)} collective-permute-done((f32[2,128,128]{2,1,0:T(8,128)S(1)}, f32[2,128,128]{2,1,0:T(8,128)S(1)}, u32[]{:S(2)}, u32[]{:S(2)}) %collective-permute-start.1) | collective-permute-done | bytes 131104 | tf_op jit(solution)/shard_map/ppermute | solution.py:399
  21.5 1.7 collective-permute-start.7
  23.3 1.8 collective-permute-start.6
  25.1 4.0 %collective-permute-done.12.refs_5_ = f32[16,40,128]{2,1,0:T(8,128)S(1)} collective-permute-done((f32[16,40,128]{2,1,0:T(8,128)S(1)}, f32[16,40,128]{2,1,0:T(8,128)S(1)}, u32[]{:S(2)}, u32[]{:S(2)}) %collective-permute-start.12) | collective-permute-done | bytes 327712 | tf_op jit(solution)/shard_map/ppermute | solution.py:396
  29.1 2.0 collective-permute-start.9
  31.1 6.3 %shard_map.54 = (f32[16,320,128]{2,1,0:T(8,128)}, f32[16,40,128]{2,1,0:T(8,128)S(1)}, f32[16,40,128]{2,1,0:T(8,128)S(1)}, f32[2,320,128]{2,1,0:T(8,128)S(1)}, f32[16,8,128]{2,1,0:T(8,128)S(1)}) custom-call(f32[16,1024,128]{2,1,0:T(8,128)} %bitcast.41, f32[16,8,128]{2,1,0:T(8,128)S(1)} %collective-permute-done.10.refs_1_, f32[16,1024,128]{2,1,0:T(8,128)} %bitcast.42, ...), custom_call_target="tpu_custom_call" | custom-call | tf_op jit(solution)/shard_map/pallas_call | solution.py:338
  37.4 2.9 %collective-permute-done.5.refs_5_ = f32[16,32,128]{2,1,0:T(8,128)S(1)} collective-permute-done((f32[16,32,128]{2,1,0:T(8,128)S(1)}, f32[16,32,128]{2,1,0:T(8,128)S(1)}, u32[]{:S(2)}, u32[]{:S(2)}) %collective-permute-start.5) | collective-permute-done | bytes 262176 | tf_op jit(solution)/shard_map/ppermute | solution.py:396
  43.9 10.4 %collective-permute-done.8.refs_5_ = f32[16,40,128]{2,1,0:T(8,128)S(1)} collective-permute-done((f32[16,40,128]{2,1,0:T(8,128)S(1)}, f32[16,40,128]{2,1,0:T(8,128)S(1)}, u32[]{:S(2)}, u32[]{:S(2)}) %collective-permute-start.8) | collective-permute-done | bytes 327712 | tf_op jit(solution)/shard_map/ppermute | solution.py:396
  54.8 1.6 collective-permute-start.26
  56.4 6.4 %shard_map.55 = (f32[16,320,128]{2,1,0:T(8,128)}, f32[16,40,128]{2,1,0:T(8,128)S(1)}, f32[16,40,128]{2,1,0:T(8,128)S(1)}, f32[2,320,128]{2,1,0:T(8,128)S(1)}) custom-call(f32[16,1024,128]{2,1,0:T(8,128)} %bitcast.43, f32[16,1024,128]{2,1,0:T(8,128)} %bitcast.44, f32[16,1024,128]{2,1,0:T(8,128)} %bitcast.45, ...), custom_call_target="tpu_custom_call" | custom-call | tf_op jit(solution)/shard_map/pallas_call | solution.py:338
  62.8 5.1 %shard_map.56 = (f32[16,256,128]{2,1,0:T(8,128)}, f32[16,32,128]{2,1,0:T(8,128)S(1)}, f32[16,32,128]{2,1,0:T(8,128)S(1)}, f32[2,256,128]{2,1,0:T(8,128)S(1)}) custom-call(f32[16,1024,128]{2,1,0:T(8,128)} %bitcast.46, f32[16,1024,128]{2,1,0:T(8,128)} %bitcast.47, f32[16,1024,128]{2,1,0:T(8,128)} %bitcast.48, ...), custom_call_target="tpu_custom_call" | custom-call | tf_op jit(solution)/shard_map/pallas_call | solution.py:338
  67.9 3.4 %shard_map.57 = (f32[16,128,128]{2,1,0:T(8,128)}, f32[16,16,128]{2,1,0:T(8,128)S(1)}, f32[16,16,128]{2,1,0:T(8,128)S(1)}, f32[2,128,128]{2,1,0:T(8,128)S(1)}, f32[16,8,128]{2,1,0:T(8,128)S(1)}) custom-call(f32[16,1024,128]{2,1,0:T(8,128)} %bitcast.49, f32[16,1024,128]{2,1,0:T(8,128)} %bitcast.50, f32[16,8,128]{2,1,0:T(8,128)S(1)} %collective-permute-done.refs_2_, ...), custom_call_target="tpu_custom_call" | custom-call | tf_op jit(solution)/shard_map/pallas_call | solution.py:338
  71.8 1.5 collective-permute-start.21
  73.3 1.7 collective-permute-done.24.refs_1_
  75.0 1.7 collective-permute-start.22
  78.6 5.3 %collective-permute-done.27.refs_6_ = f32[16,40,128]{2,1,0:T(8,128)S(1)} collective-permute-done((f32[16,40,128]{2,1,0:T(8,128)S(1)}, f32[16,40,128]{2,1,0:T(8,128)S(1)}, u32[]{:S(2)}, u32[]{:S(2)}) %collective-permute-start.27) | collective-permute-done | bytes 327712 | tf_op jit(solution)/shard_map/ppermute | solution.py:397
  85.8 5.1 %collective-permute-done.22.refs_5_ = f32[16,40,128]{2,1,0:T(8,128)S(1)} collective-permute-done((f32[16,40,128]{2,1,0:T(8,128)S(1)}, f32[16,40,128]{2,1,0:T(8,128)S(1)}, u32[]{:S(2)}, u32[]{:S(2)}) %collective-permute-start.22) | collective-permute-done | bytes 327712 | tf_op jit(solution)/shard_map/ppermute | solution.py:396
  91.5 6.4 %collective-permute-done.23.refs_6_ = f32[16,40,128]{2,1,0:T(8,128)S(1)} collective-permute-done((f32[16,40,128]{2,1,0:T(8,128)S(1)}, f32[16,40,128]{2,1,0:T(8,128)S(1)}, u32[]{:S(2)}, u32[]{:S(2)}) %collective-permute-start.23) | collective-permute-done | bytes 327712 | tf_op jit(solution)/shard_map/ppermute | solution.py:397
  97.9 6.4 %shard_map.58 = (f32[16,320,128]{2,1,0:T(8,128)}, f32[16,40,128]{2,1,0:T(8,128)S(1)}, f32[16,40,128]{2,1,0:T(8,128)S(1)}, f32[2,320,128]{2,1,0:T(8,128)S(1)}, f32[16,8,128]{2,1,0:T(8,128)S(1)}) custom-call(f32[16,320,128]{2,1,0:T(8,128)} %get-tuple-element.96.refs_9_.refs_0_.refs_1_, f32[16,8,128]{2,1,0:T(8,128)S(1)} %collective-permute-done.24.refs_1_, ...), custom_call_target="tpu_custom_call" | custom-call | tf_op jit(solution)/shard_map/pallas_call | solution.py:338
  104.3 6.4 %shard_map.59 = (f32[16,320,128]{2,1,0:T(8,128)}, f32[16,40,128]{2,1,0:T(8,128)S(1)}, f32[16,40,128]{2,1,0:T(8,128)S(1)}, f32[2,320,128]{2,1,0:T(8,128)S(1)}) custom-call(f32[16,320,128]{2,1,0:T(8,128)} %get-tuple-element.97.refs_9_.refs_2_.refs_0_.refs_1_, f32[16,320,128]{2,1,0:T(8,128)} %get-tuple-element.96.refs_9_.refs_0_.refs_1_, ...), custom_call_target="tpu_custom_call" | custom-call | tf_op jit(solution)/shard_map/pallas_call | solution.py:338
  110.7 1.6 collective-permute-start.35
  112.3 2.0 collective-permute-start.17
  114.8 1.8 collective-permute-start.40
  116.9 5.1 %shard_map.60 = (f32[16,256,128]{2,1,0:T(8,128)}, f32[16,32,128]{2,1,0:T(8,128)S(1)}, f32[16,32,128]{2,1,0:T(8,128)S(1)}, f32[2,256,128]{2,1,0:T(8,128)S(1)}) custom-call(f32[16,256,128]{2,1,0:T(8,128)} %get-tuple-element.98.refs_9_.refs_2_.refs_0_.refs_1_, f32[16,320,128]{2,1,0:T(8,128)} %get-tuple-element.97.refs_9_.refs_2_.refs_0_.refs_1_, ...), custom_call_target="tpu_custom_call" | custom-call | tf_op jit(solution)/shard_map/pallas_call | solution.py:338
  122.0 3.4 %shard_map.61 = (f32[16,128,128]{2,1,0:T(8,128)}, f32[16,16,128]{2,1,0:T(8,128)S(1)}, f32[16,16,128]{2,1,0:T(8,128)S(1)}, f32[2,128,128]{2,1,0:T(8,128)S(1)}, f32[16,8,128]{2,1,0:T(8,128)S(1)}) custom-call(f32[16,128,128]{2,1,0:T(8,128)} %get-tuple-element.99.refs_9_.refs_2_.refs_0_, f32[16,256,128]{2,1,0:T(8,128)} %get-tuple-element.98.refs_9_.refs_2_.refs_0_.refs_1_, ...), custom_call_target="tpu_custom_call" | custom-call | tf_op jit(solution)/shard_map/pallas_call | solution.py:338
  125.5 3.7 %collective-permute-done.38.refs_1_ = f32[16,8,128]{2,1,0:T(8,128)S(1)} collective-permute-done((f32[16,8,128]{2,1,0:T(8,128)S(1)}, f32[16,8,128]{2,1,0:T(8,128)S(1)}, u32[]{:S(2)}, u32[]{:S(2)}) %collective-permute-start.38) | collective-permute-done | bytes 65568 | tf_op jit(solution)/shard_map/ppermute | solution.py:408
  129.2 3.6 %collective-permute-start.36 = (f32[16,40,128]{2,1,0:T(8,128)S(1)}, f32[16,40,128]{2,1,0:T(8,128)S(1)}, u32[]{:S(2)}, u32[]{:S(2)}) collective-permute-start(f32[16,40,128]{2,1,0:T(8,128)S(1)} %get-tuple-element.126), channel_id=1, source_target_pairs={{0,1},{1,2},{2,3},{3,0},{4,5},{5,6},{6,7},{7,4},{8,9},{9,10},{10,1... | collective-permute-start | bytes 983048 | tf_op jit(solution)/shard_map/ppermute | solution.py:396
  132.8 1.6 collective-permute-start.32
  134.4 3.8 %collective-permute-start.33 = (f32[16,32,128]{2,1,0:T(8,128)S(1)}, f32[16,32,128]{2,1,0:T(8,128)S(1)}, u32[]{:S(2)}, u32[]{:S(2)}) collective-permute-start(f32[16,32,128]{2,1,0:T(8,128)S(1)} %get-tuple-element.123), channel_id=1, source_target_pairs={{0,1},{1,2},{2,3},{3,0},{4,5},{5,6},{6,7},{7,4},{8,9},{9,10},{10,1... | collective-permute-start | bytes 786440 | tf_op jit(solution)/shard_map/ppermute | solution.py:396
  138.1 6.3 %shard_map.62 = (f32[16,320,128]{2,1,0:T(8,128)}, f32[16,40,128]{2,1,0:T(8,128)S(1)}, f32[16,40,128]{2,1,0:T(8,128)S(1)}, f32[2,320,128]{2,1,0:T(8,128)S(1)}, f32[16,8,128]{2,1,0:T(8,128)S(1)}) custom-call(f32[16,320,128]{2,1,0:T(8,128)} %get-tuple-element.114.refs_9_.refs_0_.refs_1_, f32[16,8,128]{2,1,0:T(8,128)S(1)} %collective-permute-done.38.refs_1_, ...), custom_call_target="tpu_custom_call" | custom-call | tf_op jit(solution)/shard_map/pallas_call | solution.py:338
  144.5 5.4 %collective-permute-done.37.refs_6_ = f32[16,40,128]{2,1,0:T(8,128)S(1)} collective-permute-done((f32[16,40,128]{2,1,0:T(8,128)S(1)}, f32[16,40,128]{2,1,0:T(8,128)S(1)}, u32[]{:S(2)}, u32[]{:S(2)}) %collective-permute-start.37) | collective-permute-done | bytes 327712 | tf_op jit(solution)/shard_map/ppermute | solution.py:397
  149.9 6.4 %shard_map.63 = (f32[16,320,128]{2,1,0:T(8,128)}, f32[16,40,128]{2,1,0:T(8,128)S(1)}, f32[16,40,128]{2,1,0:T(8,128)S(1)}, f32[2,320,128]{2,1,0:T(8,128)S(1)}) custom-call(f32[16,320,128]{2,1,0:T(8,128)} %get-tuple-element.115.refs_9_.refs_2_.refs_0_.refs_1_, f32[16,320,128]{2,1,0:T(8,128)} %get-tuple-element.114.refs_9_.refs_0_.refs_1_, ...), custom_call_target="tpu_custom_call" | custom-call | tf_op jit(solution)/shard_map/pallas_call | solution.py:338
  156.4 2.0 collective-permute-start.29
  158.3 2.4 collective-permute-start.30
  160.8 5.1 %shard_map.64 = (f32[16,256,128]{2,1,0:T(8,128)}, f32[16,32,128]{2,1,0:T(8,128)S(1)}, f32[16,32,128]{2,1,0:T(8,128)S(1)}, f32[2,256,128]{2,1,0:T(8,128)S(1)}) custom-call(f32[16,256,128]{2,1,0:T(8,128)} %get-tuple-element.116.refs_9_.refs_2_.refs_0_.refs_1_, f32[16,320,128]{2,1,0:T(8,128)} %get-tuple-element.115.refs_9_.refs_2_.refs_0_.refs_1_, ...), custom_call_target="tpu_custom_call" | custom-call | tf_op jit(solution)/shard_map/pallas_call | solution.py:338
  165.9 1.6 collective-permute-start.53
  167.5 3.8 %collective-permute-start.54 = (f32[16,40,128]{2,1,0:T(8,128)S(1)}, f32[16,40,128]{2,1,0:T(8,128)S(1)}, u32[]{:S(2)}, u32[]{:S(2)}) collective-permute-start(f32[16,40,128]{2,1,0:T(8,128)S(1)} %get-tuple-element.148), channel_id=1, source_target_pairs={{0,1},{1,2},{2,3},{3,0},{4,5},{5,6},{6,7},{7,4},{8,9},{9,10},{10,1... | collective-permute-start | bytes 983048 | tf_op jit(solution)/shard_map/ppermute | solution.py:396
  171.2 3.4 %shard_map.65 = (f32[16,128,128]{2,1,0:T(8,128)}, f32[16,16,128]{2,1,0:T(8,128)S(1)}, f32[16,16,128]{2,1,0:T(8,128)S(1)}, f32[2,128,128]{2,1,0:T(8,128)S(1)}, f32[16,8,128]{2,1,0:T(8,128)S(1)}) custom-call(f32[16,128,128]{2,1,0:T(8,128)} %get-tuple-element.117.refs_9_.refs_2_.refs_0_, f32[16,256,128]{2,1,0:T(8,128)} %get-tuple-element.116.refs_9_.refs_2_.refs_0_.refs_1_, ...), custom_call_target="tpu_custom_call" | custom-call | tf_op jit(solution)/shard_map/pallas_call | solution.py:338
  174.7 3.6 %collective-permute-done.52.refs_1_ = f32[16,8,128]{2,1,0:T(8,128)S(1)} collective-permute-done((f32[16,8,128]{2,1,0:T(8,128)S(1)}, f32[16,8,128]{2,1,0:T(8,128)S(1)}, u32[]{:S(2)}, u32[]{:S(2)}) %collective-permute-start.52) | collective-permute-done | bytes 65568 | tf_op jit(solution)/shard_map/ppermute | solution.py:408
  178.6 1.8 collective-permute-start.51
  180.9 2.8 %collective-permute-start.47 = (f32[16,32,128]{2,1,0:T(8,128)S(1)}, f32[16,32,128]{2,1,0:T(8,128)S(1)}, u32[]{:S(2)}, u32[]{:S(2)}) collective-permute-start(f32[16,32,128]{2,1,0:T(8,128)S(1)} %get-tuple-element.141), channel_id=1, source_target_pairs={{0,1},{1,2},{2,3},{3,0},{4,5},{5,6},{6,7},{7,4},{8,9},{9,10},{10,1... | collective-permute-start | bytes 786440 | tf_op jit(solution)/shard_map/ppermute | solution.py:396
  183.7 3.5 %collective-permute-done.55.refs_6_ = f32[16,40,128]{2,1,0:T(8,128)S(1)} collective-permute-done((f32[16,40,128]{2,1,0:T(8,128)S(1)}, f32[16,40,128]{2,1,0:T(8,128)S(1)}, u32[]{:S(2)}, u32[]{:S(2)}) %collective-permute-start.55) | collective-permute-done | bytes 327712 | tf_op jit(solution)/shard_map/ppermute | solution.py:397
  187.2 1.8 collective-permute-start.48
  188.9 7.3 %shard_map.66 = (f32[16,1024,128]{2,1,0:T(8,128)}, f32[16,320,128]{2,1,0:T(8,128)}, f32[16,40,128]{2,1,0:T(8,128)S(1)}) custom-call(f32[16,320,128]{2,1,0:T(8,128)} %get-tuple-element.132.refs_9_.refs_0_.refs_1_, f32[16,8,128]{2,1,0:T(8,128)S(1)} %collective-permute-done.52.refs_1_, f32[16,320,128]{2,1,0:T(8,128)} %get-tuple-element.133.refs_9_.refs_2_.refs_0_.refs_1_, ...), custom_call_target="tpu_custom_call" | custom-call | tf_op jit(solution)/shard_map/pallas_call | solution.py:338
  196.9 4.3 %collective-permute-done.51.refs_6_ = f32[16,40,128]{2,1,0:T(8,128)S(1)} collective-permute-done((f32[16,40,128]{2,1,0:T(8,128)S(1)}, f32[16,40,128]{2,1,0:T(8,128)S(1)}, u32[]{:S(2)}, u32[]{:S(2)}) %collective-permute-start.51) | collective-permute-done | bytes 327712 | tf_op jit(solution)/shard_map/ppermute | solution.py:397
  201.2 7.4 %shard_map.67 = (f32[16,1024,128]{2,1,0:T(8,128)}, f32[16,320,128]{2,1,0:T(8,128)}, f32[16,40,128]{2,1,0:T(8,128)S(1)}) custom-call(f32[16,320,128]{2,1,0:T(8,128)} %get-tuple-element.133.refs_9_.refs_2_.refs_0_.refs_1_, f32[16,320,128]{2,1,0:T(8,128)} %get-tuple-element.132.refs_9_.refs_0_.refs_1_, ...), custom_call_target="tpu_custom_call", output_to_operand_aliasing={{0}: (9, {})} | custom-call | tf_op jit(solution)/shard_map/pallas_call | solution.py:338
  209.3 3.2 %collective-permute-done.48.refs_6_ = f32[16,32,128]{2,1,0:T(8,128)S(1)} collective-permute-done((f32[16,32,128]{2,1,0:T(8,128)S(1)}, f32[16,32,128]{2,1,0:T(8,128)S(1)}, u32[]{:S(2)}, u32[]{:S(2)}) %collective-permute-start.48) | collective-permute-done | bytes 262176 | tf_op jit(solution)/shard_map/ppermute | solution.py:397
  212.5 5.7 %shard_map.68 = (f32[16,1024,128]{2,1,0:T(8,128)}, f32[16,256,128]{2,1,0:T(8,128)}, f32[16,32,128]{2,1,0:T(8,128)S(1)}) custom-call(f32[16,256,128]{2,1,0:T(8,128)} %get-tuple-element.134.refs_9_.refs_2_.refs_0_.refs_1_, f32[16,320,128]{2,1,0:T(8,128)} %get-tuple-element.133.refs_9_.refs_2_.refs_0_.refs_1_, ...), custom_call_target="tpu_custom_call", output_to_operand_aliasing={{0}: (9, {})} | custom-call | tf_op jit(solution)/shard_map/pallas_call | solution.py:338
  221.4 1.9 collective-permute-done.42.refs_2_
  223.3 6.4 %collective-permute-start.44 = (f32[16,16,128]{2,1,0:T(8,128)S(1)}, f32[16,16,128]{2,1,0:T(8,128)S(1)}, u32[]{:S(2)}, u32[]{:S(2)}) collective-permute-start(f32[16,16,128]{2,1,0:T(8,128)S(1)} %get-tuple-element.138), channel_id=1, source_target_pairs={{0,1},{1,2},{2,3},{3,0},{4,5},{5,6},{6,7},{7,4},{8,9},{9,10},{10,1... | collective-permute-start | bytes 393224 | tf_op jit(solution)/shard_map/ppermute | solution.py:396
  230.5 2.4 collective-permute-done.44.refs_5_
  232.8 6.5 %collective-permute-done.45.refs_6_ = f32[16,16,128]{2,1,0:T(8,128)S(1)} collective-permute-done((f32[16,16,128]{2,1,0:T(8,128)S(1)}, f32[16,16,128]{2,1,0:T(8,128)S(1)}, u32[]{:S(2)}, u32[]{:S(2)}) %collective-permute-start.45) | collective-permute-done | bytes 131104 | tf_op jit(solution)/shard_map/ppermute | solution.py:397
  239.3 3.7 %shard_map.69 = (f32[16,1024,128]{2,1,0:T(8,128)}, f32[16,128,128]{2,1,0:T(8,128)}, f32[16,16,128]{2,1,0:T(8,128)S(1)}) custom-call(f32[16,128,128]{2,1,0:T(8,128)} %get-tuple-element.135.refs_9_.refs_2_.refs_0_, f32[16,256,128]{2,1,0:T(8,128)} %get-tuple-element.134.refs_9_.refs_2_.refs_0_.refs_1_, ...), custom_call_target="tpu_custom_call", output_to_operand_aliasing={{0}: (9, {})} | custom-call | tf_op jit(solution)/shard_map/pallas_call | solution.py:338
  249.8 9.7 %collective-permute-done.67.refs_3_ = f32[16,40,128]{2,1,0:T(8,128)S(1)} collective-permute-done((f32[16,40,128]{2,1,0:T(8,128)S(1)}, f32[16,40,128]{2,1,0:T(8,128)S(1)}, u32[]{:S(2)}, u32[]{:S(2)}) %collective-permute-start.67) | collective-permute-done | bytes 327712 | tf_op jit(solution)/shard_map/ppermute | solution.py:460
  259.4 3.8 %shard_map.70.refs_4_ = f32[16,1024,128]{2,1,0:T(8,128)} custom-call(f32[16,320,128]{2,1,0:T(8,128)} %get-tuple-element.159.refs_0_, f32[16,40,128]{2,1,0:T(8,128)S(1)} %collective-permute-done.65.refs_1_, f32[16,40,128]{2,1,0:T(8,128)S(1)} %collective-permute-done.66.refs_2_, f32[16,40,128]{2,1,0:T(8,128)S(1)} %collective-permute-done.67.refs_3_), custom_call_target="tpu_custom_call" | custom-call | tf_op jit(solution)/shard_map/pallas_call | solution.py:374
  263.3 3.2 %collective-permute-done.64.refs_3_ = f32[16,40,128]{2,1,0:T(8,128)S(1)} collective-permute-done((f32[16,40,128]{2,1,0:T(8,128)S(1)}, f32[16,40,128]{2,1,0:T(8,128)S(1)}, u32[]{:S(2)}, u32[]{:S(2)}) %collective-permute-start.64) | collective-permute-done | bytes 327712 | tf_op jit(solution)/shard_map/ppermute | solution.py:460
  266.4 3.8 %shard_map.71.refs_4_ = f32[16,1024,128]{2,1,0:T(8,128)} custom-call(f32[16,320,128]{2,1,0:T(8,128)} %get-tuple-element.157.refs_0_, f32[16,40,128]{2,1,0:T(8,128)S(1)} %collective-permute-done.62.refs_1_, f32[16,40,128]{2,1,0:T(8,128)S(1)} %collective-permute-done.63.refs_2_, ...), custom_call_target="tpu_custom_call", output_to_operand_aliasing={{}: (4, {})} | custom-call | tf_op jit(solution)/shard_map/pallas_call | solution.py:374
  270.3 3.1 %shard_map.72.refs_4_ = f32[16,1024,128]{2,1,0:T(8,128)} custom-call(f32[16,256,128]{2,1,0:T(8,128)} %get-tuple-element.155.refs_0_, f32[16,32,128]{2,1,0:T(8,128)S(1)} %collective-permute-done.59.refs_1_, f32[16,32,128]{2,1,0:T(8,128)S(1)} %collective-permute-done.60.refs_2_, ...), custom_call_target="tpu_custom_call", output_to_operand_aliasing={{}: (4, {})} | custom-call | tf_op jit(solution)/shard_map/pallas_call | solution.py:374
  273.4 2.3 shard_map.73
  (104 shorter events, 28.9 us)
Async XLA Ops:
  2.9 8.9 %collective-permute-start = (f32[16,8,128]{2,1,0:T(8,128)S(1)}, f32[16,8,128]{2,1,0:T(8,128)S(1)}, u32[]{:S(2)}, u32[]{:S(2)}) collective-permute-start(f32[16,8,128]{2,1,0:T(8,128)S(1)} %get-tuple-element.82), channel_id=1, source_target_pairs={{4,0},{8,4},{12,8},{0,12},{5,1},{9,5},{13,9},{1,13},{6,2},{10,6},{... | collective-permute-start | bytes 196616 | tf_op jit(solution)/shard_map/ppermute | solution.py:406
  3.9 19.4 %collective-permute-start.11 = (f32[2,320,128]{2,1,0:T(8,128)S(1)}, f32[2,320,128]{2,1,0:T(8,128)S(1)}, u32[]{:S(2)}, u32[]{:S(2)}) collective-permute-start(f32[2,320,128]{2,1,0:T(8,128)S(1)} %get-tuple-element.94), channel_id=1, source_target_pairs={{0,16},{16,0},{1,17},{17,1},{2,18},{18,2},{3,19},{19,3},{4,20},{20... | collective-permute-start | bytes 983048 | tf_op jit(solution)/shard_map/ppermute | solution.py:399
  9.6 12.0 %collective-permute-start.4 = (f32[2,256,128]{2,1,0:T(8,128)S(1)}, f32[2,256,128]{2,1,0:T(8,128)S(1)}, u32[]{:S(2)}, u32[]{:S(2)}) collective-permute-start(f32[2,256,128]{2,1,0:T(8,128)S(1)} %get-tuple-element.89), channel_id=1, source_target_pairs={{0,16},{16,0},{1,17},{17,1},{2,18},{18,2},{3,19},{19,3},{4,20},{20... | collective-permute-start | bytes 786440 | tf_op jit(solution)/shard_map/ppermute | solution.py:399
  11.5 3.7 %collective-permute-start.10 = (f32[16,8,128]{2,1,0:T(8,128)S(1)}, f32[16,8,128]{2,1,0:T(8,128)S(1)}, u32[]{:S(2)}, u32[]{:S(2)}) collective-permute-start(f32[16,8,128]{2,1,0:T(8,128)S(1)} %get-tuple-element.93), channel_id=1, source_target_pairs={{0,4},{4,8},{8,12},{12,0},{1,5},{5,9},{9,13},{13,1},{2,6},{6,10},{... | collective-permute-start | bytes 196616 | tf_op jit(solution)/shard_map/ppermute | solution.py:408
  11.6 17.5 %collective-permute-start.12 = (f32[16,40,128]{2,1,0:T(8,128)S(1)}, f32[16,40,128]{2,1,0:T(8,128)S(1)}, u32[]{:S(2)}, u32[]{:S(2)}) collective-permute-start(f32[16,40,128]{2,1,0:T(8,128)S(1)} %get-tuple-element.95), channel_id=1, source_target_pairs={{0,1},{1,2},{2,3},{3,0},{4,5},{5,6},{6,7},{7,4},{8,9},{9,10},{10,1... | collective-permute-start | bytes 983048 | tf_op jit(solution)/shard_map/ppermute | solution.py:396
  11.9 17.2 %collective-permute-start.13 = (f32[16,40,128]{2,1,0:T(8,128)S(1)}, f32[16,40,128]{2,1,0:T(8,128)S(1)}, u32[]{:S(2)}, u32[]{:S(2)}) collective-permute-start(f32[16,40,128]{2,1,0:T(8,128)S(1)} %get-tuple-element.83.refs_1_), channel_id=1, source_target_pairs={{1,0},{2,1},{3,2},{0,3},{5,4},{6,5},{7,6},{4,7},{9,8},{10,9},{11,1... | collective-permute-start | bytes 983048 | tf_op jit(solution)/shard_map/ppermute | solution.py:397
  15.3 6.3 %collective-permute-start.1 = (f32[2,128,128]{2,1,0:T(8,128)S(1)}, f32[2,128,128]{2,1,0:T(8,128)S(1)}, u32[]{:S(2)}, u32[]{:S(2)}) collective-permute-start(f32[2,128,128]{2,1,0:T(8,128)S(1)} %get-tuple-element.86), channel_id=1, source_target_pairs={{0,16},{16,0},{1,17},{17,1},{2,18},{18,2},{3,19},{19,3},{4,20},{20... | collective-permute-start | bytes 393224 | tf_op jit(solution)/shard_map/ppermute | solution.py:399
  21.5 18.8 %collective-permute-start.5 = (f32[16,32,128]{2,1,0:T(8,128)S(1)}, f32[16,32,128]{2,1,0:T(8,128)S(1)}, u32[]{:S(2)}, u32[]{:S(2)}) collective-permute-start(f32[16,32,128]{2,1,0:T(8,128)S(1)} %get-tuple-element.90), channel_id=1, source_target_pairs={{0,1},{1,2},{2,3},{3,0},{4,5},{5,6},{6,7},{7,4},{8,9},{9,10},{10,1... | collective-permute-start | bytes 786440 | tf_op jit(solution)/shard_map/ppermute | solution.py:396
  21.5 20.8 %collective-permute-start.7 = (f32[2,320,128]{2,1,0:T(8,128)S(1)}, f32[2,320,128]{2,1,0:T(8,128)S(1)}, u32[]{:S(2)}, u32[]{:S(2)}) collective-permute-start(f32[2,320,128]{2,1,0:T(8,128)S(1)} %get-tuple-element.91), channel_id=1, source_target_pairs={{0,16},{16,0},{1,17},{17,1},{2,18},{18,2},{3,19},{19,3},{4,20},{20... | collective-permute-start | bytes 983048 | tf_op jit(solution)/shard_map/ppermute | solution.py:399
  23.3 18.5 %collective-permute-start.6 = (f32[16,32,128]{2,1,0:T(8,128)S(1)}, f32[16,32,128]{2,1,0:T(8,128)S(1)}, u32[]{:S(2)}, u32[]{:S(2)}) collective-permute-start(f32[16,32,128]{2,1,0:T(8,128)S(1)} %get-tuple-element.85.refs_1_), channel_id=1, source_target_pairs={{1,0},{2,1},{3,2},{0,3},{5,4},{6,5},{7,6},{4,7},{9,8},{10,9},{11,1... | collective-permute-start | bytes 786440 | tf_op jit(solution)/shard_map/ppermute | solution.py:397
  29.1 25.2 %collective-permute-start.8 = (f32[16,40,128]{2,1,0:T(8,128)S(1)}, f32[16,40,128]{2,1,0:T(8,128)S(1)}, u32[]{:S(2)}, u32[]{:S(2)}) collective-permute-start(f32[16,40,128]{2,1,0:T(8,128)S(1)} %get-tuple-element.92), channel_id=1, source_target_pairs={{0,1},{1,2},{2,3},{3,0},{4,5},{5,6},{6,7},{7,4},{8,9},{9,10},{10,1... | collective-permute-start | bytes 983048 | tf_op jit(solution)/shard_map/ppermute | solution.py:396
  29.1 25.7 %collective-permute-start.9 = (f32[16,40,128]{2,1,0:T(8,128)S(1)}, f32[16,40,128]{2,1,0:T(8,128)S(1)}, u32[]{:S(2)}, u32[]{:S(2)}) collective-permute-start(f32[16,40,128]{2,1,0:T(8,128)S(1)} %get-tuple-element.84.refs_1_), channel_id=1, source_target_pairs={{1,0},{2,1},{3,2},{0,3},{5,4},{6,5},{7,6},{4,7},{9,8},{10,9},{11,1... | collective-permute-start | bytes 983048 | tf_op jit(solution)/shard_map/ppermute | solution.py:397
  40.3 36.4 %collective-permute-start.25 = (f32[2,320,128]{2,1,0:T(8,128)S(1)}, f32[2,320,128]{2,1,0:T(8,128)S(1)}, u32[]{:S(2)}, u32[]{:S(2)}) collective-permute-start(f32[2,320,128]{2,1,0:T(8,128)S(1)} %get-tuple-element.111), channel_id=1, source_target_pairs={{0,16},{16,0},{1,17},{17,1},{2,18},{18,2},{3,19},{19,3},{4,20},{20... | collective-permute-start | bytes 983048 | tf_op jit(solution)/shard_map/ppermute | solution.py:399
  41.8 26.1 %collective-permute-start.2 = (f32[16,16,128]{2,1,0:T(8,128)S(1)}, f32[16,16,128]{2,1,0:T(8,128)S(1)}, u32[]{:S(2)}, u32[]{:S(2)}) collective-permute-start(f32[16,16,128]{2,1,0:T(8,128)S(1)} %get-tuple-element.87), channel_id=1, source_target_pairs={{0,1},{1,2},{2,3},{3,0},{4,5},{5,6},{6,7},{7,4},{8,9},{9,10},{10,1... | collective-permute-start | bytes 393224 | tf_op jit(solution)/shard_map/ppermute | solution.py:396
  42.4 25.5 %collective-permute-start.3 = (f32[16,16,128]{2,1,0:T(8,128)S(1)}, f32[16,16,128]{2,1,0:T(8,128)S(1)}, u32[]{:S(2)}, u32[]{:S(2)}) collective-permute-start(f32[16,16,128]{2,1,0:T(8,128)S(1)} %get-tuple-element.88), channel_id=1, source_target_pairs={{1,0},{2,1},{3,2},{0,3},{5,4},{6,5},{7,6},{4,7},{9,8},{10,9},{11,1... | collective-permute-start | bytes 393224 | tf_op jit(solution)/shard_map/ppermute | solution.py:397
  54.3 17.5 %collective-permute-start.14 = (f32[16,8,128]{2,1,0:T(8,128)S(1)}, f32[16,8,128]{2,1,0:T(8,128)S(1)}, u32[]{:S(2)}, u32[]{:S(2)}) collective-permute-start(f32[16,8,128]{2,1,0:T(8,128)S(1)} %get-tuple-element.100), channel_id=1, source_target_pairs={{4,0},{8,4},{12,8},{0,12},{5,1},{9,5},{13,9},{1,13},{6,2},{10,6},{... | collective-permute-start | bytes 196616 | tf_op jit(solution)/shard_map/ppermute | solution.py:406
  54.8 22.3 %collective-permute-start.26 = (f32[16,40,128]{2,1,0:T(8,128)S(1)}, f32[16,40,128]{2,1,0:T(8,128)S(1)}, u32[]{:S(2)}, u32[]{:S(2)}) collective-permute-start(f32[16,40,128]{2,1,0:T(8,128)S(1)} %get-tuple-element.112), channel_id=1, source_target_pairs={{0,1},{1,2},{2,3},{3,0},{4,5},{5,6},{6,7},{7,4},{8,9},{9,10},{10,1... | collective-permute-start | bytes 983048 | tf_op jit(solution)/shard_map/ppermute | solution.py:396
  71.3 3.7 %collective-permute-start.24 = (f32[16,8,128]{2,1,0:T(8,128)S(1)}, f32[16,8,128]{2,1,0:T(8,128)S(1)}, u32[]{:S(2)}, u32[]{:S(2)}) collective-permute-start(f32[16,8,128]{2,1,0:T(8,128)S(1)} %get-tuple-element.110), channel_id=1, source_target_pairs={{0,4},{4,8},{8,12},{12,0},{1,5},{5,9},{9,13},{13,1},{2,6},{6,10},{... | collective-permute-start | bytes 196616 | tf_op jit(solution)/shard_map/ppermute | solution.py:408
  71.3 12.5 %collective-permute-start.27 = (f32[16,40,128]{2,1,0:T(8,128)S(1)}, f32[16,40,128]{2,1,0:T(8,128)S(1)}, u32[]{:S(2)}, u32[]{:S(2)}) collective-permute-start(f32[16,40,128]{2,1,0:T(8,128)S(1)} %get-tuple-element.113), channel_id=1, source_target_pairs={{1,0},{2,1},{3,2},{0,3},{5,4},{6,5},{7,6},{4,7},{9,8},{10,9},{11,1... | collective-permute-start | bytes 983048 | tf_op jit(solution)/shard_map/ppermute | solution.py:397
  71.8 13.6 %collective-permute-start.21 = (f32[2,320,128]{2,1,0:T(8,128)S(1)}, f32[2,320,128]{2,1,0:T(8,128)S(1)}, u32[]{:S(2)}, u32[]{:S(2)}) collective-permute-start(f32[2,320,128]{2,1,0:T(8,128)S(1)} %get-tuple-element.107), channel_id=1, source_target_pairs={{0,16},{16,0},{1,17},{17,1},{2,18},{18,2},{3,19},{19,3},{4,20},{20... | collective-permute-start | bytes 983048 | tf_op jit(solution)/shard_map/ppermute | solution.py:399
  75.0 15.9 %collective-permute-start.22 = (f32[16,40,128]{2,1,0:T(8,128)S(1)}, f32[16,40,128]{2,1,0:T(8,128)S(1)}, u32[]{:S(2)}, u32[]{:S(2)}) collective-permute-start(f32[16,40,128]{2,1,0:T(8,128)S(1)} %get-tuple-element.108), channel_id=1, source_target_pairs={{0,1},{1,2},{2,3},{3,0},{4,5},{5,6},{6,7},{7,4},{8,9},{9,10},{10,1... | collective-permute-start | bytes 983048 | tf_op jit(solution)/shard_map/ppermute | solution.py:396
  76.7 21.2 %collective-permute-start.23 = (f32[16,40,128]{2,1,0:T(8,128)S(1)}, f32[16,40,128]{2,1,0:T(8,128)S(1)}, u32[]{:S(2)}, u32[]{:S(2)}) collective-permute-start(f32[16,40,128]{2,1,0:T(8,128)S(1)} %get-tuple-element.109), channel_id=1, source_target_pairs={{1,0},{2,1},{3,2},{0,3},{5,4},{6,5},{7,6},{4,7},{9,8},{10,9},{11,1... | collective-permute-start | bytes 983048 | tf_op jit(solution)/shard_map/ppermute | solution.py:397
  77.1 33.7 %collective-permute-start.15 = (f32[2,128,128]{2,1,0:T(8,128)S(1)}, f32[2,128,128]{2,1,0:T(8,128)S(1)}, u32[]{:S(2)}, u32[]{:S(2)}) collective-permute-start(f32[2,128,128]{2,1,0:T(8,128)S(1)} %get-tuple-element.101), channel_id=1, source_target_pairs={{0,16},{16,0},{1,17},{17,1},{2,18},{18,2},{3,19},{19,3},{4,20},{20... | collective-permute-start | bytes 393224 | tf_op jit(solution)/shard_map/ppermute | solution.py:399
  83.8 30.5 %collective-permute-start.18 = (f32[2,256,128]{2,1,0:T(8,128)S(1)}, f32[2,256,128]{2,1,0:T(8,128)S(1)}, u32[]{:S(2)}, u32[]{:S(2)}) collective-permute-start(f32[2,256,128]{2,1,0:T(8,128)S(1)} %get-tuple-element.104), channel_id=1, source_target_pairs={{0,16},{16,0},{1,17},{17,1},{2,18},{18,2},{3,19},{19,3},{4,20},{20... | collective-permute-start | bytes 786440 | tf_op jit(solution)/shard_map/ppermute | solution.py:399
  85.3 29.5 %collective-permute-start.19 = (f32[16,32,128]{2,1,0:T(8,128)S(1)}, f32[16,32,128]{2,1,0:T(8,128)S(1)}, u32[]{:S(2)}, u32[]{:S(2)}) collective-permute-start(f32[16,32,128]{2,1,0:T(8,128)S(1)} %get-tuple-element.105), channel_id=1, source_target_pairs={{0,1},{1,2},{2,3},{3,0},{4,5},{5,6},{6,7},{7,4},{8,9},{9,10},{10,1... | collective-permute-start | bytes 786440 | tf_op jit(solution)/shard_map/ppermute | solution.py:396
  90.9 25.7 %collective-permute-start.20 = (f32[16,32,128]{2,1,0:T(8,128)S(1)}, f32[16,32,128]{2,1,0:T(8,128)S(1)}, u32[]{:S(2)}, u32[]{:S(2)}) collective-permute-start(f32[16,32,128]{2,1,0:T(8,128)S(1)} %get-tuple-element.106), channel_id=1, source_target_pairs={{1,0},{2,1},{3,2},{0,3},{5,4},{6,5},{7,6},{4,7},{9,8},{10,9},{11,1... | collective-permute-start | bytes 786440 | tf_op jit(solution)/shard_map/ppermute | solution.py:397
  97.9 14.4 %collective-permute-start.16 = (f32[16,16,128]{2,1,0:T(8,128)S(1)}, f32[16,16,128]{2,1,0:T(8,128)S(1)}, u32[]{:S(2)}, u32[]{:S(2)}) collective-permute-start(f32[16,16,128]{2,1,0:T(8,128)S(1)} %get-tuple-element.102), channel_id=1, source_target_pairs={{0,1},{1,2},{2,3},{3,0},{4,5},{5,6},{6,7},{7,4},{8,9},{9,10},{10,1... | collective-permute-start | bytes 393224 | tf_op jit(solution)/shard_map/ppermute | solution.py:396
  110.7 22.0 %collective-permute-start.35 = (f32[2,320,128]{2,1,0:T(8,128)S(1)}, f32[2,320,128]{2,1,0:T(8,128)S(1)}, u32[]{:S(2)}, u32[]{:S(2)}) collective-permute-start(f32[2,320,128]{2,1,0:T(8,128)S(1)} %get-tuple-element.125), channel_id=1, source_target_pairs={{0,16},{16,0},{1,17},{17,1},{2,18},{18,2},{3,19},{19,3},{4,20},{20... | collective-permute-start | bytes 983048 | tf_op jit(solution)/shard_map/ppermute | solution.py:399
  112.3 9.7 %collective-permute-start.17 = (f32[16,16,128]{2,1,0:T(8,128)S(1)}, f32[16,16,128]{2,1,0:T(8,128)S(1)}, u32[]{:S(2)}, u32[]{:S(2)}) collective-permute-start(f32[16,16,128]{2,1,0:T(8,128)S(1)} %get-tuple-element.103), channel_id=1, source_target_pairs={{1,0},{2,1},{3,2},{0,3},{5,4},{6,5},{7,6},{4,7},{9,8},{10,9},{11,1... | collective-permute-start | bytes 393224 | tf_op jit(solution)/shard_map/ppermute | solution.py:397
  114.3 18.4 %collective-permute-start.39 = (f32[2,320,128]{2,1,0:T(8,128)S(1)}, f32[2,320,128]{2,1,0:T(8,128)S(1)}, u32[]{:S(2)}, u32[]{:S(2)}) collective-permute-start(f32[2,320,128]{2,1,0:T(8,128)S(1)} %get-tuple-element.129), channel_id=1, source_target_pairs={{0,16},{16,0},{1,17},{17,1},{2,18},{18,2},{3,19},{19,3},{4,20},{20... | collective-permute-start | bytes 983048 | tf_op jit(solution)/shard_map/ppermute | solution.py:399
  114.8 19.5 %collective-permute-start.40 = (f32[16,40,128]{2,1,0:T(8,128)S(1)}, f32[16,40,128]{2,1,0:T(8,128)S(1)}, u32[]{:S(2)}, u32[]{:S(2)}) collective-permute-start(f32[16,40,128]{2,1,0:T(8,128)S(1)} %get-tuple-element.130), channel_id=1, source_target_pairs={{0,1},{1,2},{2,3},{3,0},{4,5},{5,6},{6,7},{7,4},{8,9},{9,10},{10,1... | collective-permute-start | bytes 983048 | tf_op jit(solution)/shard_map/ppermute | solution.py:396
  116.7 21.5 %collective-permute-start.41 = (f32[16,40,128]{2,1,0:T(8,128)S(1)}, f32[16,40,128]{2,1,0:T(8,128)S(1)}, u32[]{:S(2)}, u32[]{:S(2)}) collective-permute-start(f32[16,40,128]{2,1,0:T(8,128)S(1)} %get-tuple-element.131), channel_id=1, source_target_pairs={{1,0},{2,1},{3,2},{0,3},{5,4},{6,5},{7,6},{4,7},{9,8},{10,9},{11,1... | collective-permute-start | bytes 983048 | tf_op jit(solution)/shard_map/ppermute | solution.py:397
  129.2 15.3 %collective-permute-start.36 = (f32[16,40,128]{2,1,0:T(8,128)S(1)}, f32[16,40,128]{2,1,0:T(8,128)S(1)}, u32[]{:S(2)}, u32[]{:S(2)}) collective-permute-start(f32[16,40,128]{2,1,0:T(8,128)S(1)} %get-tuple-element.126), channel_id=1, source_target_pairs={{0,1},{1,2},{2,3},{3,0},{4,5},{5,6},{6,7},{7,4},{8,9},{9,10},{10,1... | collective-permute-start | bytes 983048 | tf_op jit(solution)/shard_map/ppermute | solution.py:396
  132.8 17.1 %collective-permute-start.37 = (f32[16,40,128]{2,1,0:T(8,128)S(1)}, f32[16,40,128]{2,1,0:T(8,128)S(1)}, u32[]{:S(2)}, u32[]{:S(2)}) collective-permute-start(f32[16,40,128]{2,1,0:T(8,128)S(1)} %get-tuple-element.127), channel_id=1, source_target_pairs={{1,0},{2,1},{3,2},{0,3},{5,4},{6,5},{7,6},{4,7},{9,8},{10,9},{11,1... | collective-permute-start | bytes 983048 | tf_op jit(solution)/shard_map/ppermute | solution.py:397
  132.8 25.6 %collective-permute-start.32 = (f32[2,256,128]{2,1,0:T(8,128)S(1)}, f32[2,256,128]{2,1,0:T(8,128)S(1)}, u32[]{:S(2)}, u32[]{:S(2)}) collective-permute-start(f32[2,256,128]{2,1,0:T(8,128)S(1)} %get-tuple-element.122), channel_id=1, source_target_pairs={{0,16},{16,0},{1,17},{17,1},{2,18},{18,2},{3,19},{19,3},{4,20},{20... | collective-permute-start | bytes 786440 | tf_op jit(solution)/shard_map/ppermute | solution.py:399
  134.4 26.3 %collective-permute-start.33 = (f32[16,32,128]{2,1,0:T(8,128)S(1)}, f32[16,32,128]{2,1,0:T(8,128)S(1)}, u32[]{:S(2)}, u32[]{:S(2)}) collective-permute-start(f32[16,32,128]{2,1,0:T(8,128)S(1)} %get-tuple-element.123), channel_id=1, source_target_pairs={{0,1},{1,2},{2,3},{3,0},{4,5},{5,6},{6,7},{7,4},{8,9},{9,10},{10,1... | collective-permute-start | bytes 786440 | tf_op jit(solution)/shard_map/ppermute | solution.py:396
  138.1 22.6 %collective-permute-start.34 = (f32[16,32,128]{2,1,0:T(8,128)S(1)}, f32[16,32,128]{2,1,0:T(8,128)S(1)}, u32[]{:S(2)}, u32[]{:S(2)}) collective-permute-start(f32[16,32,128]{2,1,0:T(8,128)S(1)} %get-tuple-element.124), channel_id=1, source_target_pairs={{1,0},{2,1},{3,2},{0,3},{5,4},{6,5},{7,6},{4,7},{9,8},{10,9},{11,1... | collective-permute-start | bytes 786440 | tf_op jit(solution)/shard_map/ppermute | solution.py:397
  156.2 22.3 %collective-permute-start.49 = (f32[2,320,128]{2,1,0:T(8,128)S(1)}, f32[2,320,128]{2,1,0:T(8,128)S(1)}, u32[]{:S(2)}, u32[]{:S(2)}) collective-permute-start(f32[2,320,128]{2,1,0:T(8,128)S(1)} %get-tuple-element.143), channel_id=1, source_target_pairs={{0,16},{16,0},{1,17},{17,1},{2,18},{18,2},{3,19},{19,3},{4,20},{20... | collective-permute-start | bytes 983048 | tf_op jit(solution)/shard_map/ppermute | solution.py:399
  156.4 11.1 %collective-permute-start.29 = (f32[2,128,128]{2,1,0:T(8,128)S(1)}, f32[2,128,128]{2,1,0:T(8,128)S(1)}, u32[]{:S(2)}, u32[]{:S(2)}) collective-permute-start(f32[2,128,128]{2,1,0:T(8,128)S(1)} %get-tuple-element.119), channel_id=1, source_target_pairs={{0,16},{16,0},{1,17},{17,1},{2,18},{18,2},{3,19},{19,3},{4,20},{20... | collective-permute-start | bytes 393224 | tf_op jit(solution)/shard_map/ppermute | solution.py:399
  158.3 12.9 %collective-permute-start.30 = (f32[16,16,128]{2,1,0:T(8,128)S(1)}, f32[16,16,128]{2,1,0:T(8,128)S(1)}, u32[]{:S(2)}, u32[]{:S(2)}) collective-permute-start(f32[16,16,128]{2,1,0:T(8,128)S(1)} %get-tuple-element.120), channel_id=1, source_target_pairs={{0,1},{1,2},{2,3},{3,0},{4,5},{5,6},{6,7},{7,4},{8,9},{9,10},{10,1... | collective-permute-start | bytes 393224 | tf_op jit(solution)/shard_map/ppermute | solution.py:396
  160.7 10.5 %collective-permute-start.31 = (f32[16,16,128]{2,1,0:T(8,128)S(1)}, f32[16,16,128]{2,1,0:T(8,128)S(1)}, u32[]{:S(2)}, u32[]{:S(2)}) collective-permute-start(f32[16,16,128]{2,1,0:T(8,128)S(1)} %get-tuple-element.121), channel_id=1, source_target_pairs={{1,0},{2,1},{3,2},{0,3},{5,4},{6,5},{7,6},{4,7},{9,8},{10,9},{11,1... | collective-permute-start | bytes 393224 | tf_op jit(solution)/shard_map/ppermute | solution.py:397
  160.7 5.2 %collective-permute-start.28 = (f32[16,8,128]{2,1,0:T(8,128)S(1)}, f32[16,8,128]{2,1,0:T(8,128)S(1)}, u32[]{:S(2)}, u32[]{:S(2)}) collective-permute-start(f32[16,8,128]{2,1,0:T(8,128)S(1)} %get-tuple-element.118), channel_id=1, source_target_pairs={{4,0},{8,4},{12,8},{0,12},{5,1},{9,5},{13,9},{1,13},{6,2},{10,6},{... | collective-permute-start | bytes 196616 | tf_op jit(solution)/shard_map/ppermute | solution.py:406
  165.9 14.5 %collective-permute-start.53 = (f32[2,320,128]{2,1,0:T(8,128)S(1)}, f32[2,320,128]{2,1,0:T(8,128)S(1)}, u32[]{:S(2)}, u32[]{:S(2)}) collective-permute-start(f32[2,320,128]{2,1,0:T(8,128)S(1)} %get-tuple-element.147), channel_id=1, source_target_pairs={{0,16},{16,0},{1,17},{17,1},{2,18},{18,2},{3,19},{19,3},{4,20},{20... | collective-permute-start | bytes 983048 | tf_op jit(solution)/shard_map/ppermute | solution.py:399
  167.5 13.4 %collective-permute-start.54 = (f32[16,40,128]{2,1,0:T(8,128)S(1)}, f32[16,40,128]{2,1,0:T(8,128)S(1)}, u32[]{:S(2)}, u32[]{:S(2)}) collective-permute-start(f32[16,40,128]{2,1,0:T(8,128)S(1)} %get-tuple-element.148), channel_id=1, source_target_pairs={{0,1},{1,2},{2,3},{3,0},{4,5},{5,6},{6,7},{7,4},{8,9},{9,10},{10,1... | collective-permute-start | bytes 983048 | tf_op jit(solution)/shard_map/ppermute | solution.py:396
  174.6 3.7 %collective-permute-start.52 = (f32[16,8,128]{2,1,0:T(8,128)S(1)}, f32[16,8,128]{2,1,0:T(8,128)S(1)}, u32[]{:S(2)}, u32[]{:S(2)}) collective-permute-start(f32[16,8,128]{2,1,0:T(8,128)S(1)} %get-tuple-element.146), channel_id=1, source_target_pairs={{0,4},{4,8},{8,12},{12,0},{1,5},{5,9},{9,13},{13,1},{2,6},{6,10},{... | collective-permute-start | bytes 196616 | tf_op jit(solution)/shard_map/ppermute | solution.py:408
  174.7 12.5 %collective-permute-start.55 = (f32[16,40,128]{2,1,0:T(8,128)S(1)}, f32[16,40,128]{2,1,0:T(8,128)S(1)}, u32[]{:S(2)}, u32[]{:S(2)}) collective-permute-start(f32[16,40,128]{2,1,0:T(8,128)S(1)} %get-tuple-element.149), channel_id=1, source_target_pairs={{1,0},{2,1},{3,2},{0,3},{5,4},{6,5},{7,6},{4,7},{9,8},{10,9},{11,1... | collective-permute-start | bytes 983048 | tf_op jit(solution)/shard_map/ppermute | solution.py:397
  178.4 17.9 %collective-permute-start.50 = (f32[16,40,128]{2,1,0:T(8,128)S(1)}, f32[16,40,128]{2,1,0:T(8,128)S(1)}, u32[]{:S(2)}, u32[]{:S(2)}) collective-permute-start(f32[16,40,128]{2,1,0:T(8,128)S(1)} %get-tuple-element.144), channel_id=1, source_target_pairs={{0,1},{1,2},{2,3},{3,0},{4,5},{5,6},{6,7},{7,4},{8,9},{9,10},{10,1... | collective-permute-start | bytes 983048 | tf_op jit(solution)/shard_map/ppermute | solution.py:396
  178.6 22.7 %collective-permute-start.51 = (f32[16,40,128]{2,1,0:T(8,128)S(1)}, f32[16,40,128]{2,1,0:T(8,128)S(1)}, u32[]{:S(2)}, u32[]{:S(2)}) collective-permute-start(f32[16,40,128]{2,1,0:T(8,128)S(1)} %get-tuple-element.145), channel_id=1, source_target_pairs={{1,0},{2,1},{3,2},{0,3},{5,4},{6,5},{7,6},{4,7},{9,8},{10,9},{11,1... | collective-permute-start | bytes 983048 | tf_op jit(solution)/shard_map/ppermute | solution.py:397
  180.4 28.9 %collective-permute-start.46 = (f32[2,256,128]{2,1,0:T(8,128)S(1)}, f32[2,256,128]{2,1,0:T(8,128)S(1)}, u32[]{:S(2)}, u32[]{:S(2)}) collective-permute-start(f32[2,256,128]{2,1,0:T(8,128)S(1)} %get-tuple-element.140), channel_id=1, source_target_pairs={{0,16},{16,0},{1,17},{17,1},{2,18},{18,2},{3,19},{19,3},{4,20},{20... | collective-permute-start | bytes 786440 | tf_op jit(solution)/shard_map/ppermute | solution.py:399
  180.9 28.4 %collective-permute-start.47 = (f32[16,32,128]{2,1,0:T(8,128)S(1)}, f32[16,32,128]{2,1,0:T(8,128)S(1)}, u32[]{:S(2)}, u32[]{:S(2)}) collective-permute-start(f32[16,32,128]{2,1,0:T(8,128)S(1)} %get-tuple-element.141), channel_id=1, source_target_pairs={{0,1},{1,2},{2,3},{3,0},{4,5},{5,6},{6,7},{7,4},{8,9},{9,10},{10,1... | collective-permute-start | bytes 786440 | tf_op jit(solution)/shard_map/ppermute | solution.py:396
  187.2 25.3 %collective-permute-start.48 = (f32[16,32,128]{2,1,0:T(8,128)S(1)}, f32[16,32,128]{2,1,0:T(8,128)S(1)}, u32[]{:S(2)}, u32[]{:S(2)}) collective-permute-start(f32[16,32,128]{2,1,0:T(8,128)S(1)} %get-tuple-element.142), channel_id=1, source_target_pairs={{1,0},{2,1},{3,2},{0,3},{5,4},{6,5},{7,6},{4,7},{9,8},{10,9},{11,1... | collective-permute-start | bytes 786440 | tf_op jit(solution)/shard_map/ppermute | solution.py:397
  196.2 22.7 %collective-permute-start.65 = (f32[16,40,128]{2,1,0:T(8,128)S(1)}, f32[16,40,128]{2,1,0:T(8,128)S(1)}, u32[]{:S(2)}, u32[]{:S(2)}) collective-permute-start(f32[16,40,128]{2,1,0:T(8,128)S(1)} %get-tuple-element.160), channel_id=1, source_target_pairs={{0,1},{4,5},{8,9},{12,13},{16,17},{20,21},{24,25},{28,29}} | collective-permute-start | bytes 983048 | tf_op jit(solution)/shard_map/ppermute | solution.py:460
  208.6 11.1 %collective-permute-start.62 = (f32[16,40,128]{2,1,0:T(8,128)S(1)}, f32[16,40,128]{2,1,0:T(8,128)S(1)}, u32[]{:S(2)}, u32[]{:S(2)}) collective-permute-start(f32[16,40,128]{2,1,0:T(8,128)S(1)} %get-tuple-element.158), channel_id=1, source_target_pairs={{0,1},{4,5},{8,9},{12,13},{16,17},{20,21},{24,25},{28,29}} | collective-permute-start | bytes 983048 | tf_op jit(solution)/shard_map/ppermute | solution.py:460
  218.2 11.5 %collective-permute-start.59 = (f32[16,32,128]{2,1,0:T(8,128)S(1)}, f32[16,32,128]{2,1,0:T(8,128)S(1)}, u32[]{:S(2)}, u32[]{:S(2)}) collective-permute-start(f32[16,32,128]{2,1,0:T(8,128)S(1)} %get-tuple-element.156), channel_id=1, source_target_pairs={{0,1},{4,5},{8,9},{12,13},{16,17},{20,21},{24,25},{28,29}} | collective-permute-start | bytes 786440 | tf_op jit(solution)/shard_map/ppermute | solution.py:460
  219.0 24.7 %collective-permute-start.66 = (f32[16,40,128]{2,1,0:T(8,128)S(1)}, f32[16,40,128]{2,1,0:T(8,128)S(1)}, u32[]{:S(2)}, u32[]{:S(2)}) collective-permute-start(f32[16,40,128]{2,1,0:T(8,128)S(1)} %add.30), channel_id=1, source_target_pairs={{1,2},{5,6},{9,10},{13,14},{17,18},{21,22},{25,26},{29,30}} | collective-permute-start | bytes 983048 | tf_op jit(solution)/shard_map/ppermute | solution.py:460
  219.7 25.3 %collective-permute-start.63 = (f32[16,40,128]{2,1,0:T(8,128)S(1)}, f32[16,40,128]{2,1,0:T(8,128)S(1)}, u32[]{:S(2)}, u32[]{:S(2)}) collective-permute-start(f32[16,40,128]{2,1,0:T(8,128)S(1)} %add.28), channel_id=1, source_target_pairs={{1,2},{5,6},{9,10},{13,14},{17,18},{21,22},{25,26},{29,30}} | collective-permute-start | bytes 983048 | tf_op jit(solution)/shard_map/ppermute | solution.py:460
  220.4 9.4 %collective-permute-start.43 = (f32[2,128,128]{2,1,0:T(8,128)S(1)}, f32[2,128,128]{2,1,0:T(8,128)S(1)}, u32[]{:S(2)}, u32[]{:S(2)}) collective-permute-start(f32[2,128,128]{2,1,0:T(8,128)S(1)} %get-tuple-element.137), channel_id=1, source_target_pairs={{0,16},{16,0},{1,17},{17,1},{2,18},{18,2},{3,19},{19,3},{4,20},{20... | collective-permute-start | bytes 393224 | tf_op jit(solution)/shard_map/ppermute | solution.py:399
  223.3 9.5 %collective-permute-start.44 = (f32[16,16,128]{2,1,0:T(8,128)S(1)}, f32[16,16,128]{2,1,0:T(8,128)S(1)}, u32[]{:S(2)}, u32[]{:S(2)}) collective-permute-start(f32[16,16,128]{2,1,0:T(8,128)S(1)} %get-tuple-element.138), channel_id=1, source_target_pairs={{0,1},{1,2},{2,3},{3,0},{4,5},{5,6},{6,7},{7,4},{8,9},{9,10},{10,1... | collective-permute-start | bytes 393224 | tf_op jit(solution)/shard_map/ppermute | solution.py:396
  229.7 9.6 %collective-permute-start.45 = (f32[16,16,128]{2,1,0:T(8,128)S(1)}, f32[16,16,128]{2,1,0:T(8,128)S(1)}, u32[]{:S(2)}, u32[]{:S(2)}) collective-permute-start(f32[16,16,128]{2,1,0:T(8,128)S(1)} %get-tuple-element.139), channel_id=1, source_target_pairs={{1,0},{2,1},{3,2},{0,3},{5,4},{6,5},{7,6},{4,7},{9,8},{10,9},{11,1... | collective-permute-start | bytes 393224 | tf_op jit(solution)/shard_map/ppermute | solution.py:397
  229.8 16.6 %collective-permute-start.60 = (f32[16,32,128]{2,1,0:T(8,128)S(1)}, f32[16,32,128]{2,1,0:T(8,128)S(1)}, u32[]{:S(2)}, u32[]{:S(2)}) collective-permute-start(f32[16,32,128]{2,1,0:T(8,128)S(1)} %add.26), channel_id=1, source_target_pairs={{1,2},{5,6},{9,10},{13,14},{17,18},{21,22},{25,26},{29,30}} | collective-permute-start | bytes 786440 | tf_op jit(solution)/shard_map/ppermute | solution.py:460
  243.7 15.7 %collective-permute-start.67 = (f32[16,40,128]{2,1,0:T(8,128)S(1)}, f32[16,40,128]{2,1,0:T(8,128)S(1)}, u32[]{:S(2)}, u32[]{:S(2)}) collective-permute-start(f32[16,40,128]{2,1,0:T(8,128)S(1)} %add.31), channel_id=1, source_target_pairs={{2,3},{6,7},{10,11},{14,15},{18,19},{22,23},{26,27},{30,31}} | collective-permute-start | bytes 983048 | tf_op jit(solution)/shard_map/ppermute | solution.py:460
  245.0 21.4 %collective-permute-start.64 = (f32[16,40,128]{2,1,0:T(8,128)S(1)}, f32[16,40,128]{2,1,0:T(8,128)S(1)}, u32[]{:S(2)}, u32[]{:S(2)}) collective-permute-start(f32[16,40,128]{2,1,0:T(8,128)S(1)} %add.29), channel_id=1, source_target_pairs={{2,3},{6,7},{10,11},{14,15},{18,19},{22,23},{26,27},{30,31}} | collective-permute-start | bytes 983048 | tf_op jit(solution)/shard_map/ppermute | solution.py:460
  246.4 23.8 %collective-permute-start.61 = (f32[16,32,128]{2,1,0:T(8,128)S(1)}, f32[16,32,128]{2,1,0:T(8,128)S(1)}, u32[]{:S(2)}, u32[]{:S(2)}) collective-permute-start(f32[16,32,128]{2,1,0:T(8,128)S(1)} %add.27), channel_id=1, source_target_pairs={{2,3},{6,7},{10,11},{14,15},{18,19},{22,23},{26,27},{30,31}} | collective-permute-start | bytes 786440 | tf_op jit(solution)/shard_map/ppermute | solution.py:460
  248.5 25.0 %collective-permute-start.58 = (f32[16,16,128]{2,1,0:T(8,128)S(1)}, f32[16,16,128]{2,1,0:T(8,128)S(1)}, u32[]{:S(2)}, u32[]{:S(2)}) collective-permute-start(f32[16,16,128]{2,1,0:T(8,128)S(1)} %add.25), channel_id=1, source_target_pairs={{2,3},{6,7},{10,11},{14,15},{18,19},{22,23},{26,27},{30,31}} | collective-permute-start | bytes 393224 | tf_op jit(solution)/shard_map/ppermute | solution.py:460
  (4 other events, 10.4 us)

commit v2 on v0

v2 whole, which is shorter than its diff:
```python
import math

import jax
import jax.numpy as jnp
from jax import lax
from jax.experimental import pallas as pl
from jax.experimental.pallas import tpu as pltpu
from jax.sharding import PartitionSpec as P


STEPS = 4
ROWS = 8
SHARES = (5, 5, 4, 2)
GROUPS = 4
LONGEST = 5
VMEM_LIMIT = 10 * 1024 * 1024


HBM = pl.BlockSpec(memory_space=pltpu.HBM)
VMEM = pl.BlockSpec(memory_space=pltpu.VMEM)


def pieces_of(width):
    tiles = width // ROWS
    total = sum(SHARES)
    ends = [tiles * sum(SHARES[: i + 1]) // total for i in range(len(SHARES))]
    starts = [0] + ends[:-1]
    return [(a * ROWS, (b - a) * ROWS) for a, b in zip(starts, ends)]


def groups_of(planes):
    count = math.gcd(planes, GROUPS)
    return count, planes // count


def spans_of(planes, count):
    ends = [planes * (n + 1) // count for n in range(count)]
    return [(a, b - a) for a, b in zip([0] + ends[:-1], ends)]


def parts_of(k):
    return max(1, math.ceil(SHARES[k] / LONGEST))


def take_rows(block, bottom, top, y, width, depth):
    for x in range(0, width, ROWS):
        bottom[y, pl.ds(x, ROWS), :] = block[y, pl.ds(x * depth, ROWS, stride=depth), :]
        top[y, pl.ds(x, ROWS), :] = block[y, pl.ds(x * depth + depth - 1, ROWS, stride=depth), :]


def take_sides(block, rows, edges, lead, trail, width, depth):
    planes = block.shape[0]
    rows[0] = block[planes - 1]
    rows[1] = block[0]
    columns = ([0] if lead else []) + ([width - 1] if trail else [])
    for column, edge in zip(columns, edges):
        edge[...] = block[:, pl.ds(column * depth, depth), :]


def prepare_kernel(plan, tracer, *refs):
    first, width, depth, lead, trail, extras = plan
    refs = refs[extras:]
    block, bottom, top, rows = refs[:4]
    edges = refs[4 : 4 + lead + trail]
    (sem_in,) = refs[4 + lead + trail :]
    planes = block.shape[0]
    count, each = groups_of(planes)

    def load(g):
        span = pl.ds(g * each, each)
        return pltpu.make_async_copy(
            tracer.at[span, pl.ds(first * depth, width * depth)], block.at[span], sem_in.at[g]
        )

    for g in range(count):
        load(g).start()
    for g in range(count):
        load(g).wait()
        for y in range(g * each, (g + 1) * each):
            take_rows(block, bottom, top, y, width, depth)
    take_sides(block, rows, edges, lead, trail, width, depth)


def scaled(value, scale):
    return value * scale[0] if scale[1] else value / scale[0]


def step_kernel(plan, *refs):
    width, depth, first, where, lead, trail, load_rest, last, parts, scale, extras = plan
    old, left, right, lower_y, upper_y, low, high, conductance, source = refs[:9]
    refs = refs[9 + extras :]
    if last:
        field, sums = refs[:2]
        totals = refs[2 : 2 + parts]
        new = refs[2 + parts]
        refs = refs[3 + parts :]
    else:
        new, bottom, top, rows = refs[:4]
        edges = refs[4 : 4 + lead + trail]
        refs = refs[4 + lead + trail :]
    planes = new.shape[0]
    cells = width * depth
    spans = spans_of(planes, parts if last else math.gcd(planes, GROUPS) if load_rest else 1)
    loads = []
    if load_rest:
        coefficient, extra, sem_in = refs[0], refs[1], refs[2]
        refs = refs[3:]
        for g, span in enumerate(spans):
            span = pl.ds(*span)
            part = pl.ds(first * depth, cells)
            loads.append(
                [
                    pltpu.make_async_copy(ref.at[span, part], to.at[span], sem_in.at[n, g])
                    for n, (ref, to) in enumerate(((conductance, coefficient), (source, extra)))
                ]
            )
            for copy in loads[-1]:
                copy.start()
    else:
        coefficient, extra = conductance, source

    here = lax.broadcasted_iota(jnp.int32, (depth, new.shape[2]), 0)
    at_low = here == 0
    at_high = here == depth - 1

    def plane(y, before_y, after_y, g):
        def column(x):
            if x < 0:
                return left[y, pl.ds(where[0] * depth, depth), :]
            if x == width:
                return right[y, pl.ds(where[1] * depth, depth), :]
            return old[y, pl.ds(x * depth, depth), :]

        before, centre = column(-1), column(0)
        for x in range(width):
            span = pl.ds(x * depth, depth)
            after = column(x + 1)
            below = jnp.where(at_low, low[y, pl.ds(x, depth, stride=0), :], pltpu.roll(centre, 1, 0))
            above = jnp.where(
                at_high, high[y, pl.ds(x, depth, stride=0), :], pltpu.roll(centre, depth - 1, 0)
            )
            near = (before_y(span) + after_y(span)) + (before + after) + (below + above) - 6.0 * centre
            new[y, span, :] = centre + coefficient[y, span, :] * near + extra[y, span, :]
            before, centre = centre, after
        if last:
            for x in range(0, width, ROWS):
                total = None
                for z in range(depth):
                    span = pl.ds(x * depth + z, ROWS, stride=depth)
                    value = scaled(new[y, span, :], scale)
                    total = value if z == 0 else total + value
                    sums[y, span, :] = total
                totals[g][y - spans[g][0], pl.ds(x, ROWS), :] = total
        else:
            take_rows(new, bottom, top, y, width, depth)

    def of_plane(y):
        return lambda span: old[y, span, :]

    def outer(ref, row):
        return lambda span: ref[row, span, :]

    def save(g):
        span = pl.ds(*spans[g])
        return pltpu.make_async_copy(
            new.at[span], field.at[span, pl.ds(first * depth, cells)], refs[0].at[g]
        )

    for g, (start, length) in enumerate(spans):
        for copy in loads[g] if load_rest else []:
            copy.wait()
        stop = start + length
        if start == 0:
            plane(0, outer(lower_y, where[2]), of_plane(1), g)
            start = 1
        top_plane = stop == planes
        if top_plane:
            stop = planes - 1

        def walk(y, carry):
            plane(y, of_plane(y - 1), of_plane(y + 1), g)
            return carry

        lax.fori_loop(start, stop, walk, 0)
        if top_plane:
            plane(planes - 1, of_plane(planes - 2), outer(upper_y, where[3]), g)
        if last:
            save(g).start()
    if last:
        for g in range(len(spans)):
            save(g).wait()
    else:
        take_sides(new, rows, edges, lead, trail, width, depth)


def potential_kernel(plan, *refs):
    width, depth, first, parts, earlier, extras = plan
    sums = refs[0]
    offsets = refs[1 : 1 + parts * earlier]
    potential, out, sem_out = refs[1 + parts * earlier + extras :]
    spans = spans_of(sums.shape[0], parts)

    def save(g):
        span = pl.ds(*spans[g])
        return pltpu.make_async_copy(
            out.at[span], potential.at[span, pl.ds(first * depth, width * depth)], sem_out.at[g]
        )

    for g, (start, length) in enumerate(spans):
        below = offsets[g * earlier : (g + 1) * earlier]

        def walk(y, carry):
            for x in range(width):
                row = pl.ds(x, depth, stride=0)
                total = below[0][y - start, row, :]
                for offset in below[1:]:
                    total = total + offset[y - start, row, :]
                span = pl.ds(x * depth, depth)
                out[y, span, :] = sums[y, span, :] + total
            return carry

        lax.fori_loop(start, start + length, walk, 0)
        save(g).start()
    for g in range(parts):
        save(g).wait()


def ring(axis):
    count = lax.axis_size(axis)
    forward = [(i, (i + 1) % count) for i in range(count)]
    return forward, [(target, origin) for origin, target in forward]


def on_device(tracer, conductance, source):
    shape = tracer.shape
    planes, columns, depth, members = shape
    pieces = pieces_of(columns)
    last_piece = len(pieces) - 1
    flat = (planes, columns * depth, members)
    tracer, conductance, source = (v.reshape(flat) for v in (tracer, conductance, source))
    count, _ = groups_of(planes)

    def far(*dims):
        return pltpu.HBM(dims, jnp.float32)

    def near(*dims):
        return pltpu.VMEM(dims, jnp.float32)

    def call(kernel, operands, specs, outs, out_specs, scratch=(), aliases=None):
        operands = [
            pltpu.with_memory_space_constraint(v, pltpu.VMEM if spec is VMEM else pltpu.HBM)
            for v, spec in zip(operands, specs)
        ]
        return pl.pallas_call(
            kernel,
            out_shape=outs,
            in_specs=specs,
            out_specs=out_specs,
            input_output_aliases=aliases or {},
            scratch_shapes=list(scratch),
            compiler_params=pltpu.CompilerParams(vmem_limit_bytes=VMEM_LIMIT),
        )(*operands)

    def ends(k):
        return int(k == 0), int(k == last_piece)

    def block(k):
        return near(planes, pieces[k][1] * depth, members)

    def outer_arrays(k):
        width = pieces[k][1]
        return [
            near(planes, width, members),
            near(planes, width, members),
            near(2, width * depth, members),
        ] + [near(planes, depth, members)] * sum(ends(k))

    def prepare(k, token):
        plan = (*pieces[k], depth, *ends(k), len(token))

        def kernel(*refs):
            prepare_kernel(plan, *refs)

        outs = [block(k)] + outer_arrays(k)
        return call(
            kernel,
            [tracer] + token,
            [HBM] + [VMEM] * len(token),
            outs,
            [VMEM] * len(outs),
            [pltpu.SemaphoreType.DMA((count,))],
        )

    def advance(k, step, where, operands, whole, token):
        first, width = pieces[k]
        load_rest, last = step == 0, step == STEPS - 1
        rest = HBM if load_rest else VMEM
        specs = [VMEM] * 7 + [rest] * 2 + [VMEM] * len(token)
        operands = operands + token
        aliases = {}
        if last and k > 0:
            aliases = {len(operands): 0}
            operands = operands + [whole]
            specs = specs + [HBM]
        parts = parts_of(k)
        plan = (width, depth, first, where, *ends(k), load_rest, last, parts, scale, len(operands) - 9)

        def kernel(*refs):
            step_kernel(plan, *refs)

        if last:
            outs = [far(*flat), block(k)]
            outs += [near(length, width, members) for _, length in spans_of(planes, parts)]
            out_specs = [HBM] + [VMEM] * (1 + parts)
            scratch = [
                pltpu.VMEM((planes, width * depth, members), jnp.float32),
                pltpu.SemaphoreType.DMA((parts,)),
            ]
        else:
            outs = [block(k)] + outer_arrays(k) + [block(k)] * (2 * load_rest)
            out_specs = [VMEM] * len(outs)
            scratch = [pltpu.SemaphoreType.DMA((2, count))] * load_rest
        return call(kernel, operands, specs, outs, out_specs, scratch, aliases)

    def finish(k, sums, offsets, whole):
        first, width = pieces[k]
        parts, earlier = len(offsets), len(offsets[0])
        operands = [sums] + [v for part in offsets for v in part]
        specs = [VMEM] * len(operands)
        aliases = {}
        if k > 0:
            aliases = {len(operands): 0}
            operands = operands + [whole]
            specs = specs + [HBM]
        extras = len(operands) - 1 - parts * earlier
        plan = (width, depth, first, parts, earlier, extras)

        def kernel(*refs):
            potential_kernel(plan, *refs)

        scratch = [
            pltpu.VMEM((planes, width * depth, members), jnp.float32),
            pltpu.SemaphoreType.DMA((parts,)),
        ]
        return call(kernel, operands, specs, [far(*flat)], [HBM], scratch, aliases)[0]

    blocks = lax.axis_size("pz")
    cells_along = depth * blocks
    exact = cells_along & (cells_along - 1) == 0
    scale = (1.0 / cells_along, True) if exact else (float(cells_along), False)
    z_up, z_down = ring("pz")
    y_up, y_down = ring("py")
    x_up, x_down = ring("px")

    def exchange(k, outer, sides):
        bottom, top, rows = outer[:3]
        edges = list(outer[3:])
        from_below = lax.ppermute(top, "pz", z_up)
        from_above = lax.ppermute(bottom, "pz", z_down)
        if len(y_up) <= 2:
            rows = lax.ppermute(rows, "py", y_up)
            lower_y, upper_y = (rows, 0), (rows, 1)
        else:
            lower_y = (lax.ppermute(rows[0:1], "py", y_up), 0)
            upper_y = (lax.ppermute(rows[1:2], "py", y_down), 0)
        lead, trail = ends(k)
        if lead:
            sides["right"] = lax.ppermute(edges.pop(0), "px", x_down)
        if trail:
            sides["left"] = lax.ppermute(edges.pop(0), "px", x_up)
        return lower_y, upper_y, from_below, from_above

    fields, rest, halos, sides, token = [], [], [], {}, []
    for k in range(len(pieces)):
        field, *outer = prepare(k, token)
        token = [outer[0]]
        fields.append(field)
        rest.append((conductance, source))
        halos.append(exchange(k, outer, sides))
    token = []
    end, totals = None, []
    for step in range(STEPS):
        next_fields, next_halos, next_sides = [], [], {}
        for k, (first, width) in enumerate(pieces):
            lower_y, upper_y, from_below, from_above = halos[k]
            left = (fields[k - 1], pieces[k - 1][1] - 1) if k > 0 else (sides["left"], 0)
            right = (fields[k + 1], 0) if k < last_piece else (sides["right"], 0)
            where = (left[1], right[1], lower_y[1], upper_y[1])
            operands = [fields[k], left[0], right[0], lower_y[0], upper_y[0]]
            operands += [from_below, from_above, *rest[k]]
            results = list(advance(k, step, where, operands, end, token))
            if step == STEPS - 1:
                end, field, *total = results
                token = []
                next_fields.append(field)
                totals.append(total)
                continue
            if step == 0:
                rest[k] = tuple(results[-2:])
                results = results[:-2]
            token = [results[1]]
            next_fields.append(results[0])
            next_halos.append(exchange(k, results[1:], next_sides))
        fields, halos, sides = next_fields, next_halos, next_sides

    potential = None
    for k in range(len(pieces)):
        offsets = []
        for carried in totals[k]:
            offsets.append([])
            for hop in range(blocks - 1):
                arrived = lax.ppermute(carried, "pz", [(hop, hop + 1)])
                offsets[-1].append(arrived)
                carried = carried + arrived
        potential = finish(k, fields[k], offsets, potential)
    return (potential.reshape(shape), end.reshape(shape))


def solution(mesh):
    placed = P("py", "px", "pz", None)

    return jax.shard_map(
        on_device,
        mesh=mesh,
        in_specs=(placed, placed, placed),
        out_specs=(placed, placed),
        check_vma=False,
    )
```

time: 1190 us -> 255 us (0.21)
  the two profiles are of different devices: /device:TPU:0 before, /device:TPU:24 now
where the time goes in v2:
time: 255 us
  waiting for transfers between devices  125 us (49%)
  starting transfers between devices  83.3 us (33%)
  Pallas kernels  45.6 us (18%)
    ppermute x16, waiting for transfers between devices, exchange(): from_above = lax.ppermute(bottom, 'pz', z_down)  47.7 us
    pallas_call x24, Pallas kernels, call(): pl.pallas_call(kernel, out_shape=outs, in_specs=specs, out_specs=out_spec...  45.6 us
    ppermute x16, waiting for transfers between devices, exchange(): from_below = lax.ppermute(top, 'pz', z_up)  44.6 us
    ppermute x16, starting transfers between devices, exchange(): from_below = lax.ppermute(top, 'pz', z_up)  31.3 us
    ppermute x16, starting transfers between devices, exchange(): rows = lax.ppermute(rows, 'py', y_up)  21.8 us
    ppermute x16, starting transfers between devices, exchange(): from_above = lax.ppermute(bottom, 'pz', z_down)  16.1 us
    ppermute x12, waiting for transfers between devices, on_device(): arrived = lax.ppermute(carried, 'pz', [(hop, hop + 1)])  15.5 us
    ppermute x12, starting transfers between devices, on_device(): arrived = lax.ppermute(carried, 'pz', [(hop, hop + 1)])  10.6 us
  transfers between devices with their start and end apart: 68, of which 33 were waited for; matrix products, arithmetic and copies ran while one was open for 0% of the time, Pallas kernels for 17%

profile of v2, /device:TPU:24, one launch (start us, length us, event | category | flops | bytes accessed | tf_op | source)
XLA Modules:
  0.0 254.8 jit_solution(17883578049148160455)
XLA Ops:
  0.6 1.8 shard_map.50
  4.9 1.8 shard_map.51
  6.7 1.6 shard_map.52
  10.5 1.8 collective-permute-start.13
  12.3 1.6 collective-permute-done.10.refs_1_
  15.4 5.6 %collective-permute-done.1.refs_3_.refs_4_ = f32[2,128,128]{2,1,0:T(8,128)S(1)} collective-permute-done((f32[2,128,128]{2,1,0:T(8,128)S(1)}, f32[2,128,128]{2,1,0:T(8,128)S(1)}, u32[]{:S(2)}, u32[]{:S(2)}) %collective-permute-start.1) | collective-permute-done | bytes 131104 | tf_op jit(solution)/shard_map/ppermute | solution.py:361
  21.0 1.7 collective-permute-start.7
  22.8 1.8 collective-permute-start.6
  24.6 3.1 %collective-permute-done.12.refs_5_ = f32[16,40,128]{2,1,0:T(8,128)S(1)} collective-permute-done((f32[16,40,128]{2,1,0:T(8,128)S(1)}, f32[16,40,128]{2,1,0:T(8,128)S(1)}, u32[]{:S(2)}, u32[]{:S(2)}) %collective-permute-start.12) | collective-permute-done | bytes 327712 | tf_op jit(solution)/shard_map/ppermute | solution.py:358
  27.7 2.0 collective-permute-start.9
  29.7 2.9 %shard_map.54 = (f32[16,320,128]{2,1,0:T(8,128)S(1)}, f32[16,40,128]{2,1,0:T(8,128)S(1)}, f32[16,40,128]{2,1,0:T(8,128)S(1)}, f32[2,320,128]{2,1,0:T(8,128)S(1)}...) custom-call(f32[16,320,128]{2,1,0:T(8,128)S(1)} %get-tuple-element.106.refs_0_.refs_1_, ...), custom_call_target="tpu_custom_call" | custom-call | tf_op jit(solution)/shard_map/pallas_call | solution.py:254
  32.7 6.3 %collective-permute-done.5.refs_5_ = f32[16,32,128]{2,1,0:T(8,128)S(1)} collective-permute-done((f32[16,32,128]{2,1,0:T(8,128)S(1)}, f32[16,32,128]{2,1,0:T(8,128)S(1)}, u32[]{:S(2)}, u32[]{:S(2)}) %collective-permute-start.5) | collective-permute-done | bytes 262176 | tf_op jit(solution)/shard_map/ppermute | solution.py:358
  42.5 10.4 %collective-permute-done.8.refs_5_ = f32[16,40,128]{2,1,0:T(8,128)S(1)} collective-permute-done((f32[16,40,128]{2,1,0:T(8,128)S(1)}, f32[16,40,128]{2,1,0:T(8,128)S(1)}, u32[]{:S(2)}, u32[]{:S(2)}) %collective-permute-start.8) | collective-permute-done | bytes 327712 | tf_op jit(solution)/shard_map/ppermute | solution.py:358
  53.4 1.6 collective-permute-start.26
  55.0 2.9 %shard_map.55 = (f32[16,320,128]{2,1,0:T(8,128)S(1)}, f32[16,40,128]{2,1,0:T(8,128)S(1)}, f32[16,40,128]{2,1,0:T(8,128)S(1)}, f32[2,320,128]{2,1,0:T(8,128)S(1)}...) custom-call(f32[16,320,128]{2,1,0:T(8,128)S(1)} %get-tuple-element.103.refs_2_.refs_0_.refs_1_, ...), custom_call_target="tpu_custom_call" | custom-call | tf_op jit(solution)/shard_map/pallas_call | solution.py:254
  57.9 2.5 shard_map.56
  60.5 1.9 shard_map.57
  62.9 1.5 collective-permute-start.21
  64.4 1.7 collective-permute-done.24.refs_1_
  66.1 1.7 collective-permute-start.22
  68.2 1.5 collective-permute-start.15
  69.7 5.3 %collective-permute-done.27.refs_6_ = f32[16,40,128]{2,1,0:T(8,128)S(1)} collective-permute-done((f32[16,40,128]{2,1,0:T(8,128)S(1)}, f32[16,40,128]{2,1,0:T(8,128)S(1)}, u32[]{:S(2)}, u32[]{:S(2)}) %collective-permute-start.27) | collective-permute-done | bytes 327712 | tf_op jit(solution)/shard_map/ppermute | solution.py:359
  76.9 5.1 %collective-permute-done.22.refs_5_ = f32[16,40,128]{2,1,0:T(8,128)S(1)} collective-permute-done((f32[16,40,128]{2,1,0:T(8,128)S(1)}, f32[16,40,128]{2,1,0:T(8,128)S(1)}, u32[]{:S(2)}, u32[]{:S(2)}) %collective-permute-start.22) | collective-permute-done | bytes 327712 | tf_op jit(solution)/shard_map/ppermute | solution.py:358
  82.6 6.4 %collective-permute-done.23.refs_6_ = f32[16,40,128]{2,1,0:T(8,128)S(1)} collective-permute-done((f32[16,40,128]{2,1,0:T(8,128)S(1)}, f32[16,40,128]{2,1,0:T(8,128)S(1)}, u32[]{:S(2)}, u32[]{:S(2)}) %collective-permute-start.23) | collective-permute-done | bytes 327712 | tf_op jit(solution)/shard_map/ppermute | solution.py:359
  89.3 1.6 shard_map.58
  90.9 1.6 shard_map.59
  92.4 1.6 collective-permute-start.35
  94.0 7.9 %collective-permute-done.16.refs_5_ = f32[16,16,128]{2,1,0:T(8,128)S(1)} collective-permute-done((f32[16,16,128]{2,1,0:T(8,128)S(1)}, f32[16,16,128]{2,1,0:T(8,128)S(1)}, u32[]{:S(2)}, u32[]{:S(2)}) %collective-permute-start.16) | collective-permute-done | bytes 131104 | tf_op jit(solution)/shard_map/ppermute | solution.py:358
  103.5 3.8 %collective-permute-start.40 = (f32[16,40,128]{2,1,0:T(8,128)S(1)}, f32[16,40,128]{2,1,0:T(8,128)S(1)}, u32[]{:S(2)}, u32[]{:S(2)}) collective-permute-start(f32[16,40,128]{2,1,0:T(8,128)S(1)} %get-tuple-element.155), channel_id=1, source_target_pairs={{0,1},{1,2},{2,3},{3,0},{4,5},{5,6},{6,7},{7,4},{8,9},{9,10},{10,1... | collective-permute-start | bytes 983048 | tf_op jit(solution)/shard_map/ppermute | solution.py:358
  108.5 1.6 collective-permute-done.17.refs_6_
  110.9 3.7 %collective-permute-done.38.refs_1_ = f32[16,8,128]{2,1,0:T(8,128)S(1)} collective-permute-done((f32[16,8,128]{2,1,0:T(8,128)S(1)}, f32[16,8,128]{2,1,0:T(8,128)S(1)}, u32[]{:S(2)}, u32[]{:S(2)}) %collective-permute-start.38) | collective-permute-done | bytes 65568 | tf_op jit(solution)/shard_map/ppermute | solution.py:370
  114.6 2.2 collective-permute-start.36
  118.2 4.0 %collective-permute-start.33 = (f32[16,32,128]{2,1,0:T(8,128)S(1)}, f32[16,32,128]{2,1,0:T(8,128)S(1)}, u32[]{:S(2)}, u32[]{:S(2)}) collective-permute-start(f32[16,32,128]{2,1,0:T(8,128)S(1)} %get-tuple-element.149), channel_id=1, source_target_pairs={{0,1},{1,2},{2,3},{3,0},{4,5},{5,6},{6,7},{7,4},{8,9},{9,10},{10,1... | collective-permute-start | bytes 786440 | tf_op jit(solution)/shard_map/ppermute | solution.py:358
  122.2 2.0 collective-permute-done.41.refs_6_
  124.9 1.6 shard_map.62
  126.5 4.8 %collective-permute-done.36.refs_5_ = f32[16,40,128]{2,1,0:T(8,128)S(1)} collective-permute-done((f32[16,40,128]{2,1,0:T(8,128)S(1)}, f32[16,40,128]{2,1,0:T(8,128)S(1)}, u32[]{:S(2)}, u32[]{:S(2)}) %collective-permute-start.36) | collective-permute-done | bytes 327712 | tf_op jit(solution)/shard_map/ppermute | solution.py:358
  131.3 7.0 %collective-permute-done.37.refs_6_ = f32[16,40,128]{2,1,0:T(8,128)S(1)} collective-permute-done((f32[16,40,128]{2,1,0:T(8,128)S(1)}, f32[16,40,128]{2,1,0:T(8,128)S(1)}, u32[]{:S(2)}, u32[]{:S(2)}) %collective-permute-start.37) | collective-permute-done | bytes 327712 | tf_op jit(solution)/shard_map/ppermute | solution.py:359
  138.3 1.6 shard_map.63
  139.9 1.6 collective-permute-start.49
  142.0 2.5 collective-permute-start.30
  144.5 3.5 %collective-permute-start.31 = (f32[16,16,128]{2,1,0:T(8,128)S(1)}, f32[16,16,128]{2,1,0:T(8,128)S(1)}, u32[]{:S(2)}, u32[]{:S(2)}) collective-permute-start(f32[16,16,128]{2,1,0:T(8,128)S(1)} %get-tuple-element.146.refs_9_), channel_id=1, source_target_pairs={{1,0},{2,1},{3,2},{0,3},{5,4},{6,5},{7,6},{4,7},{9,8},{10,9},{11,1... | collective-permute-start | bytes 393224 | tf_op jit(solution)/shard_map/ppermute | solution.py:359
  148.0 1.6 collective-permute-done.34.refs_6_
  151.5 1.5 collective-permute-start.53
  155.7 1.7 collective-permute-start.55
  160.9 1.6 collective-permute-start.46
  162.8 2.6 %collective-permute-start.47 = (f32[16,32,128]{2,1,0:T(8,128)S(1)}, f32[16,32,128]{2,1,0:T(8,128)S(1)}, u32[]{:S(2)}, u32[]{:S(2)}) collective-permute-start(f32[16,32,128]{2,1,0:T(8,128)S(1)} %get-tuple-element.167), channel_id=1, source_target_pairs={{0,1},{1,2},{2,3},{3,0},{4,5},{5,6},{6,7},{7,4},{8,9},{9,10},{10,1... | collective-permute-start | bytes 786440 | tf_op jit(solution)/shard_map/ppermute | solution.py:358
  165.4 4.6 %collective-permute-done.55.refs_6_ = f32[16,40,128]{2,1,0:T(8,128)S(1)} collective-permute-done((f32[16,40,128]{2,1,0:T(8,128)S(1)}, f32[16,40,128]{2,1,0:T(8,128)S(1)}, u32[]{:S(2)}, u32[]{:S(2)}) %collective-permute-start.55) | collective-permute-done | bytes 327712 | tf_op jit(solution)/shard_map/ppermute | solution.py:359
  170.6 3.5 %shard_map.66 = (f32[16,1024,128]{2,1,0:T(8,128)}, f32[16,320,128]{2,1,0:T(8,128)S(1)}, f32[16,40,128]{2,1,0:T(8,128)S(1)}) custom-call(f32[16,320,128]{2,1,0:T(8,128)S(1)} %get-tuple-element.168.refs_0_.refs_1_, f32[16,8,128]{2,1,0:T(8,128)S(1)} %collective-permute-done.52.refs_1_, f32[16,320,128]{2,1,0:T(8,128)S(1)} %get-tuple-element.165.refs_2_.refs_0_.refs_1_, ...), custom_call_target="tpu_custom_call" | custom-call | tf_op jit(solution)/shard_map/pallas_call | solution.py:254
  174.0 2.8 %collective-permute-done.50.refs_5_ = f32[16,40,128]{2,1,0:T(8,128)S(1)} collective-permute-done((f32[16,40,128]{2,1,0:T(8,128)S(1)}, f32[16,40,128]{2,1,0:T(8,128)S(1)}, u32[]{:S(2)}, u32[]{:S(2)}) %collective-permute-start.50) | collective-permute-done | bytes 327712 | tf_op jit(solution)/shard_map/ppermute | solution.py:358
  177.5 6.5 %collective-permute-done.51.refs_6_ = f32[16,40,128]{2,1,0:T(8,128)S(1)} collective-permute-done((f32[16,40,128]{2,1,0:T(8,128)S(1)}, f32[16,40,128]{2,1,0:T(8,128)S(1)}, u32[]{:S(2)}, u32[]{:S(2)}) %collective-permute-start.51) | collective-permute-done | bytes 327712 | tf_op jit(solution)/shard_map/ppermute | solution.py:359
  184.0 3.5 %shard_map.67 = (f32[16,1024,128]{2,1,0:T(8,128)}, f32[16,320,128]{2,1,0:T(8,128)S(1)}, f32[16,40,128]{2,1,0:T(8,128)S(1)}) custom-call(f32[16,320,128]{2,1,0:T(8,128)S(1)} %get-tuple-element.165.refs_2_.refs_0_.refs_1_, f32[16,320,128]{2,1,0:T(8,128)S(1)} %get-tuple-element.168.refs_0_.refs_1_, ...), custom_call_target="tpu_custom_call", output_to_operand_aliasing={{0}: (9, {})} | custom-call | tf_op jit(solution)/shard_map/pallas_call | solution.py:254
  189.4 5.8 %collective-permute-done.48.refs_6_ = f32[16,32,128]{2,1,0:T(8,128)S(1)} collective-permute-done((f32[16,32,128]{2,1,0:T(8,128)S(1)}, f32[16,32,128]{2,1,0:T(8,128)S(1)}, u32[]{:S(2)}, u32[]{:S(2)}) %collective-permute-start.48) | collective-permute-done | bytes 262176 | tf_op jit(solution)/shard_map/ppermute | solution.py:359
  195.3 2.8 %shard_map.68 = (f32[16,1024,128]{2,1,0:T(8,128)}, f32[16,256,128]{2,1,0:T(8,128)S(1)}, f32[16,32,128]{2,1,0:T(8,128)S(1)}) custom-call(f32[16,256,128]{2,1,0:T(8,128)S(1)} %get-tuple-element.160.refs_2_.refs_0_.refs_1_, f32[16,320,128]{2,1,0:T(8,128)S(1)} %get-tuple-element.165.refs_2_.refs_0_.refs_1_, ...), custom_call_target="tpu_custom_call", output_to_operand_aliasing={{0}: (9, {})} | custom-call | tf_op jit(solution)/shard_map/pallas_call | solution.py:254
  202.2 1.9 collective-permute-done.42.refs_2_
  204.1 9.5 %collective-permute-start.44 = (f32[16,16,128]{2,1,0:T(8,128)S(1)}, f32[16,16,128]{2,1,0:T(8,128)S(1)}, u32[]{:S(2)}, u32[]{:S(2)}) collective-permute-start(f32[16,16,128]{2,1,0:T(8,128)S(1)} %get-tuple-element.163), channel_id=1, source_target_pairs={{0,1},{1,2},{2,3},{3,0},{4,5},{5,6},{6,7},{7,4},{8,9},{9,10},{10,1... | collective-permute-start | bytes 393224 | tf_op jit(solution)/shard_map/ppermute | solution.py:358
  214.3 2.6 %collective-permute-done.44.refs_5_ = f32[16,16,128]{2,1,0:T(8,128)S(1)} collective-permute-done((f32[16,16,128]{2,1,0:T(8,128)S(1)}, f32[16,16,128]{2,1,0:T(8,128)S(1)}, u32[]{:S(2)}, u32[]{:S(2)}) %collective-permute-start.44) | collective-permute-done | bytes 131104 | tf_op jit(solution)/shard_map/ppermute | solution.py:358
  216.9 6.5 %collective-permute-done.45.refs_6_ = f32[16,16,128]{2,1,0:T(8,128)S(1)} collective-permute-done((f32[16,16,128]{2,1,0:T(8,128)S(1)}, f32[16,16,128]{2,1,0:T(8,128)S(1)}, u32[]{:S(2)}, u32[]{:S(2)}) %collective-permute-start.45) | collective-permute-done | bytes 131104 | tf_op jit(solution)/shard_map/ppermute | solution.py:359
  223.4 1.8 shard_map.69
  232.0 6.4 %collective-permute-done.67.refs_3_ = f32[16,40,128]{2,1,0:T(8,128)S(1)} collective-permute-done((f32[16,40,128]{2,1,0:T(8,128)S(1)}, f32[16,40,128]{2,1,0:T(8,128)S(1)}, u32[]{:S(2)}, u32[]{:S(2)}) %collective-permute-start.67) | collective-permute-done | bytes 327712 | tf_op jit(solution)/shard_map/ppermute | solution.py:412
  238.5 2.1 shard_map.70.refs_4_
  240.6 4.9 %collective-permute-done.64.refs_3_ = f32[16,40,128]{2,1,0:T(8,128)S(1)} collective-permute-done((f32[16,40,128]{2,1,0:T(8,128)S(1)}, f32[16,40,128]{2,1,0:T(8,128)S(1)}, u32[]{:S(2)}, u32[]{:S(2)}) %collective-permute-start.64) | collective-permute-done | bytes 327712 | tf_op jit(solution)/shard_map/ppermute | solution.py:412
  245.5 2.1 shard_map.71.refs_4_
  247.6 3.5 %collective-permute-done.61.refs_3_ = f32[16,32,128]{2,1,0:T(8,128)S(1)} collective-permute-done((f32[16,32,128]{2,1,0:T(8,128)S(1)}, f32[16,32,128]{2,1,0:T(8,128)S(1)}, u32[]{:S(2)}, u32[]{:S(2)}) %collective-permute-start.61) | collective-permute-done | bytes 262176 | tf_op jit(solution)/shard_map/ppermute | solution.py:412
  251.1 1.8 shard_map.72.refs_4_
  (104 shorter events, 44.8 us)
Async XLA Ops:
  2.4 8.1 %collective-permute-start = (f32[16,8,128]{2,1,0:T(8,128)S(1)}, f32[16,8,128]{2,1,0:T(8,128)S(1)}, u32[]{:S(2)}, u32[]{:S(2)}) collective-permute-start(f32[16,8,128]{2,1,0:T(8,128)S(1)} %get-tuple-element.99), channel_id=1, source_target_pairs={{4,0},{8,4},{12,8},{0,12},{5,1},{9,5},{13,9},{1,13},{6,2},{10,6},{... | collective-permute-start | bytes 196616 | tf_op jit(solution)/shard_map/ppermute | solution.py:368
  3.4 19.4 %collective-permute-start.11 = (f32[2,320,128]{2,1,0:T(8,128)S(1)}, f32[2,320,128]{2,1,0:T(8,128)S(1)}, u32[]{:S(2)}, u32[]{:S(2)}) collective-permute-start(f32[2,320,128]{2,1,0:T(8,128)S(1)} %get-tuple-element.110), channel_id=1, source_target_pairs={{0,16},{16,0},{1,17},{17,1},{2,18},{18,2},{3,19},{19,3},{4,20},{20... | collective-permute-start | bytes 983048 | tf_op jit(solution)/shard_map/ppermute | solution.py:361
  8.3 12.7 %collective-permute-start.4 = (f32[2,256,128]{2,1,0:T(8,128)S(1)}, f32[2,256,128]{2,1,0:T(8,128)S(1)}, u32[]{:S(2)}, u32[]{:S(2)}) collective-permute-start(f32[2,256,128]{2,1,0:T(8,128)S(1)} %get-tuple-element.104), channel_id=1, source_target_pairs={{0,16},{16,0},{1,17},{17,1},{2,18},{18,2},{3,19},{19,3},{4,20},{20... | collective-permute-start | bytes 786440 | tf_op jit(solution)/shard_map/ppermute | solution.py:361
  10.1 3.7 %collective-permute-start.10 = (f32[16,8,128]{2,1,0:T(8,128)S(1)}, f32[16,8,128]{2,1,0:T(8,128)S(1)}, u32[]{:S(2)}, u32[]{:S(2)}) collective-permute-start(f32[16,8,128]{2,1,0:T(8,128)S(1)} %get-tuple-element.109), channel_id=1, source_target_pairs={{0,4},{4,8},{8,12},{12,0},{1,5},{5,9},{9,13},{13,1},{2,6},{6,10},{... | collective-permute-start | bytes 196616 | tf_op jit(solution)/shard_map/ppermute | solution.py:370
  10.2 17.5 %collective-permute-start.12 = (f32[16,40,128]{2,1,0:T(8,128)S(1)}, f32[16,40,128]{2,1,0:T(8,128)S(1)}, u32[]{:S(2)}, u32[]{:S(2)}) collective-permute-start(f32[16,40,128]{2,1,0:T(8,128)S(1)} %get-tuple-element.111), channel_id=1, source_target_pairs={{0,1},{1,2},{2,3},{3,0},{4,5},{5,6},{6,7},{7,4},{8,9},{9,10},{10,1... | collective-permute-start | bytes 983048 | tf_op jit(solution)/shard_map/ppermute | solution.py:358
  10.5 17.2 %collective-permute-start.13 = (f32[16,40,128]{2,1,0:T(8,128)S(1)}, f32[16,40,128]{2,1,0:T(8,128)S(1)}, u32[]{:S(2)}, u32[]{:S(2)}) collective-permute-start(f32[16,40,128]{2,1,0:T(8,128)S(1)} %get-tuple-element.94.refs_1_), channel_id=1, source_target_pairs={{1,0},{2,1},{3,2},{0,3},{5,4},{6,5},{7,6},{4,7},{9,8},{10,9},{11,1... | collective-permute-start | bytes 983048 | tf_op jit(solution)/shard_map/ppermute | solution.py:359
  13.9 7.2 %collective-permute-start.1 = (f32[2,128,128]{2,1,0:T(8,128)S(1)}, f32[2,128,128]{2,1,0:T(8,128)S(1)}, u32[]{:S(2)}, u32[]{:S(2)}) collective-permute-start(f32[2,128,128]{2,1,0:T(8,128)S(1)} %get-tuple-element.100), channel_id=1, source_target_pairs={{0,16},{16,0},{1,17},{17,1},{2,18},{18,2},{3,19},{19,3},{4,20},{20... | collective-permute-start | bytes 393224 | tf_op jit(solution)/shard_map/ppermute | solution.py:361
  21.0 17.9 %collective-permute-start.5 = (f32[16,32,128]{2,1,0:T(8,128)S(1)}, f32[16,32,128]{2,1,0:T(8,128)S(1)}, u32[]{:S(2)}, u32[]{:S(2)}) collective-permute-start(f32[16,32,128]{2,1,0:T(8,128)S(1)} %get-tuple-element.105), channel_id=1, source_target_pairs={{0,1},{1,2},{2,3},{3,0},{4,5},{5,6},{6,7},{7,4},{8,9},{9,10},{10,1... | collective-permute-start | bytes 786440 | tf_op jit(solution)/shard_map/ppermute | solution.py:358
  21.0 20.0 %collective-permute-start.7 = (f32[2,320,128]{2,1,0:T(8,128)S(1)}, f32[2,320,128]{2,1,0:T(8,128)S(1)}, u32[]{:S(2)}, u32[]{:S(2)}) collective-permute-start(f32[2,320,128]{2,1,0:T(8,128)S(1)} %get-tuple-element.107), channel_id=1, source_target_pairs={{0,16},{16,0},{1,17},{17,1},{2,18},{18,2},{3,19},{19,3},{4,20},{20... | collective-permute-start | bytes 983048 | tf_op jit(solution)/shard_map/ppermute | solution.py:361
  22.8 17.7 %collective-permute-start.6 = (f32[16,32,128]{2,1,0:T(8,128)S(1)}, f32[16,32,128]{2,1,0:T(8,128)S(1)}, u32[]{:S(2)}, u32[]{:S(2)}) collective-permute-start(f32[16,32,128]{2,1,0:T(8,128)S(1)} %get-tuple-element.96.refs_1_), channel_id=1, source_target_pairs={{1,0},{2,1},{3,2},{0,3},{5,4},{6,5},{7,6},{4,7},{9,8},{10,9},{11,1... | collective-permute-start | bytes 786440 | tf_op jit(solution)/shard_map/ppermute | solution.py:359
  27.7 25.2 %collective-permute-start.8 = (f32[16,40,128]{2,1,0:T(8,128)S(1)}, f32[16,40,128]{2,1,0:T(8,128)S(1)}, u32[]{:S(2)}, u32[]{:S(2)}) collective-permute-start(f32[16,40,128]{2,1,0:T(8,128)S(1)} %get-tuple-element.108), channel_id=1, source_target_pairs={{0,1},{1,2},{2,3},{3,0},{4,5},{5,6},{6,7},{7,4},{8,9},{9,10},{10,1... | collective-permute-start | bytes 983048 | tf_op jit(solution)/shard_map/ppermute | solution.py:358
  27.7 25.7 %collective-permute-start.9 = (f32[16,40,128]{2,1,0:T(8,128)S(1)}, f32[16,40,128]{2,1,0:T(8,128)S(1)}, u32[]{:S(2)}, u32[]{:S(2)}) collective-permute-start(f32[16,40,128]{2,1,0:T(8,128)S(1)} %get-tuple-element.95.refs_1_), channel_id=1, source_target_pairs={{1,0},{2,1},{3,2},{0,3},{5,4},{6,5},{7,6},{4,7},{9,8},{10,9},{11,1... | collective-permute-start | bytes 983048 | tf_op jit(solution)/shard_map/ppermute | solution.py:359
  38.9 28.9 %collective-permute-start.25 = (f32[2,320,128]{2,1,0:T(8,128)S(1)}, f32[2,320,128]{2,1,0:T(8,128)S(1)}, u32[]{:S(2)}, u32[]{:S(2)}) collective-permute-start(f32[2,320,128]{2,1,0:T(8,128)S(1)} %get-tuple-element.134), channel_id=1, source_target_pairs={{0,16},{16,0},{1,17},{17,1},{2,18},{18,2},{3,19},{19,3},{4,20},{20... | collective-permute-start | bytes 983048 | tf_op jit(solution)/shard_map/ppermute | solution.py:361
  40.4 20.0 %collective-permute-start.2 = (f32[16,16,128]{2,1,0:T(8,128)S(1)}, f32[16,16,128]{2,1,0:T(8,128)S(1)}, u32[]{:S(2)}, u32[]{:S(2)}) collective-permute-start(f32[16,16,128]{2,1,0:T(8,128)S(1)} %get-tuple-element.101), channel_id=1, source_target_pairs={{0,1},{1,2},{2,3},{3,0},{4,5},{5,6},{6,7},{7,4},{8,9},{9,10},{10,1... | collective-permute-start | bytes 393224 | tf_op jit(solution)/shard_map/ppermute | solution.py:358
  41.0 19.5 %collective-permute-start.3 = (f32[16,16,128]{2,1,0:T(8,128)S(1)}, f32[16,16,128]{2,1,0:T(8,128)S(1)}, u32[]{:S(2)}, u32[]{:S(2)}) collective-permute-start(f32[16,16,128]{2,1,0:T(8,128)S(1)} %get-tuple-element.102), channel_id=1, source_target_pairs={{1,0},{2,1},{3,2},{0,3},{5,4},{6,5},{7,6},{4,7},{9,8},{10,9},{11,1... | collective-permute-start | bytes 393224 | tf_op jit(solution)/shard_map/ppermute | solution.py:359
  52.9 10.0 %collective-permute-start.14 = (f32[16,8,128]{2,1,0:T(8,128)S(1)}, f32[16,8,128]{2,1,0:T(8,128)S(1)}, u32[]{:S(2)}, u32[]{:S(2)}) collective-permute-start(f32[16,8,128]{2,1,0:T(8,128)S(1)} %get-tuple-element.117), channel_id=1, source_target_pairs={{4,0},{8,4},{12,8},{0,12},{5,1},{9,5},{13,9},{1,13},{6,2},{10,6},{... | collective-permute-start | bytes 196616 | tf_op jit(solution)/shard_map/ppermute | solution.py:368
  53.4 14.8 %collective-permute-start.26 = (f32[16,40,128]{2,1,0:T(8,128)S(1)}, f32[16,40,128]{2,1,0:T(8,128)S(1)}, u32[]{:S(2)}, u32[]{:S(2)}) collective-permute-start(f32[16,40,128]{2,1,0:T(8,128)S(1)} %get-tuple-element.135), channel_id=1, source_target_pairs={{0,1},{1,2},{2,3},{3,0},{4,5},{5,6},{6,7},{7,4},{8,9},{9,10},{10,1... | collective-permute-start | bytes 983048 | tf_op jit(solution)/shard_map/ppermute | solution.py:358
  62.4 3.7 %collective-permute-start.24 = (f32[16,8,128]{2,1,0:T(8,128)S(1)}, f32[16,8,128]{2,1,0:T(8,128)S(1)}, u32[]{:S(2)}, u32[]{:S(2)}) collective-permute-start(f32[16,8,128]{2,1,0:T(8,128)S(1)} %get-tuple-element.133), channel_id=1, source_target_pairs={{0,4},{4,8},{8,12},{12,0},{1,5},{5,9},{9,13},{13,1},{2,6},{6,10},{... | collective-permute-start | bytes 196616 | tf_op jit(solution)/shard_map/ppermute | solution.py:370
  62.4 12.5 %collective-permute-start.27 = (f32[16,40,128]{2,1,0:T(8,128)S(1)}, f32[16,40,128]{2,1,0:T(8,128)S(1)}, u32[]{:S(2)}, u32[]{:S(2)}) collective-permute-start(f32[16,40,128]{2,1,0:T(8,128)S(1)} %get-tuple-element.112.refs_9_), channel_id=1, source_target_pairs={{1,0},{2,1},{3,2},{0,3},{5,4},{6,5},{7,6},{4,7},{9,8},{10,9},{11,1... | collective-permute-start | bytes 983048 | tf_op jit(solution)/shard_map/ppermute | solution.py:359
  62.9 13.6 %collective-permute-start.21 = (f32[2,320,128]{2,1,0:T(8,128)S(1)}, f32[2,320,128]{2,1,0:T(8,128)S(1)}, u32[]{:S(2)}, u32[]{:S(2)}) collective-permute-start(f32[2,320,128]{2,1,0:T(8,128)S(1)} %get-tuple-element.129), channel_id=1, source_target_pairs={{0,16},{16,0},{1,17},{17,1},{2,18},{18,2},{3,19},{19,3},{4,20},{20... | collective-permute-start | bytes 983048 | tf_op jit(solution)/shard_map/ppermute | solution.py:361
  66.1 15.9 %collective-permute-start.22 = (f32[16,40,128]{2,1,0:T(8,128)S(1)}, f32[16,40,128]{2,1,0:T(8,128)S(1)}, u32[]{:S(2)}, u32[]{:S(2)}) collective-permute-start(f32[16,40,128]{2,1,0:T(8,128)S(1)} %get-tuple-element.130), channel_id=1, source_target_pairs={{0,1},{1,2},{2,3},{3,0},{4,5},{5,6},{6,7},{7,4},{8,9},{9,10},{10,1... | collective-permute-start | bytes 983048 | tf_op jit(solution)/shard_map/ppermute | solution.py:358
  67.9 21.2 %collective-permute-start.23 = (f32[16,40,128]{2,1,0:T(8,128)S(1)}, f32[16,40,128]{2,1,0:T(8,128)S(1)}, u32[]{:S(2)}, u32[]{:S(2)}) collective-permute-start(f32[16,40,128]{2,1,0:T(8,128)S(1)} %get-tuple-element.113.refs_9_), channel_id=1, source_target_pairs={{1,0},{2,1},{3,2},{0,3},{5,4},{6,5},{7,6},{4,7},{9,8},{10,9},{11,1... | collective-permute-start | bytes 983048 | tf_op jit(solution)/shard_map/ppermute | solution.py:359
  68.2 24.3 %collective-permute-start.15 = (f32[2,128,128]{2,1,0:T(8,128)S(1)}, f32[2,128,128]{2,1,0:T(8,128)S(1)}, u32[]{:S(2)}, u32[]{:S(2)}) collective-permute-start(f32[2,128,128]{2,1,0:T(8,128)S(1)} %get-tuple-element.118), channel_id=1, source_target_pairs={{0,16},{16,0},{1,17},{17,1},{2,18},{18,2},{3,19},{19,3},{4,20},{20... | collective-permute-start | bytes 393224 | tf_op jit(solution)/shard_map/ppermute | solution.py:361
  74.9 27.4 %collective-permute-start.18 = (f32[2,256,128]{2,1,0:T(8,128)S(1)}, f32[2,256,128]{2,1,0:T(8,128)S(1)}, u32[]{:S(2)}, u32[]{:S(2)}) collective-permute-start(f32[2,256,128]{2,1,0:T(8,128)S(1)} %get-tuple-element.124), channel_id=1, source_target_pairs={{0,16},{16,0},{1,17},{17,1},{2,18},{18,2},{3,19},{19,3},{4,20},{20... | collective-permute-start | bytes 786440 | tf_op jit(solution)/shard_map/ppermute | solution.py:361
  76.5 27.0 %collective-permute-start.19 = (f32[16,32,128]{2,1,0:T(8,128)S(1)}, f32[16,32,128]{2,1,0:T(8,128)S(1)}, u32[]{:S(2)}, u32[]{:S(2)}) collective-permute-start(f32[16,32,128]{2,1,0:T(8,128)S(1)} %get-tuple-element.125), channel_id=1, source_target_pairs={{0,1},{1,2},{2,3},{3,0},{4,5},{5,6},{6,7},{7,4},{8,9},{9,10},{10,1... | collective-permute-start | bytes 786440 | tf_op jit(solution)/shard_map/ppermute | solution.py:358
  82.0 25.3 %collective-permute-start.20 = (f32[16,32,128]{2,1,0:T(8,128)S(1)}, f32[16,32,128]{2,1,0:T(8,128)S(1)}, u32[]{:S(2)}, u32[]{:S(2)}) collective-permute-start(f32[16,32,128]{2,1,0:T(8,128)S(1)} %get-tuple-element.114.refs_9_), channel_id=1, source_target_pairs={{1,0},{2,1},{3,2},{0,3},{5,4},{6,5},{7,6},{4,7},{9,8},{10,9},{11,1... | collective-permute-start | bytes 786440 | tf_op jit(solution)/shard_map/ppermute | solution.py:359
  89.0 12.9 %collective-permute-start.16 = (f32[16,16,128]{2,1,0:T(8,128)S(1)}, f32[16,16,128]{2,1,0:T(8,128)S(1)}, u32[]{:S(2)}, u32[]{:S(2)}) collective-permute-start(f32[16,16,128]{2,1,0:T(8,128)S(1)} %get-tuple-element.119), channel_id=1, source_target_pairs={{0,1},{1,2},{2,3},{3,0},{4,5},{5,6},{6,7},{7,4},{8,9},{9,10},{10,1... | collective-permute-start | bytes 393224 | tf_op jit(solution)/shard_map/ppermute | solution.py:358
  92.4 24.4 %collective-permute-start.35 = (f32[2,320,128]{2,1,0:T(8,128)S(1)}, f32[2,320,128]{2,1,0:T(8,128)S(1)}, u32[]{:S(2)}, u32[]{:S(2)}) collective-permute-start(f32[2,320,128]{2,1,0:T(8,128)S(1)} %get-tuple-element.151), channel_id=1, source_target_pairs={{0,16},{16,0},{1,17},{17,1},{2,18},{18,2},{3,19},{19,3},{4,20},{20... | collective-permute-start | bytes 983048 | tf_op jit(solution)/shard_map/ppermute | solution.py:361
  102.0 8.2 %collective-permute-start.17 = (f32[16,16,128]{2,1,0:T(8,128)S(1)}, f32[16,16,128]{2,1,0:T(8,128)S(1)}, u32[]{:S(2)}, u32[]{:S(2)}) collective-permute-start(f32[16,16,128]{2,1,0:T(8,128)S(1)} %get-tuple-element.120.refs_9_), channel_id=1, source_target_pairs={{1,0},{2,1},{3,2},{0,3},{5,4},{6,5},{7,6},{4,7},{9,8},{10,9},{11,1... | collective-permute-start | bytes 393224 | tf_op jit(solution)/shard_map/ppermute | solution.py:359
  102.3 14.5 %collective-permute-start.39 = (f32[2,320,128]{2,1,0:T(8,128)S(1)}, f32[2,320,128]{2,1,0:T(8,128)S(1)}, u32[]{:S(2)}, u32[]{:S(2)}) collective-permute-start(f32[2,320,128]{2,1,0:T(8,128)S(1)} %get-tuple-element.154), channel_id=1, source_target_pairs={{0,16},{16,0},{1,17},{17,1},{2,18},{18,2},{3,19},{19,3},{4,20},{20... | collective-permute-start | bytes 983048 | tf_op jit(solution)/shard_map/ppermute | solution.py:361
  103.5 14.7 %collective-permute-start.40 = (f32[16,40,128]{2,1,0:T(8,128)S(1)}, f32[16,40,128]{2,1,0:T(8,128)S(1)}, u32[]{:S(2)}, u32[]{:S(2)}) collective-permute-start(f32[16,40,128]{2,1,0:T(8,128)S(1)} %get-tuple-element.155), channel_id=1, source_target_pairs={{0,1},{1,2},{2,3},{3,0},{4,5},{5,6},{6,7},{7,4},{8,9},{9,10},{10,1... | collective-permute-start | bytes 983048 | tf_op jit(solution)/shard_map/ppermute | solution.py:358
  107.3 16.9 %collective-permute-start.41 = (f32[16,40,128]{2,1,0:T(8,128)S(1)}, f32[16,40,128]{2,1,0:T(8,128)S(1)}, u32[]{:S(2)}, u32[]{:S(2)}) collective-permute-start(f32[16,40,128]{2,1,0:T(8,128)S(1)} %get-tuple-element.138.refs_9_), channel_id=1, source_target_pairs={{1,0},{2,1},{3,2},{0,3},{5,4},{6,5},{7,6},{4,7},{9,8},{10,9},{11,1... | collective-permute-start | bytes 983048 | tf_op jit(solution)/shard_map/ppermute | solution.py:359
  110.9 3.7 %collective-permute-start.38 = (f32[16,8,128]{2,1,0:T(8,128)S(1)}, f32[16,8,128]{2,1,0:T(8,128)S(1)}, u32[]{:S(2)}, u32[]{:S(2)}) collective-permute-start(f32[16,8,128]{2,1,0:T(8,128)S(1)} %get-tuple-element.153), channel_id=1, source_target_pairs={{0,4},{4,8},{8,12},{12,0},{1,5},{5,9},{9,13},{13,1},{2,6},{6,10},{... | collective-permute-start | bytes 196616 | tf_op jit(solution)/shard_map/ppermute | solution.py:370
  114.6 16.7 %collective-permute-start.36 = (f32[16,40,128]{2,1,0:T(8,128)S(1)}, f32[16,40,128]{2,1,0:T(8,128)S(1)}, u32[]{:S(2)}, u32[]{:S(2)}) collective-permute-start(f32[16,40,128]{2,1,0:T(8,128)S(1)} %get-tuple-element.152), channel_id=1, source_target_pairs={{0,1},{1,2},{2,3},{3,0},{4,5},{5,6},{6,7},{7,4},{8,9},{9,10},{10,1... | collective-permute-start | bytes 983048 | tf_op jit(solution)/shard_map/ppermute | solution.py:358
  116.8 21.5 %collective-permute-start.37 = (f32[16,40,128]{2,1,0:T(8,128)S(1)}, f32[16,40,128]{2,1,0:T(8,128)S(1)}, u32[]{:S(2)}, u32[]{:S(2)}) collective-permute-start(f32[16,40,128]{2,1,0:T(8,128)S(1)} %get-tuple-element.139.refs_9_), channel_id=1, source_target_pairs={{1,0},{2,1},{3,2},{0,3},{5,4},{6,5},{7,6},{4,7},{9,8},{10,9},{11,1... | collective-permute-start | bytes 983048 | tf_op jit(solution)/shard_map/ppermute | solution.py:359
  116.8 25.1 %collective-permute-start.32 = (f32[2,256,128]{2,1,0:T(8,128)S(1)}, f32[2,256,128]{2,1,0:T(8,128)S(1)}, u32[]{:S(2)}, u32[]{:S(2)}) collective-permute-start(f32[2,256,128]{2,1,0:T(8,128)S(1)} %get-tuple-element.148), channel_id=1, source_target_pairs={{0,16},{16,0},{1,17},{17,1},{2,18},{18,2},{3,19},{19,3},{4,20},{20... | collective-permute-start | bytes 786440 | tf_op jit(solution)/shard_map/ppermute | solution.py:361
  118.2 26.3 %collective-permute-start.33 = (f32[16,32,128]{2,1,0:T(8,128)S(1)}, f32[16,32,128]{2,1,0:T(8,128)S(1)}, u32[]{:S(2)}, u32[]{:S(2)}) collective-permute-start(f32[16,32,128]{2,1,0:T(8,128)S(1)} %get-tuple-element.149), channel_id=1, source_target_pairs={{0,1},{1,2},{2,3},{3,0},{4,5},{5,6},{6,7},{7,4},{8,9},{9,10},{10,1... | collective-permute-start | bytes 786440 | tf_op jit(solution)/shard_map/ppermute | solution.py:358
  124.2 25.4 %collective-permute-start.34 = (f32[16,32,128]{2,1,0:T(8,128)S(1)}, f32[16,32,128]{2,1,0:T(8,128)S(1)}, u32[]{:S(2)}, u32[]{:S(2)}) collective-permute-start(f32[16,32,128]{2,1,0:T(8,128)S(1)} %get-tuple-element.140.refs_9_), channel_id=1, source_target_pairs={{1,0},{2,1},{3,2},{0,3},{5,4},{6,5},{7,6},{4,7},{9,8},{10,9},{11,1... | collective-permute-start | bytes 786440 | tf_op jit(solution)/shard_map/ppermute | solution.py:359
  139.9 19.6 %collective-permute-start.49 = (f32[2,320,128]{2,1,0:T(8,128)S(1)}, f32[2,320,128]{2,1,0:T(8,128)S(1)}, u32[]{:S(2)}, u32[]{:S(2)}) collective-permute-start(f32[2,320,128]{2,1,0:T(8,128)S(1)} %get-tuple-element.169), channel_id=1, source_target_pairs={{0,16},{16,0},{1,17},{17,1},{2,18},{18,2},{3,19},{19,3},{4,20},{20... | collective-permute-start | bytes 983048 | tf_op jit(solution)/shard_map/ppermute | solution.py:361
  141.5 11.6 %collective-permute-start.29 = (f32[2,128,128]{2,1,0:T(8,128)S(1)}, f32[2,128,128]{2,1,0:T(8,128)S(1)}, u32[]{:S(2)}, u32[]{:S(2)}) collective-permute-start(f32[2,128,128]{2,1,0:T(8,128)S(1)} %get-tuple-element.144), channel_id=1, source_target_pairs={{0,16},{16,0},{1,17},{17,1},{2,18},{18,2},{3,19},{19,3},{4,20},{20... | collective-permute-start | bytes 393224 | tf_op jit(solution)/shard_map/ppermute | solution.py:361
  142.0 11.6 %collective-permute-start.30 = (f32[16,16,128]{2,1,0:T(8,128)S(1)}, f32[16,16,128]{2,1,0:T(8,128)S(1)}, u32[]{:S(2)}, u32[]{:S(2)}) collective-permute-start(f32[16,16,128]{2,1,0:T(8,128)S(1)} %get-tuple-element.145), channel_id=1, source_target_pairs={{0,1},{1,2},{2,3},{3,0},{4,5},{5,6},{6,7},{7,4},{8,9},{9,10},{10,1... | collective-permute-start | bytes 393224 | tf_op jit(solution)/shard_map/ppermute | solution.py:358
  144.5 9.3 %collective-permute-start.31 = (f32[16,16,128]{2,1,0:T(8,128)S(1)}, f32[16,16,128]{2,1,0:T(8,128)S(1)}, u32[]{:S(2)}, u32[]{:S(2)}) collective-permute-start(f32[16,16,128]{2,1,0:T(8,128)S(1)} %get-tuple-element.146.refs_9_), channel_id=1, source_target_pairs={{1,0},{2,1},{3,2},{0,3},{5,4},{6,5},{7,6},{4,7},{9,8},{10,9},{11,1... | collective-permute-start | bytes 393224 | tf_op jit(solution)/shard_map/ppermute | solution.py:359
  151.5 9.4 %collective-permute-start.53 = (f32[2,320,128]{2,1,0:T(8,128)S(1)}, f32[2,320,128]{2,1,0:T(8,128)S(1)}, u32[]{:S(2)}, u32[]{:S(2)}) collective-permute-start(f32[2,320,128]{2,1,0:T(8,128)S(1)} %get-tuple-element.172), channel_id=1, source_target_pairs={{0,16},{16,0},{1,17},{17,1},{2,18},{18,2},{3,19},{19,3},{4,20},{20... | collective-permute-start | bytes 983048 | tf_op jit(solution)/shard_map/ppermute | solution.py:361
  153.0 9.7 %collective-permute-start.54 = (f32[16,40,128]{2,1,0:T(8,128)S(1)}, f32[16,40,128]{2,1,0:T(8,128)S(1)}, u32[]{:S(2)}, u32[]{:S(2)}) collective-permute-start(f32[16,40,128]{2,1,0:T(8,128)S(1)} %get-tuple-element.173), channel_id=1, source_target_pairs={{0,1},{1,2},{2,3},{3,0},{4,5},{5,6},{6,7},{7,4},{8,9},{9,10},{10,1... | collective-permute-start | bytes 983048 | tf_op jit(solution)/shard_map/ppermute | solution.py:358
  154.5 3.7 %collective-permute-start.52 = (f32[16,8,128]{2,1,0:T(8,128)S(1)}, f32[16,8,128]{2,1,0:T(8,128)S(1)}, u32[]{:S(2)}, u32[]{:S(2)}) collective-permute-start(f32[16,8,128]{2,1,0:T(8,128)S(1)} %get-tuple-element.171), channel_id=1, source_target_pairs={{0,4},{4,8},{8,12},{12,0},{1,5},{5,9},{9,13},{13,1},{2,6},{6,10},{... | collective-permute-start | bytes 196616 | tf_op jit(solution)/shard_map/ppermute | solution.py:370
  155.7 14.3 %collective-permute-start.55 = (f32[16,40,128]{2,1,0:T(8,128)S(1)}, f32[16,40,128]{2,1,0:T(8,128)S(1)}, u32[]{:S(2)}, u32[]{:S(2)}) collective-permute-start(f32[16,40,128]{2,1,0:T(8,128)S(1)} %get-tuple-element.156.refs_9_), channel_id=1, source_target_pairs={{1,0},{2,1},{3,2},{0,3},{5,4},{6,5},{7,6},{4,7},{9,8},{10,9},{11,1... | collective-permute-start | bytes 983048 | tf_op jit(solution)/shard_map/ppermute | solution.py:359
  158.3 18.5 %collective-permute-start.50 = (f32[16,40,128]{2,1,0:T(8,128)S(1)}, f32[16,40,128]{2,1,0:T(8,128)S(1)}, u32[]{:S(2)}, u32[]{:S(2)}) collective-permute-start(f32[16,40,128]{2,1,0:T(8,128)S(1)} %get-tuple-element.170), channel_id=1, source_target_pairs={{0,1},{1,2},{2,3},{3,0},{4,5},{5,6},{6,7},{7,4},{8,9},{9,10},{10,1... | collective-permute-start | bytes 983048 | tf_op jit(solution)/shard_map/ppermute | solution.py:358
  159.5 24.5 %collective-permute-start.51 = (f32[16,40,128]{2,1,0:T(8,128)S(1)}, f32[16,40,128]{2,1,0:T(8,128)S(1)}, u32[]{:S(2)}, u32[]{:S(2)}) collective-permute-start(f32[16,40,128]{2,1,0:T(8,128)S(1)} %get-tuple-element.157.refs_9_), channel_id=1, source_target_pairs={{1,0},{2,1},{3,2},{0,3},{5,4},{6,5},{7,6},{4,7},{9,8},{10,9},{11,1... | collective-permute-start | bytes 983048 | tf_op jit(solution)/shard_map/ppermute | solution.py:359
  160.9 27.3 %collective-permute-start.46 = (f32[2,256,128]{2,1,0:T(8,128)S(1)}, f32[2,256,128]{2,1,0:T(8,128)S(1)}, u32[]{:S(2)}, u32[]{:S(2)}) collective-permute-start(f32[2,256,128]{2,1,0:T(8,128)S(1)} %get-tuple-element.166), channel_id=1, source_target_pairs={{0,16},{16,0},{1,17},{17,1},{2,18},{18,2},{3,19},{19,3},{4,20},{20... | collective-permute-start | bytes 786440 | tf_op jit(solution)/shard_map/ppermute | solution.py:361
  162.8 26.7 %collective-permute-start.47 = (f32[16,32,128]{2,1,0:T(8,128)S(1)}, f32[16,32,128]{2,1,0:T(8,128)S(1)}, u32[]{:S(2)}, u32[]{:S(2)}) collective-permute-start(f32[16,32,128]{2,1,0:T(8,128)S(1)} %get-tuple-element.167), channel_id=1, source_target_pairs={{0,1},{1,2},{2,3},{3,0},{4,5},{5,6},{6,7},{7,4},{8,9},{9,10},{10,1... | collective-permute-start | bytes 786440 | tf_op jit(solution)/shard_map/ppermute | solution.py:358
  169.9 25.4 %collective-permute-start.48 = (f32[16,32,128]{2,1,0:T(8,128)S(1)}, f32[16,32,128]{2,1,0:T(8,128)S(1)}, u32[]{:S(2)}, u32[]{:S(2)}) collective-permute-start(f32[16,32,128]{2,1,0:T(8,128)S(1)} %get-tuple-element.158.refs_9_), channel_id=1, source_target_pairs={{1,0},{2,1},{3,2},{0,3},{5,4},{6,5},{7,6},{4,7},{9,8},{10,9},{11,1... | collective-permute-start | bytes 786440 | tf_op jit(solution)/shard_map/ppermute | solution.py:359
  176.8 22.0 %collective-permute-start.65 = (f32[16,40,128]{2,1,0:T(8,128)S(1)}, f32[16,40,128]{2,1,0:T(8,128)S(1)}, u32[]{:S(2)}, u32[]{:S(2)}) collective-permute-start(f32[16,40,128]{2,1,0:T(8,128)S(1)} %get-tuple-element.184), channel_id=1, source_target_pairs={{0,1},{4,5},{8,9},{12,13},{16,17},{20,21},{24,25},{28,29}} | collective-permute-start | bytes 983048 | tf_op jit(solution)/shard_map/ppermute | solution.py:412
  187.5 12.1 %collective-permute-start.62 = (f32[16,40,128]{2,1,0:T(8,128)S(1)}, f32[16,40,128]{2,1,0:T(8,128)S(1)}, u32[]{:S(2)}, u32[]{:S(2)}) collective-permute-start(f32[16,40,128]{2,1,0:T(8,128)S(1)} %get-tuple-element.182), channel_id=1, source_target_pairs={{0,1},{4,5},{8,9},{12,13},{16,17},{20,21},{24,25},{28,29}} | collective-permute-start | bytes 983048 | tf_op jit(solution)/shard_map/ppermute | solution.py:412
  198.1 15.4 %collective-permute-start.59 = (f32[16,32,128]{2,1,0:T(8,128)S(1)}, f32[16,32,128]{2,1,0:T(8,128)S(1)}, u32[]{:S(2)}, u32[]{:S(2)}) collective-permute-start(f32[16,32,128]{2,1,0:T(8,128)S(1)} %get-tuple-element.180), channel_id=1, source_target_pairs={{0,1},{4,5},{8,9},{12,13},{16,17},{20,21},{24,25},{28,29}} | collective-permute-start | bytes 786440 | tf_op jit(solution)/shard_map/ppermute | solution.py:412
  198.9 27.0 %collective-permute-start.66 = (f32[16,40,128]{2,1,0:T(8,128)S(1)}, f32[16,40,128]{2,1,0:T(8,128)S(1)}, u32[]{:S(2)}, u32[]{:S(2)}) collective-permute-start(f32[16,40,128]{2,1,0:T(8,128)S(1)} %add.30), channel_id=1, source_target_pairs={{1,2},{5,6},{9,10},{13,14},{17,18},{21,22},{25,26},{29,30}} | collective-permute-start | bytes 983048 | tf_op jit(solution)/shard_map/ppermute | solution.py:412
  199.6 27.6 %collective-permute-start.63 = (f32[16,40,128]{2,1,0:T(8,128)S(1)}, f32[16,40,128]{2,1,0:T(8,128)S(1)}, u32[]{:S(2)}, u32[]{:S(2)}) collective-permute-start(f32[16,40,128]{2,1,0:T(8,128)S(1)} %add.28), channel_id=1, source_target_pairs={{1,2},{5,6},{9,10},{13,14},{17,18},{21,22},{25,26},{29,30}} | collective-permute-start | bytes 983048 | tf_op jit(solution)/shard_map/ppermute | solution.py:412
  200.3 13.3 %collective-permute-start.43 = (f32[2,128,128]{2,1,0:T(8,128)S(1)}, f32[2,128,128]{2,1,0:T(8,128)S(1)}, u32[]{:S(2)}, u32[]{:S(2)}) collective-permute-start(f32[2,128,128]{2,1,0:T(8,128)S(1)} %get-tuple-element.162), channel_id=1, source_target_pairs={{0,16},{16,0},{1,17},{17,1},{2,18},{18,2},{3,19},{19,3},{4,20},{20... | collective-permute-start | bytes 393224 | tf_op jit(solution)/shard_map/ppermute | solution.py:361
  204.1 12.9 %collective-permute-start.44 = (f32[16,16,128]{2,1,0:T(8,128)S(1)}, f32[16,16,128]{2,1,0:T(8,128)S(1)}, u32[]{:S(2)}, u32[]{:S(2)}) collective-permute-start(f32[16,16,128]{2,1,0:T(8,128)S(1)} %get-tuple-element.163), channel_id=1, source_target_pairs={{0,1},{1,2},{2,3},{3,0},{4,5},{5,6},{6,7},{7,4},{8,9},{9,10},{10,1... | collective-permute-start | bytes 393224 | tf_op jit(solution)/shard_map/ppermute | solution.py:358
  213.6 9.8 %collective-permute-start.45 = (f32[16,16,128]{2,1,0:T(8,128)S(1)}, f32[16,16,128]{2,1,0:T(8,128)S(1)}, u32[]{:S(2)}, u32[]{:S(2)}) collective-permute-start(f32[16,16,128]{2,1,0:T(8,128)S(1)} %get-tuple-element.164.refs_9_), channel_id=1, source_target_pairs={{1,0},{2,1},{3,2},{0,3},{5,4},{6,5},{7,6},{4,7},{9,8},{10,9},{11,1... | collective-permute-start | bytes 393224 | tf_op jit(solution)/shard_map/ppermute | solution.py:359
  213.6 15.0 %collective-permute-start.60 = (f32[16,32,128]{2,1,0:T(8,128)S(1)}, f32[16,32,128]{2,1,0:T(8,128)S(1)}, u32[]{:S(2)}, u32[]{:S(2)}) collective-permute-start(f32[16,32,128]{2,1,0:T(8,128)S(1)} %add.26), channel_id=1, source_target_pairs={{1,2},{5,6},{9,10},{13,14},{17,18},{21,22},{25,26},{29,30}} | collective-permute-start | bytes 786440 | tf_op jit(solution)/shard_map/ppermute | solution.py:412
  226.0 12.5 %collective-permute-start.67 = (f32[16,40,128]{2,1,0:T(8,128)S(1)}, f32[16,40,128]{2,1,0:T(8,128)S(1)}, u32[]{:S(2)}, u32[]{:S(2)}) collective-permute-start(f32[16,40,128]{2,1,0:T(8,128)S(1)} %add.31), channel_id=1, source_target_pairs={{2,3},{6,7},{10,11},{14,15},{18,19},{22,23},{26,27},{30,31}} | collective-permute-start | bytes 983048 | tf_op jit(solution)/shard_map/ppermute | solution.py:412
  227.3 18.1 %collective-permute-start.64 = (f32[16,40,128]{2,1,0:T(8,128)S(1)}, f32[16,40,128]{2,1,0:T(8,128)S(1)}, u32[]{:S(2)}, u32[]{:S(2)}) collective-permute-start(f32[16,40,128]{2,1,0:T(8,128)S(1)} %add.29), channel_id=1, source_target_pairs={{2,3},{6,7},{10,11},{14,15},{18,19},{22,23},{26,27},{30,31}} | collective-permute-start | bytes 983048 | tf_op jit(solution)/shard_map/ppermute | solution.py:412
  228.7 22.4 %collective-permute-start.61 = (f32[16,32,128]{2,1,0:T(8,128)S(1)}, f32[16,32,128]{2,1,0:T(8,128)S(1)}, u32[]{:S(2)}, u32[]{:S(2)}) collective-permute-start(f32[16,32,128]{2,1,0:T(8,128)S(1)} %add.27), channel_id=1, source_target_pairs={{2,3},{6,7},{10,11},{14,15},{18,19},{22,23},{26,27},{30,31}} | collective-permute-start | bytes 786440 | tf_op jit(solution)/shard_map/ppermute | solution.py:412
  230.7 22.8 %collective-permute-start.58 = (f32[16,16,128]{2,1,0:T(8,128)S(1)}, f32[16,16,128]{2,1,0:T(8,128)S(1)}, u32[]{:S(2)}, u32[]{:S(2)}) collective-permute-start(f32[16,16,128]{2,1,0:T(8,128)S(1)} %add.25), channel_id=1, source_target_pairs={{2,3},{6,7},{10,11},{14,15},{18,19},{22,23},{26,27},{30,31}} | collective-permute-start | bytes 393224 | tf_op jit(solution)/shard_map/ppermute | solution.py:412
  (4 other events, 8.7 us)

commit v3 on v2

--- a/solution.py
+++ b/solution.py
@@ -10,9 +10,9 @@
 
 STEPS = 4
 ROWS = 8
-SHARES = (5, 5, 4, 2)
+SHARES = (5, 4, 4, 3)
 GROUPS = 4
-LONGEST = 5
+PARTS = (1, 1, 1, 2)
 VMEM_LIMIT = 10 * 1024 * 1024
 
 
@@ -39,7 +39,7 @@
 
 
 def parts_of(k):
-    return max(1, math.ceil(SHARES[k] / LONGEST))
+    return PARTS[k]
 
 
 def take_rows(block, bottom, top, y, width, depth):
@@ -411,7 +411,8 @@
             for hop in range(blocks - 1):
                 arrived = lax.ppermute(carried, "pz", [(hop, hop + 1)])
                 offsets[-1].append(arrived)
-                carried = carried + arrived
+                if hop < blocks - 2:
+                    carried = carried + arrived
         potential = finish(k, fields[k], offsets, potential)
     return (potential.reshape(shape), end.reshape(shape))
 

time: 255 us -> 266 us (1.043)
  the two profiles are of different devices: /device:TPU:24 before, /device:TPU:0 now
where the time goes in v3:
time: 266 us; the launch traced here: 262 us
  waiting for transfers between devices  114 us (43%)
  starting transfers between devices  101 us (38%)
  Pallas kernels  44.9 us (17%)
    ppermute x16, waiting for transfers between devices, exchange(): from_above = lax.ppermute(bottom, 'pz', z_down)  49.3 us
    pallas_call x24, Pallas kernels, call(): pl.pallas_call(kernel, out_shape=outs, in_specs=specs, out_specs=out_spec...  44.9 us
    ppermute x16, waiting for transfers between devices, exchange(): from_below = lax.ppermute(top, 'pz', z_up)  43 us
    ppermute x16, starting transfers between devices, exchange(): from_above = lax.ppermute(bottom, 'pz', z_down)  42 us
    ppermute x16, starting transfers between devices, exchange(): rows = lax.ppermute(rows, 'py', y_up)  22.7 us
    ppermute x15, starting transfers between devices, on_device(): arrived = lax.ppermute(carried, 'pz', [(hop, hop + 1)])  22.6 us
    ppermute x16, waiting for transfers between devices, exchange(): rows = lax.ppermute(rows, 'py', y_up)  13.8 us
    ppermute x16, starting transfers between devices, exchange(): from_below = lax.ppermute(top, 'pz', z_up)  10.5 us
  transfers between devices with their start and end apart: 71, of which 28 were waited for; matrix products, arithmetic and copies ran while one was open for 0% of the time, Pallas kernels for 14%

profile of v3, /device:TPU:0, one launch (start us, length us, event | category | flops | bytes accessed | tf_op | source)
XLA Modules:
  0.0 261.6 jit_solution(12142774959266178660)
XLA Ops:
  0.6 1.8 shard_map.50
  2.4 1.6 shard_map.51
  4.0 3.1 %collective-permute-start.7 = (f32[2,256,128]{2,1,0:T(8,128)S(1)}, f32[2,256,128]{2,1,0:T(8,128)S(1)}, u32[]{:S(2)}, u32[]{:S(2)}) collective-permute-start(f32[2,256,128]{2,1,0:T(8,128)S(1)} %get-tuple-element.108), channel_id=1, source_target_pairs={{0,16},{16,0},{1,17},{17,1},{2,18},{18,2},{3,19},{19,3},{4,20},{20... | collective-permute-start | bytes 786440 | tf_op jit(solution)/shard_map/ppermute | solution.py:361
  7.1 1.6 shard_map.52
  11.1 1.7 collective-permute-start.8
  13.0 3.6 %collective-permute-start.9 = (f32[16,32,128]{2,1,0:T(8,128)S(1)}, f32[16,32,128]{2,1,0:T(8,128)S(1)}, u32[]{:S(2)}, u32[]{:S(2)}) collective-permute-start(f32[16,32,128]{2,1,0:T(8,128)S(1)} %get-tuple-element.96.refs_1_), channel_id=1, source_target_pairs={{1,0},{2,1},{3,2},{0,3},{5,4},{6,5},{7,6},{4,7},{9,8},{10,9},{11,1... | collective-permute-start | bytes 786440 | tf_op jit(solution)/shard_map/ppermute | solution.py:359
  19.5 2.4 collective-permute-start.13
  22.0 1.7 collective-permute-start.4
  23.7 4.1 %collective-permute-done.9.refs_6_ = f32[16,32,128]{2,1,0:T(8,128)S(1)} collective-permute-done((f32[16,32,128]{2,1,0:T(8,128)S(1)}, f32[16,32,128]{2,1,0:T(8,128)S(1)}, u32[]{:S(2)}, u32[]{:S(2)}) %collective-permute-start.9) | collective-permute-done | bytes 262176 | tf_op jit(solution)/shard_map/ppermute | solution.py:359
  28.3 3.3 %collective-permute-start.6 = (f32[16,32,128]{2,1,0:T(8,128)S(1)}, f32[16,32,128]{2,1,0:T(8,128)S(1)}, u32[]{:S(2)}, u32[]{:S(2)}) collective-permute-start(f32[16,32,128]{2,1,0:T(8,128)S(1)} %get-tuple-element.97.refs_1_), channel_id=1, source_target_pairs={{1,0},{2,1},{3,2},{0,3},{5,4},{6,5},{7,6},{4,7},{9,8},{10,9},{11,1... | collective-permute-start | bytes 786440 | tf_op jit(solution)/shard_map/ppermute | solution.py:359
  31.6 2.9 %collective-permute-done.12.refs_5_ = f32[16,40,128]{2,1,0:T(8,128)S(1)} collective-permute-done((f32[16,40,128]{2,1,0:T(8,128)S(1)}, f32[16,40,128]{2,1,0:T(8,128)S(1)}, u32[]{:S(2)}, u32[]{:S(2)}) %collective-permute-start.12) | collective-permute-done | bytes 327712 | tf_op jit(solution)/shard_map/ppermute | solution.py:358
  34.5 7.2 %collective-permute-done.13.refs_6_ = f32[16,40,128]{2,1,0:T(8,128)S(1)} collective-permute-done((f32[16,40,128]{2,1,0:T(8,128)S(1)}, f32[16,40,128]{2,1,0:T(8,128)S(1)}, u32[]{:S(2)}, u32[]{:S(2)}) %collective-permute-start.13) | collective-permute-done | bytes 327712 | tf_op jit(solution)/shard_map/ppermute | solution.py:359
  41.8 1.7 collective-permute-start.3
  43.4 2.9 %shard_map.54 = (f32[16,320,128]{2,1,0:T(8,128)S(1)}, f32[16,40,128]{2,1,0:T(8,128)S(1)}, f32[16,40,128]{2,1,0:T(8,128)S(1)}, f32[2,320,128]{2,1,0:T(8,128)S(1)}...) custom-call(f32[16,320,128]{2,1,0:T(8,128)S(1)} %get-tuple-element.107.refs_0_.refs_1_, ...), custom_call_target="tpu_custom_call" | custom-call | tf_op jit(solution)/shard_map/pallas_call | solution.py:254
  46.4 2.5 shard_map.55
  50.8 2.1 collective-permute-done.6.refs_6_
  52.9 1.8 collective-permute-start.23
  54.7 2.5 shard_map.56
  57.2 4.1 %collective-permute-done.3.refs_6_ = f32[16,24,128]{2,1,0:T(8,128)S(1)} collective-permute-done((f32[16,24,128]{2,1,0:T(8,128)S(1)}, f32[16,24,128]{2,1,0:T(8,128)S(1)}, u32[]{:S(2)}, u32[]{:S(2)}) %collective-permute-start.3) | collective-permute-done | bytes 196640 | tf_op jit(solution)/shard_map/ppermute | solution.py:359
  61.3 2.3 shard_map.57
  65.6 1.7 collective-permute-done.24.refs_1_
  70.2 2.3 collective-permute-done.23.refs_6_
  72.5 2.0 collective-permute-start.27
  74.8 12.2 %collective-permute-done.19.refs_5_ = f32[16,32,128]{2,1,0:T(8,128)S(1)} collective-permute-done((f32[16,32,128]{2,1,0:T(8,128)S(1)}, f32[16,32,128]{2,1,0:T(8,128)S(1)}, u32[]{:S(2)}, u32[]{:S(2)}) %collective-permute-start.19) | collective-permute-done | bytes 262176 | tf_op jit(solution)/shard_map/ppermute | solution.py:358
  87.4 3.8 %collective-permute-start.17 = (f32[16,24,128]{2,1,0:T(8,128)S(1)}, f32[16,24,128]{2,1,0:T(8,128)S(1)}, u32[]{:S(2)}, u32[]{:S(2)}) collective-permute-start(f32[16,24,128]{2,1,0:T(8,128)S(1)} %get-tuple-element.121.refs_9_), channel_id=1, source_target_pairs={{1,0},{2,1},{3,2},{0,3},{5,4},{6,5},{7,6},{4,7},{9,8},{10,9},{11,1... | collective-permute-start | bytes 589832 | tf_op jit(solution)/shard_map/ppermute | solution.py:359
  96.1 3.6 %collective-permute-done.20.refs_6_ = f32[16,32,128]{2,1,0:T(8,128)S(1)} collective-permute-done((f32[16,32,128]{2,1,0:T(8,128)S(1)}, f32[16,32,128]{2,1,0:T(8,128)S(1)}, u32[]{:S(2)}, u32[]{:S(2)}) %collective-permute-start.20) | collective-permute-done | bytes 262176 | tf_op jit(solution)/shard_map/ppermute | solution.py:359
  100.8 3.0 %collective-permute-done.16.refs_5_ = f32[16,24,128]{2,1,0:T(8,128)S(1)} collective-permute-done((f32[16,24,128]{2,1,0:T(8,128)S(1)}, f32[16,24,128]{2,1,0:T(8,128)S(1)}, u32[]{:S(2)}, u32[]{:S(2)}) %collective-permute-start.16) | collective-permute-done | bytes 196640 | tf_op jit(solution)/shard_map/ppermute | solution.py:358
  103.9 2.7 %collective-permute-done.17.refs_6_ = f32[16,24,128]{2,1,0:T(8,128)S(1)} collective-permute-done((f32[16,24,128]{2,1,0:T(8,128)S(1)}, f32[16,24,128]{2,1,0:T(8,128)S(1)}, u32[]{:S(2)}, u32[]{:S(2)}) %collective-permute-start.17) | collective-permute-done | bytes 196640 | tf_op jit(solution)/shard_map/ppermute | solution.py:359
  107.6 1.7 collective-permute-start.39
  111.1 3.3 %collective-permute-start.41 = (f32[16,40,128]{2,1,0:T(8,128)S(1)}, f32[16,40,128]{2,1,0:T(8,128)S(1)}, u32[]{:S(2)}, u32[]{:S(2)}) collective-permute-start(f32[16,40,128]{2,1,0:T(8,128)S(1)} %get-tuple-element.139.refs_9_), channel_id=1, source_target_pairs={{1,0},{2,1},{3,2},{0,3},{5,4},{6,5},{7,6},{4,7},{9,8},{10,9},{11,1... | collective-permute-start | bytes 983048 | tf_op jit(solution)/shard_map/ppermute | solution.py:359
  114.7 1.7 collective-permute-start.29
  116.4 11.4 %collective-permute-done.29.refs_3_.refs_4_ = f32[2,192,128]{2,1,0:T(8,128)S(1)} collective-permute-done((f32[2,192,128]{2,1,0:T(8,128)S(1)}, f32[2,192,128]{2,1,0:T(8,128)S(1)}, u32[]{:S(2)}, u32[]{:S(2)}) %collective-permute-start.29) | collective-permute-done | bytes 196640 | tf_op jit(solution)/shard_map/ppermute | solution.py:361
  128.4 3.3 %collective-permute-start.34 = (f32[16,32,128]{2,1,0:T(8,128)S(1)}, f32[16,32,128]{2,1,0:T(8,128)S(1)}, u32[]{:S(2)}, u32[]{:S(2)}) collective-permute-start(f32[16,32,128]{2,1,0:T(8,128)S(1)} %get-tuple-element.141.refs_9_), channel_id=1, source_target_pairs={{1,0},{2,1},{3,2},{0,3},{5,4},{6,5},{7,6},{4,7},{9,8},{10,9},{11,1... | collective-permute-start | bytes 786440 | tf_op jit(solution)/shard_map/ppermute | solution.py:359
  131.6 1.9 collective-permute-start.35
  133.5 3.8 %collective-permute-start.37 = (f32[16,32,128]{2,1,0:T(8,128)S(1)}, f32[16,32,128]{2,1,0:T(8,128)S(1)}, u32[]{:S(2)}, u32[]{:S(2)}) collective-permute-start(f32[16,32,128]{2,1,0:T(8,128)S(1)} %get-tuple-element.140.refs_9_), channel_id=1, source_target_pairs={{1,0},{2,1},{3,2},{0,3},{5,4},{6,5},{7,6},{4,7},{9,8},{10,9},{11,1... | collective-permute-start | bytes 786440 | tf_op jit(solution)/shard_map/ppermute | solution.py:359
  138.9 1.8 collective-permute-start.53
  140.7 2.9 %collective-permute-done.34.refs_6_ = f32[16,32,128]{2,1,0:T(8,128)S(1)} collective-permute-done((f32[16,32,128]{2,1,0:T(8,128)S(1)}, f32[16,32,128]{2,1,0:T(8,128)S(1)}, u32[]{:S(2)}, u32[]{:S(2)}) %collective-permute-start.34) | collective-permute-done | bytes 262176 | tf_op jit(solution)/shard_map/ppermute | solution.py:359
  144.3 3.1 %collective-permute-start.55 = (f32[16,40,128]{2,1,0:T(8,128)S(1)}, f32[16,40,128]{2,1,0:T(8,128)S(1)}, u32[]{:S(2)}, u32[]{:S(2)}) collective-permute-start(f32[16,40,128]{2,1,0:T(8,128)S(1)} %get-tuple-element.157.refs_9_), channel_id=1, source_target_pairs={{1,0},{2,1},{3,2},{0,3},{5,4},{6,5},{7,6},{4,7},{9,8},{10,9},{11,1... | collective-permute-start | bytes 983048 | tf_op jit(solution)/shard_map/ppermute | solution.py:359
  147.4 2.7 %collective-permute-done.36.refs_5_ = f32[16,32,128]{2,1,0:T(8,128)S(1)} collective-permute-done((f32[16,32,128]{2,1,0:T(8,128)S(1)}, f32[16,32,128]{2,1,0:T(8,128)S(1)}, u32[]{:S(2)}, u32[]{:S(2)}) %collective-permute-start.36) | collective-permute-done | bytes 262176 | tf_op jit(solution)/shard_map/ppermute | solution.py:358
  150.1 4.7 %collective-permute-done.37.refs_6_ = f32[16,32,128]{2,1,0:T(8,128)S(1)} collective-permute-done((f32[16,32,128]{2,1,0:T(8,128)S(1)}, f32[16,32,128]{2,1,0:T(8,128)S(1)}, u32[]{:S(2)}, u32[]{:S(2)}) %collective-permute-start.37) | collective-permute-done | bytes 262176 | tf_op jit(solution)/shard_map/ppermute | solution.py:359
  158.6 15.4 %collective-permute-done.30.refs_5_ = f32[16,24,128]{2,1,0:T(8,128)S(1)} collective-permute-done((f32[16,24,128]{2,1,0:T(8,128)S(1)}, f32[16,24,128]{2,1,0:T(8,128)S(1)}, u32[]{:S(2)}, u32[]{:S(2)}) %collective-permute-start.30) | collective-permute-done | bytes 196640 | tf_op jit(solution)/shard_map/ppermute | solution.py:358
  174.1 1.7 collective-permute-done.31.refs_6_
  176.8 3.7 %collective-permute-done.52.refs_1_ = f32[16,8,128]{2,1,0:T(8,128)S(1)} collective-permute-done((f32[16,8,128]{2,1,0:T(8,128)S(1)}, f32[16,8,128]{2,1,0:T(8,128)S(1)}, u32[]{:S(2)}, u32[]{:S(2)}) %collective-permute-start.52) | collective-permute-done | bytes 65568 | tf_op jit(solution)/shard_map/ppermute | solution.py:370
  180.5 3.5 %shard_map.66 = (f32[16,1024,128]{2,1,0:T(8,128)}, f32[16,320,128]{2,1,0:T(8,128)S(1)}, f32[16,40,128]{2,1,0:T(8,128)S(1)}) custom-call(f32[16,320,128]{2,1,0:T(8,128)S(1)} %get-tuple-element.169.refs_0_.refs_1_, f32[16,8,128]{2,1,0:T(8,128)S(1)} %collective-permute-done.52.refs_1_, f32[16,256,128]{2,1,0:T(8,128)S(1)} %get-tuple-element.166.refs_2_.refs_0_.refs_1_, ...), custom_call_target="tpu_custom_call" | custom-call | tf_op jit(solution)/shard_map/pallas_call | solution.py:254
  184.0 2.9 %collective-permute-start.68 = (f32[16,40,128]{2,1,0:T(8,128)S(1)}, f32[16,40,128]{2,1,0:T(8,128)S(1)}, u32[]{:S(2)}, u32[]{:S(2)}) collective-permute-start(f32[16,40,128]{2,1,0:T(8,128)S(1)} %get-tuple-element.186), channel_id=1, source_target_pairs={{0,1},{4,5},{8,9},{12,13},{16,17},{20,21},{24,25},{28,29}} | collective-permute-start | bytes 983048 | tf_op jit(solution)/shard_map/ppermute | solution.py:412
  186.9 1.7 collective-permute-start.49
  188.6 3.8 %collective-permute-start.51 = (f32[16,32,128]{2,1,0:T(8,128)S(1)}, f32[16,32,128]{2,1,0:T(8,128)S(1)}, u32[]{:S(2)}, u32[]{:S(2)}) collective-permute-start(f32[16,32,128]{2,1,0:T(8,128)S(1)} %get-tuple-element.158.refs_9_), channel_id=1, source_target_pairs={{1,0},{2,1},{3,2},{0,3},{5,4},{6,5},{7,6},{4,7},{9,8},{10,9},{11,1... | collective-permute-start | bytes 786440 | tf_op jit(solution)/shard_map/ppermute | solution.py:359
  192.8 2.3 collective-permute-done.49.refs_3_.refs_4_
  195.3 3.7 %collective-permute-start.48 = (f32[16,32,128]{2,1,0:T(8,128)S(1)}, f32[16,32,128]{2,1,0:T(8,128)S(1)}, u32[]{:S(2)}, u32[]{:S(2)}) collective-permute-start(f32[16,32,128]{2,1,0:T(8,128)S(1)} %get-tuple-element.159.refs_9_), channel_id=1, source_target_pairs={{1,0},{2,1},{3,2},{0,3},{5,4},{6,5},{7,6},{4,7},{9,8},{10,9},{11,1... | collective-permute-start | bytes 786440 | tf_op jit(solution)/shard_map/ppermute | solution.py:359
  201.3 5.0 %collective-permute-done.51.refs_6_ = f32[16,32,128]{2,1,0:T(8,128)S(1)} collective-permute-done((f32[16,32,128]{2,1,0:T(8,128)S(1)}, f32[16,32,128]{2,1,0:T(8,128)S(1)}, u32[]{:S(2)}, u32[]{:S(2)}) %collective-permute-start.51) | collective-permute-done | bytes 262176 | tf_op jit(solution)/shard_map/ppermute | solution.py:359
  206.2 2.8 %shard_map.67 = (f32[16,1024,128]{2,1,0:T(8,128)}, f32[16,256,128]{2,1,0:T(8,128)S(1)}, f32[16,32,128]{2,1,0:T(8,128)S(1)}) custom-call(f32[16,256,128]{2,1,0:T(8,128)S(1)} %get-tuple-element.166.refs_2_.refs_0_.refs_1_, f32[16,320,128]{2,1,0:T(8,128)S(1)} %get-tuple-element.169.refs_0_.refs_1_, ...), custom_call_target="tpu_custom_call", output_to_operand_aliasing={{0}: (9, {})} | custom-call | tf_op jit(solution)/shard_map/pallas_call | solution.py:254
  209.1 1.9 collective-permute-start.65
  211.9 5.7 %collective-permute-done.48.refs_6_ = f32[16,32,128]{2,1,0:T(8,128)S(1)} collective-permute-done((f32[16,32,128]{2,1,0:T(8,128)S(1)}, f32[16,32,128]{2,1,0:T(8,128)S(1)}, u32[]{:S(2)}, u32[]{:S(2)}) %collective-permute-start.48) | collective-permute-done | bytes 262176 | tf_op jit(solution)/shard_map/ppermute | solution.py:359
  217.5 3.0 %shard_map.68 = (f32[16,1024,128]{2,1,0:T(8,128)}, f32[16,256,128]{2,1,0:T(8,128)S(1)}, f32[16,32,128]{2,1,0:T(8,128)S(1)}) custom-call(f32[16,256,128]{2,1,0:T(8,128)S(1)} %get-tuple-element.161.refs_2_.refs_0_.refs_1_, f32[16,256,128]{2,1,0:T(8,128)S(1)} %get-tuple-element.166.refs_2_.refs_0_.refs_1_, ...), custom_call_target="tpu_custom_call", output_to_operand_aliasing={{0}: (9, {})} | custom-call | tf_op jit(solution)/shard_map/pallas_call | solution.py:254
  221.9 1.7 collective-permute-start.43
  224.3 2.2 collective-permute-done.62.refs_1_
  227.2 3.2 %collective-permute-start.44 = (f32[16,24,128]{2,1,0:T(8,128)S(1)}, f32[16,24,128]{2,1,0:T(8,128)S(1)}, u32[]{:S(2)}, u32[]{:S(2)}) collective-permute-start(f32[16,24,128]{2,1,0:T(8,128)S(1)} %get-tuple-element.164), channel_id=1, source_target_pairs={{0,1},{1,2},{2,3},{3,0},{4,5},{5,6},{6,7},{7,4},{8,9},{9,10},{10,1... | collective-permute-start | bytes 589832 | tf_op jit(solution)/shard_map/ppermute | solution.py:358
  231.9 4.3 %collective-permute-done.44.refs_5_ = f32[16,24,128]{2,1,0:T(8,128)S(1)} collective-permute-done((f32[16,24,128]{2,1,0:T(8,128)S(1)}, f32[16,24,128]{2,1,0:T(8,128)S(1)}, u32[]{:S(2)}, u32[]{:S(2)}) %collective-permute-start.44) | collective-permute-done | bytes 196640 | tf_op jit(solution)/shard_map/ppermute | solution.py:358
  236.2 2.0 collective-permute-done.45.refs_6_
  238.2 2.1 shard_map.69
  240.3 8.6 %collective-permute-start.56 = (f32[8,24,128]{2,1,0:T(8,128)S(1)}, f32[8,24,128]{2,1,0:T(8,128)S(1)}, u32[]{:S(2)}, u32[]{:S(2)}) collective-permute-start(f32[8,24,128]{2,1,0:T(8,128)S(1)} %get-tuple-element.179), channel_id=1, source_target_pairs={{0,1},{4,5},{8,9},{12,13},{16,17},{20,21},{24,25},{28,29}} | collective-permute-start | bytes 294920 | tf_op jit(solution)/shard_map/ppermute | solution.py:412
  254.5 2.1 shard_map.70.refs_4_
  256.7 1.8 shard_map.71.refs_4_
  258.5 1.8 shard_map.72.refs_7_
  (112 shorter events, 45.4 us)
Async XLA Ops:
  4.0 15.5 %collective-permute-start.7 = (f32[2,256,128]{2,1,0:T(8,128)S(1)}, f32[2,256,128]{2,1,0:T(8,128)S(1)}, u32[]{:S(2)}, u32[]{:S(2)}) collective-permute-start(f32[2,256,128]{2,1,0:T(8,128)S(1)} %get-tuple-element.108), channel_id=1, source_target_pairs={{0,16},{16,0},{1,17},{17,1},{2,18},{18,2},{3,19},{19,3},{4,20},{20... | collective-permute-start | bytes 786440 | tf_op jit(solution)/shard_map/ppermute | solution.py:361
  10.1 8.0 %collective-permute-start.1 = (f32[2,192,128]{2,1,0:T(8,128)S(1)}, f32[2,192,128]{2,1,0:T(8,128)S(1)}, u32[]{:S(2)}, u32[]{:S(2)}) collective-permute-start(f32[2,192,128]{2,1,0:T(8,128)S(1)} %get-tuple-element.101), channel_id=1, source_target_pairs={{0,16},{16,0},{1,17},{17,1},{2,18},{18,2},{3,19},{19,3},{4,20},{20... | collective-permute-start | bytes 589832 | tf_op jit(solution)/shard_map/ppermute | solution.py:361
  11.1 5.5 %collective-permute-start.10 = (f32[16,8,128]{2,1,0:T(8,128)S(1)}, f32[16,8,128]{2,1,0:T(8,128)S(1)}, u32[]{:S(2)}, u32[]{:S(2)}) collective-permute-start(f32[16,8,128]{2,1,0:T(8,128)S(1)} %get-tuple-element.110), channel_id=1, source_target_pairs={{0,4},{4,8},{8,12},{12,0},{1,5},{5,9},{9,13},{13,1},{2,6},{6,10},{... | collective-permute-start | bytes 196616 | tf_op jit(solution)/shard_map/ppermute | solution.py:370
  11.1 10.9 %collective-permute-start.8 = (f32[16,32,128]{2,1,0:T(8,128)S(1)}, f32[16,32,128]{2,1,0:T(8,128)S(1)}, u32[]{:S(2)}, u32[]{:S(2)}) collective-permute-start(f32[16,32,128]{2,1,0:T(8,128)S(1)} %get-tuple-element.109), channel_id=1, source_target_pairs={{0,1},{1,2},{2,3},{3,0},{4,5},{5,6},{6,7},{7,4},{8,9},{9,10},{10,1... | collective-permute-start | bytes 786440 | tf_op jit(solution)/shard_map/ppermute | solution.py:358
  13.0 14.8 %collective-permute-start.9 = (f32[16,32,128]{2,1,0:T(8,128)S(1)}, f32[16,32,128]{2,1,0:T(8,128)S(1)}, u32[]{:S(2)}, u32[]{:S(2)}) collective-permute-start(f32[16,32,128]{2,1,0:T(8,128)S(1)} %get-tuple-element.96.refs_1_), channel_id=1, source_target_pairs={{1,0},{2,1},{3,2},{0,3},{5,4},{6,5},{7,6},{4,7},{9,8},{10,9},{11,1... | collective-permute-start | bytes 786440 | tf_op jit(solution)/shard_map/ppermute | solution.py:359
  16.6 11.7 %collective-permute-start.11 = (f32[2,320,128]{2,1,0:T(8,128)S(1)}, f32[2,320,128]{2,1,0:T(8,128)S(1)}, u32[]{:S(2)}, u32[]{:S(2)}) collective-permute-start(f32[2,320,128]{2,1,0:T(8,128)S(1)} %get-tuple-element.111), channel_id=1, source_target_pairs={{0,16},{16,0},{1,17},{17,1},{2,18},{18,2},{3,19},{19,3},{4,20},{20... | collective-permute-start | bytes 983048 | tf_op jit(solution)/shard_map/ppermute | solution.py:361
  18.1 16.4 %collective-permute-start.12 = (f32[16,40,128]{2,1,0:T(8,128)S(1)}, f32[16,40,128]{2,1,0:T(8,128)S(1)}, u32[]{:S(2)}, u32[]{:S(2)}) collective-permute-start(f32[16,40,128]{2,1,0:T(8,128)S(1)} %get-tuple-element.112), channel_id=1, source_target_pairs={{0,1},{1,2},{2,3},{3,0},{4,5},{5,6},{6,7},{7,4},{8,9},{9,10},{10,1... | collective-permute-start | bytes 983048 | tf_op jit(solution)/shard_map/ppermute | solution.py:358
  19.5 22.2 %collective-permute-start.13 = (f32[16,40,128]{2,1,0:T(8,128)S(1)}, f32[16,40,128]{2,1,0:T(8,128)S(1)}, u32[]{:S(2)}, u32[]{:S(2)}) collective-permute-start(f32[16,40,128]{2,1,0:T(8,128)S(1)} %get-tuple-element.95.refs_1_), channel_id=1, source_target_pairs={{1,0},{2,1},{3,2},{0,3},{5,4},{6,5},{7,6},{4,7},{9,8},{10,9},{11,1... | collective-permute-start | bytes 983048 | tf_op jit(solution)/shard_map/ppermute | solution.py:359
  22.0 26.9 %collective-permute-start.4 = (f32[2,256,128]{2,1,0:T(8,128)S(1)}, f32[2,256,128]{2,1,0:T(8,128)S(1)}, u32[]{:S(2)}, u32[]{:S(2)}) collective-permute-start(f32[2,256,128]{2,1,0:T(8,128)S(1)} %get-tuple-element.105), channel_id=1, source_target_pairs={{0,16},{16,0},{1,17},{17,1},{2,18},{18,2},{3,19},{19,3},{4,20},{20... | collective-permute-start | bytes 786440 | tf_op jit(solution)/shard_map/ppermute | solution.py:361
  27.8 22.7 %collective-permute-start.5 = (f32[16,32,128]{2,1,0:T(8,128)S(1)}, f32[16,32,128]{2,1,0:T(8,128)S(1)}, u32[]{:S(2)}, u32[]{:S(2)}) collective-permute-start(f32[16,32,128]{2,1,0:T(8,128)S(1)} %get-tuple-element.106), channel_id=1, source_target_pairs={{0,1},{1,2},{2,3},{3,0},{4,5},{5,6},{6,7},{7,4},{8,9},{9,10},{10,1... | collective-permute-start | bytes 786440 | tf_op jit(solution)/shard_map/ppermute | solution.py:358
  28.3 24.6 %collective-permute-start.6 = (f32[16,32,128]{2,1,0:T(8,128)S(1)}, f32[16,32,128]{2,1,0:T(8,128)S(1)}, u32[]{:S(2)}, u32[]{:S(2)}) collective-permute-start(f32[16,32,128]{2,1,0:T(8,128)S(1)} %get-tuple-element.97.refs_1_), channel_id=1, source_target_pairs={{1,0},{2,1},{3,2},{0,3},{5,4},{6,5},{7,6},{4,7},{9,8},{10,9},{11,1... | collective-permute-start | bytes 786440 | tf_op jit(solution)/shard_map/ppermute | solution.py:359
  34.5 22.7 %collective-permute-start.2 = (f32[16,24,128]{2,1,0:T(8,128)S(1)}, f32[16,24,128]{2,1,0:T(8,128)S(1)}, u32[]{:S(2)}, u32[]{:S(2)}) collective-permute-start(f32[16,24,128]{2,1,0:T(8,128)S(1)} %get-tuple-element.102), channel_id=1, source_target_pairs={{0,1},{1,2},{2,3},{3,0},{4,5},{5,6},{6,7},{7,4},{8,9},{9,10},{10,1... | collective-permute-start | bytes 589832 | tf_op jit(solution)/shard_map/ppermute | solution.py:358
  41.8 19.6 %collective-permute-start.3 = (f32[16,24,128]{2,1,0:T(8,128)S(1)}, f32[16,24,128]{2,1,0:T(8,128)S(1)}, u32[]{:S(2)}, u32[]{:S(2)}) collective-permute-start(f32[16,24,128]{2,1,0:T(8,128)S(1)} %get-tuple-element.103), channel_id=1, source_target_pairs={{1,0},{2,1},{3,2},{0,3},{5,4},{6,5},{7,6},{4,7},{9,8},{10,9},{11,1... | collective-permute-start | bytes 589832 | tf_op jit(solution)/shard_map/ppermute | solution.py:359
  48.9 20.0 %collective-permute-start.21 = (f32[2,256,128]{2,1,0:T(8,128)S(1)}, f32[2,256,128]{2,1,0:T(8,128)S(1)}, u32[]{:S(2)}, u32[]{:S(2)}) collective-permute-start(f32[2,256,128]{2,1,0:T(8,128)S(1)} %get-tuple-element.130), channel_id=1, source_target_pairs={{0,16},{16,0},{1,17},{17,1},{2,18},{18,2},{3,19},{19,3},{4,20},{20... | collective-permute-start | bytes 786440 | tf_op jit(solution)/shard_map/ppermute | solution.py:361
  50.5 19.1 %collective-permute-start.22 = (f32[16,32,128]{2,1,0:T(8,128)S(1)}, f32[16,32,128]{2,1,0:T(8,128)S(1)}, u32[]{:S(2)}, u32[]{:S(2)}) collective-permute-start(f32[16,32,128]{2,1,0:T(8,128)S(1)} %get-tuple-element.131), channel_id=1, source_target_pairs={{0,1},{1,2},{2,3},{3,0},{4,5},{5,6},{6,7},{7,4},{8,9},{9,10},{10,1... | collective-permute-start | bytes 786440 | tf_op jit(solution)/shard_map/ppermute | solution.py:358
  52.9 19.6 %collective-permute-start.23 = (f32[16,32,128]{2,1,0:T(8,128)S(1)}, f32[16,32,128]{2,1,0:T(8,128)S(1)}, u32[]{:S(2)}, u32[]{:S(2)}) collective-permute-start(f32[16,32,128]{2,1,0:T(8,128)S(1)} %get-tuple-element.114.refs_9_), channel_id=1, source_target_pairs={{1,0},{2,1},{3,2},{0,3},{5,4},{6,5},{7,6},{4,7},{9,8},{10,9},{11,1... | collective-permute-start | bytes 786440 | tf_op jit(solution)/shard_map/ppermute | solution.py:359
  64.1 10.3 %collective-permute-start.18 = (f32[2,256,128]{2,1,0:T(8,128)S(1)}, f32[2,256,128]{2,1,0:T(8,128)S(1)}, u32[]{:S(2)}, u32[]{:S(2)}) collective-permute-start(f32[2,256,128]{2,1,0:T(8,128)S(1)} %get-tuple-element.125), channel_id=1, source_target_pairs={{0,16},{16,0},{1,17},{17,1},{2,18},{18,2},{3,19},{19,3},{4,20},{20... | collective-permute-start | bytes 786440 | tf_op jit(solution)/shard_map/ppermute | solution.py:361
  67.3 20.1 %collective-permute-start.25 = (f32[2,320,128]{2,1,0:T(8,128)S(1)}, f32[2,320,128]{2,1,0:T(8,128)S(1)}, u32[]{:S(2)}, u32[]{:S(2)}) collective-permute-start(f32[2,320,128]{2,1,0:T(8,128)S(1)} %get-tuple-element.135), channel_id=1, source_target_pairs={{0,16},{16,0},{1,17},{17,1},{2,18},{18,2},{3,19},{19,3},{4,20},{20... | collective-permute-start | bytes 983048 | tf_op jit(solution)/shard_map/ppermute | solution.py:361
  68.9 18.5 %collective-permute-start.26 = (f32[16,40,128]{2,1,0:T(8,128)S(1)}, f32[16,40,128]{2,1,0:T(8,128)S(1)}, u32[]{:S(2)}, u32[]{:S(2)}) collective-permute-start(f32[16,40,128]{2,1,0:T(8,128)S(1)} %get-tuple-element.136), channel_id=1, source_target_pairs={{0,1},{1,2},{2,3},{3,0},{4,5},{5,6},{6,7},{7,4},{8,9},{9,10},{10,1... | collective-permute-start | bytes 983048 | tf_op jit(solution)/shard_map/ppermute | solution.py:358
  69.5 17.4 %collective-permute-start.19 = (f32[16,32,128]{2,1,0:T(8,128)S(1)}, f32[16,32,128]{2,1,0:T(8,128)S(1)}, u32[]{:S(2)}, u32[]{:S(2)}) collective-permute-start(f32[16,32,128]{2,1,0:T(8,128)S(1)} %get-tuple-element.126), channel_id=1, source_target_pairs={{0,1},{1,2},{2,3},{3,0},{4,5},{5,6},{6,7},{7,4},{8,9},{9,10},{10,1... | collective-permute-start | bytes 786440 | tf_op jit(solution)/shard_map/ppermute | solution.py:358
  72.5 20.0 %collective-permute-start.27 = (f32[16,40,128]{2,1,0:T(8,128)S(1)}, f32[16,40,128]{2,1,0:T(8,128)S(1)}, u32[]{:S(2)}, u32[]{:S(2)}) collective-permute-start(f32[16,40,128]{2,1,0:T(8,128)S(1)} %get-tuple-element.113.refs_9_), channel_id=1, source_target_pairs={{1,0},{2,1},{3,2},{0,3},{5,4},{6,5},{7,6},{4,7},{9,8},{10,9},{11,1... | collective-permute-start | bytes 983048 | tf_op jit(solution)/shard_map/ppermute | solution.py:359
  74.5 25.2 %collective-permute-start.20 = (f32[16,32,128]{2,1,0:T(8,128)S(1)}, f32[16,32,128]{2,1,0:T(8,128)S(1)}, u32[]{:S(2)}, u32[]{:S(2)}) collective-permute-start(f32[16,32,128]{2,1,0:T(8,128)S(1)} %get-tuple-element.115.refs_9_), channel_id=1, source_target_pairs={{1,0},{2,1},{3,2},{0,3},{5,4},{6,5},{7,6},{4,7},{9,8},{10,9},{11,1... | collective-permute-start | bytes 786440 | tf_op jit(solution)/shard_map/ppermute | solution.py:359
  87.0 13.9 %collective-permute-start.15 = (f32[2,192,128]{2,1,0:T(8,128)S(1)}, f32[2,192,128]{2,1,0:T(8,128)S(1)}, u32[]{:S(2)}, u32[]{:S(2)}) collective-permute-start(f32[2,192,128]{2,1,0:T(8,128)S(1)} %get-tuple-element.119), channel_id=1, source_target_pairs={{0,16},{16,0},{1,17},{17,1},{2,18},{18,2},{3,19},{19,3},{4,20},{20... | collective-permute-start | bytes 589832 | tf_op jit(solution)/shard_map/ppermute | solution.py:361
  87.4 16.5 %collective-permute-start.16 = (f32[16,24,128]{2,1,0:T(8,128)S(1)}, f32[16,24,128]{2,1,0:T(8,128)S(1)}, u32[]{:S(2)}, u32[]{:S(2)}) collective-permute-start(f32[16,24,128]{2,1,0:T(8,128)S(1)} %get-tuple-element.120), channel_id=1, source_target_pairs={{0,1},{1,2},{2,3},{3,0},{4,5},{5,6},{6,7},{7,4},{8,9},{9,10},{10,1... | collective-permute-start | bytes 589832 | tf_op jit(solution)/shard_map/ppermute | solution.py:358
  87.4 19.1 %collective-permute-start.17 = (f32[16,24,128]{2,1,0:T(8,128)S(1)}, f32[16,24,128]{2,1,0:T(8,128)S(1)}, u32[]{:S(2)}, u32[]{:S(2)}) collective-permute-start(f32[16,24,128]{2,1,0:T(8,128)S(1)} %get-tuple-element.121.refs_9_), channel_id=1, source_target_pairs={{1,0},{2,1},{3,2},{0,3},{5,4},{6,5},{7,6},{4,7},{9,8},{10,9},{11,1... | collective-permute-start | bytes 589832 | tf_op jit(solution)/shard_map/ppermute | solution.py:359
  92.5 8.3 %collective-permute-start.14 = (f32[16,8,128]{2,1,0:T(8,128)S(1)}, f32[16,8,128]{2,1,0:T(8,128)S(1)}, u32[]{:S(2)}, u32[]{:S(2)}) collective-permute-start(f32[16,8,128]{2,1,0:T(8,128)S(1)} %get-tuple-element.118), channel_id=1, source_target_pairs={{4,0},{8,4},{12,8},{0,12},{5,1},{9,5},{13,9},{1,13},{6,2},{10,6},{... | collective-permute-start | bytes 196616 | tf_op jit(solution)/shard_map/ppermute | solution.py:368
  107.6 6.8 %collective-permute-start.38 = (f32[16,8,128]{2,1,0:T(8,128)S(1)}, f32[16,8,128]{2,1,0:T(8,128)S(1)}, u32[]{:S(2)}, u32[]{:S(2)}) collective-permute-start(f32[16,8,128]{2,1,0:T(8,128)S(1)} %get-tuple-element.154), channel_id=1, source_target_pairs={{0,4},{4,8},{8,12},{12,0},{1,5},{5,9},{9,13},{13,1},{2,6},{6,10},{... | collective-permute-start | bytes 196616 | tf_op jit(solution)/shard_map/ppermute | solution.py:370
  107.6 24.0 %collective-permute-start.39 = (f32[2,320,128]{2,1,0:T(8,128)S(1)}, f32[2,320,128]{2,1,0:T(8,128)S(1)}, u32[]{:S(2)}, u32[]{:S(2)}) collective-permute-start(f32[2,320,128]{2,1,0:T(8,128)S(1)} %get-tuple-element.155), channel_id=1, source_target_pairs={{0,16},{16,0},{1,17},{17,1},{2,18},{18,2},{3,19},{19,3},{4,20},{20... | collective-permute-start | bytes 983048 | tf_op jit(solution)/shard_map/ppermute | solution.py:361
  109.4 24.1 %collective-permute-start.40 = (f32[16,40,128]{2,1,0:T(8,128)S(1)}, f32[16,40,128]{2,1,0:T(8,128)S(1)}, u32[]{:S(2)}, u32[]{:S(2)}) collective-permute-start(f32[16,40,128]{2,1,0:T(8,128)S(1)} %get-tuple-element.156), channel_id=1, source_target_pairs={{0,1},{1,2},{2,3},{3,0},{4,5},{5,6},{6,7},{7,4},{8,9},{9,10},{10,1... | collective-permute-start | bytes 983048 | tf_op jit(solution)/shard_map/ppermute | solution.py:358
  111.1 22.5 %collective-permute-start.41 = (f32[16,40,128]{2,1,0:T(8,128)S(1)}, f32[16,40,128]{2,1,0:T(8,128)S(1)}, u32[]{:S(2)}, u32[]{:S(2)}) collective-permute-start(f32[16,40,128]{2,1,0:T(8,128)S(1)} %get-tuple-element.139.refs_9_), channel_id=1, source_target_pairs={{1,0},{2,1},{3,2},{0,3},{5,4},{6,5},{7,6},{4,7},{9,8},{10,9},{11,1... | collective-permute-start | bytes 983048 | tf_op jit(solution)/shard_map/ppermute | solution.py:359
  114.3 14.0 %collective-permute-start.32 = (f32[2,256,128]{2,1,0:T(8,128)S(1)}, f32[2,256,128]{2,1,0:T(8,128)S(1)}, u32[]{:S(2)}, u32[]{:S(2)}) collective-permute-start(f32[2,256,128]{2,1,0:T(8,128)S(1)} %get-tuple-element.149), channel_id=1, source_target_pairs={{0,16},{16,0},{1,17},{17,1},{2,18},{18,2},{3,19},{19,3},{4,20},{20... | collective-permute-start | bytes 786440 | tf_op jit(solution)/shard_map/ppermute | solution.py:361
  114.7 13.2 %collective-permute-start.29 = (f32[2,192,128]{2,1,0:T(8,128)S(1)}, f32[2,192,128]{2,1,0:T(8,128)S(1)}, u32[]{:S(2)}, u32[]{:S(2)}) collective-permute-start(f32[2,192,128]{2,1,0:T(8,128)S(1)} %get-tuple-element.145), channel_id=1, source_target_pairs={{0,16},{16,0},{1,17},{17,1},{2,18},{18,2},{3,19},{19,3},{4,20},{20... | collective-permute-start | bytes 589832 | tf_op jit(solution)/shard_map/ppermute | solution.py:361
  127.8 11.1 %collective-permute-start.33 = (f32[16,32,128]{2,1,0:T(8,128)S(1)}, f32[16,32,128]{2,1,0:T(8,128)S(1)}, u32[]{:S(2)}, u32[]{:S(2)}) collective-permute-start(f32[16,32,128]{2,1,0:T(8,128)S(1)} %get-tuple-element.150), channel_id=1, source_target_pairs={{0,1},{1,2},{2,3},{3,0},{4,5},{5,6},{6,7},{7,4},{8,9},{9,10},{10,1... | collective-permute-start | bytes 786440 | tf_op jit(solution)/shard_map/ppermute | solution.py:358
  128.4 15.2 %collective-permute-start.34 = (f32[16,32,128]{2,1,0:T(8,128)S(1)}, f32[16,32,128]{2,1,0:T(8,128)S(1)}, u32[]{:S(2)}, u32[]{:S(2)}) collective-permute-start(f32[16,32,128]{2,1,0:T(8,128)S(1)} %get-tuple-element.141.refs_9_), channel_id=1, source_target_pairs={{1,0},{2,1},{3,2},{0,3},{5,4},{6,5},{7,6},{4,7},{9,8},{10,9},{11,1... | collective-permute-start | bytes 786440 | tf_op jit(solution)/shard_map/ppermute | solution.py:359
  131.6 12.7 %collective-permute-start.35 = (f32[2,256,128]{2,1,0:T(8,128)S(1)}, f32[2,256,128]{2,1,0:T(8,128)S(1)}, u32[]{:S(2)}, u32[]{:S(2)}) collective-permute-start(f32[2,256,128]{2,1,0:T(8,128)S(1)} %get-tuple-element.152), channel_id=1, source_target_pairs={{0,16},{16,0},{1,17},{17,1},{2,18},{18,2},{3,19},{19,3},{4,20},{20... | collective-permute-start | bytes 786440 | tf_op jit(solution)/shard_map/ppermute | solution.py:361
  133.5 16.6 %collective-permute-start.36 = (f32[16,32,128]{2,1,0:T(8,128)S(1)}, f32[16,32,128]{2,1,0:T(8,128)S(1)}, u32[]{:S(2)}, u32[]{:S(2)}) collective-permute-start(f32[16,32,128]{2,1,0:T(8,128)S(1)} %get-tuple-element.153), channel_id=1, source_target_pairs={{0,1},{1,2},{2,3},{3,0},{4,5},{5,6},{6,7},{7,4},{8,9},{9,10},{10,1... | collective-permute-start | bytes 786440 | tf_op jit(solution)/shard_map/ppermute | solution.py:358
  133.5 21.2 %collective-permute-start.37 = (f32[16,32,128]{2,1,0:T(8,128)S(1)}, f32[16,32,128]{2,1,0:T(8,128)S(1)}, u32[]{:S(2)}, u32[]{:S(2)}) collective-permute-start(f32[16,32,128]{2,1,0:T(8,128)S(1)} %get-tuple-element.140.refs_9_), channel_id=1, source_target_pairs={{1,0},{2,1},{3,2},{0,3},{5,4},{6,5},{7,6},{4,7},{9,8},{10,9},{11,1... | collective-permute-start | bytes 786440 | tf_op jit(solution)/shard_map/ppermute | solution.py:359
  138.9 41.6 %collective-permute-start.53 = (f32[2,320,128]{2,1,0:T(8,128)S(1)}, f32[2,320,128]{2,1,0:T(8,128)S(1)}, u32[]{:S(2)}, u32[]{:S(2)}) collective-permute-start(f32[2,320,128]{2,1,0:T(8,128)S(1)} %get-tuple-element.173), channel_id=1, source_target_pairs={{0,16},{16,0},{1,17},{17,1},{2,18},{18,2},{3,19},{19,3},{4,20},{20... | collective-permute-start | bytes 983048 | tf_op jit(solution)/shard_map/ppermute | solution.py:361
  143.6 36.9 %collective-permute-start.54 = (f32[16,40,128]{2,1,0:T(8,128)S(1)}, f32[16,40,128]{2,1,0:T(8,128)S(1)}, u32[]{:S(2)}, u32[]{:S(2)}) collective-permute-start(f32[16,40,128]{2,1,0:T(8,128)S(1)} %get-tuple-element.174), channel_id=1, source_target_pairs={{0,1},{1,2},{2,3},{3,0},{4,5},{5,6},{6,7},{7,4},{8,9},{9,10},{10,1... | collective-permute-start | bytes 983048 | tf_op jit(solution)/shard_map/ppermute | solution.py:358
  144.3 36.2 %collective-permute-start.55 = (f32[16,40,128]{2,1,0:T(8,128)S(1)}, f32[16,40,128]{2,1,0:T(8,128)S(1)}, u32[]{:S(2)}, u32[]{:S(2)}) collective-permute-start(f32[16,40,128]{2,1,0:T(8,128)S(1)} %get-tuple-element.157.refs_9_), channel_id=1, source_target_pairs={{1,0},{2,1},{3,2},{0,3},{5,4},{6,5},{7,6},{4,7},{9,8},{10,9},{11,1... | collective-permute-start | bytes 983048 | tf_op jit(solution)/shard_map/ppermute | solution.py:359
  150.1 24.0 %collective-permute-start.30 = (f32[16,24,128]{2,1,0:T(8,128)S(1)}, f32[16,24,128]{2,1,0:T(8,128)S(1)}, u32[]{:S(2)}, u32[]{:S(2)}) collective-permute-start(f32[16,24,128]{2,1,0:T(8,128)S(1)} %get-tuple-element.146), channel_id=1, source_target_pairs={{0,1},{1,2},{2,3},{3,0},{4,5},{5,6},{6,7},{7,4},{8,9},{9,10},{10,1... | collective-permute-start | bytes 589832 | tf_op jit(solution)/shard_map/ppermute | solution.py:358
  154.8 21.0 %collective-permute-start.31 = (f32[16,24,128]{2,1,0:T(8,128)S(1)}, f32[16,24,128]{2,1,0:T(8,128)S(1)}, u32[]{:S(2)}, u32[]{:S(2)}) collective-permute-start(f32[16,24,128]{2,1,0:T(8,128)S(1)} %get-tuple-element.147.refs_9_), channel_id=1, source_target_pairs={{1,0},{2,1},{3,2},{0,3},{5,4},{6,5},{7,6},{4,7},{9,8},{10,9},{11,1... | collective-permute-start | bytes 589832 | tf_op jit(solution)/shard_map/ppermute | solution.py:359
  184.0 11.3 %collective-permute-start.68 = (f32[16,40,128]{2,1,0:T(8,128)S(1)}, f32[16,40,128]{2,1,0:T(8,128)S(1)}, u32[]{:S(2)}, u32[]{:S(2)}) collective-permute-start(f32[16,40,128]{2,1,0:T(8,128)S(1)} %get-tuple-element.186), channel_id=1, source_target_pairs={{0,1},{4,5},{8,9},{12,13},{16,17},{20,21},{24,25},{28,29}} | collective-permute-start | bytes 983048 | tf_op jit(solution)/shard_map/ppermute | solution.py:412
  186.9 8.3 %collective-permute-start.49 = (f32[2,256,128]{2,1,0:T(8,128)S(1)}, f32[2,256,128]{2,1,0:T(8,128)S(1)}, u32[]{:S(2)}, u32[]{:S(2)}) collective-permute-start(f32[2,256,128]{2,1,0:T(8,128)S(1)} %get-tuple-element.170), channel_id=1, source_target_pairs={{0,16},{16,0},{1,17},{17,1},{2,18},{18,2},{3,19},{19,3},{4,20},{20... | collective-permute-start | bytes 786440 | tf_op jit(solution)/shard_map/ppermute | solution.py:361
  188.6 12.0 %collective-permute-start.50 = (f32[16,32,128]{2,1,0:T(8,128)S(1)}, f32[16,32,128]{2,1,0:T(8,128)S(1)}, u32[]{:S(2)}, u32[]{:S(2)}) collective-permute-start(f32[16,32,128]{2,1,0:T(8,128)S(1)} %get-tuple-element.171), channel_id=1, source_target_pairs={{0,1},{1,2},{2,3},{3,0},{4,5},{5,6},{6,7},{7,4},{8,9},{9,10},{10,1... | collective-permute-start | bytes 786440 | tf_op jit(solution)/shard_map/ppermute | solution.py:358
  188.6 17.7 %collective-permute-start.51 = (f32[16,32,128]{2,1,0:T(8,128)S(1)}, f32[16,32,128]{2,1,0:T(8,128)S(1)}, u32[]{:S(2)}, u32[]{:S(2)}) collective-permute-start(f32[16,32,128]{2,1,0:T(8,128)S(1)} %get-tuple-element.158.refs_9_), channel_id=1, source_target_pairs={{1,0},{2,1},{3,2},{0,3},{5,4},{6,5},{7,6},{4,7},{9,8},{10,9},{11,1... | collective-permute-start | bytes 786440 | tf_op jit(solution)/shard_map/ppermute | solution.py:359
  192.4 18.6 %collective-permute-start.46 = (f32[2,256,128]{2,1,0:T(8,128)S(1)}, f32[2,256,128]{2,1,0:T(8,128)S(1)}, u32[]{:S(2)}, u32[]{:S(2)}) collective-permute-start(f32[2,256,128]{2,1,0:T(8,128)S(1)} %get-tuple-element.167), channel_id=1, source_target_pairs={{0,16},{16,0},{1,17},{17,1},{2,18},{18,2},{3,19},{19,3},{4,20},{20... | collective-permute-start | bytes 786440 | tf_op jit(solution)/shard_map/ppermute | solution.py:361
  195.2 16.7 %collective-permute-start.47 = (f32[16,32,128]{2,1,0:T(8,128)S(1)}, f32[16,32,128]{2,1,0:T(8,128)S(1)}, u32[]{:S(2)}, u32[]{:S(2)}) collective-permute-start(f32[16,32,128]{2,1,0:T(8,128)S(1)} %get-tuple-element.168), channel_id=1, source_target_pairs={{0,1},{1,2},{2,3},{3,0},{4,5},{5,6},{6,7},{7,4},{8,9},{9,10},{10,1... | collective-permute-start | bytes 786440 | tf_op jit(solution)/shard_map/ppermute | solution.py:358
  195.3 22.2 %collective-permute-start.48 = (f32[16,32,128]{2,1,0:T(8,128)S(1)}, f32[16,32,128]{2,1,0:T(8,128)S(1)}, u32[]{:S(2)}, u32[]{:S(2)}) collective-permute-start(f32[16,32,128]{2,1,0:T(8,128)S(1)} %get-tuple-element.159.refs_9_), channel_id=1, source_target_pairs={{1,0},{2,1},{3,2},{0,3},{5,4},{6,5},{7,6},{4,7},{9,8},{10,9},{11,1... | collective-permute-start | bytes 786440 | tf_op jit(solution)/shard_map/ppermute | solution.py:359
  200.6 29.8 %collective-permute-start.69 = (f32[16,40,128]{2,1,0:T(8,128)S(1)}, f32[16,40,128]{2,1,0:T(8,128)S(1)}, u32[]{:S(2)}, u32[]{:S(2)}) collective-permute-start(f32[16,40,128]{2,1,0:T(8,128)S(1)} %add.38), channel_id=1, source_target_pairs={{1,2},{5,6},{9,10},{13,14},{17,18},{21,22},{25,26},{29,30}} | collective-permute-start | bytes 983048 | tf_op jit(solution)/shard_map/ppermute | solution.py:412
  209.1 14.5 %collective-permute-start.65 = (f32[16,32,128]{2,1,0:T(8,128)S(1)}, f32[16,32,128]{2,1,0:T(8,128)S(1)}, u32[]{:S(2)}, u32[]{:S(2)}) collective-permute-start(f32[16,32,128]{2,1,0:T(8,128)S(1)} %get-tuple-element.184), channel_id=1, source_target_pairs={{0,1},{4,5},{8,9},{12,13},{16,17},{20,21},{24,25},{28,29}} | collective-permute-start | bytes 786440 | tf_op jit(solution)/shard_map/ppermute | solution.py:412
  220.5 6.0 %collective-permute-start.62 = (f32[16,32,128]{2,1,0:T(8,128)S(1)}, f32[16,32,128]{2,1,0:T(8,128)S(1)}, u32[]{:S(2)}, u32[]{:S(2)}) collective-permute-start(f32[16,32,128]{2,1,0:T(8,128)S(1)} %get-tuple-element.182), channel_id=1, source_target_pairs={{0,1},{4,5},{8,9},{12,13},{16,17},{20,21},{24,25},{28,29}} | collective-permute-start | bytes 786440 | tf_op jit(solution)/shard_map/ppermute | solution.py:412
  221.9 5.4 %collective-permute-start.42 = (f32[16,8,128]{2,1,0:T(8,128)S(1)}, f32[16,8,128]{2,1,0:T(8,128)S(1)}, u32[]{:S(2)}, u32[]{:S(2)}) collective-permute-start(f32[16,8,128]{2,1,0:T(8,128)S(1)} %get-tuple-element.162), channel_id=1, source_target_pairs={{4,0},{8,4},{12,8},{0,12},{5,1},{9,5},{13,9},{1,13},{6,2},{10,6},{... | collective-permute-start | bytes 196616 | tf_op jit(solution)/shard_map/ppermute | solution.py:368
  221.9 9.3 %collective-permute-start.43 = (f32[2,192,128]{2,1,0:T(8,128)S(1)}, f32[2,192,128]{2,1,0:T(8,128)S(1)}, u32[]{:S(2)}, u32[]{:S(2)}) collective-permute-start(f32[2,192,128]{2,1,0:T(8,128)S(1)} %get-tuple-element.163), channel_id=1, source_target_pairs={{0,16},{16,0},{1,17},{17,1},{2,18},{18,2},{3,19},{19,3},{4,20},{20... | collective-permute-start | bytes 589832 | tf_op jit(solution)/shard_map/ppermute | solution.py:361
  223.6 26.6 %collective-permute-start.66 = (f32[16,32,128]{2,1,0:T(8,128)S(1)}, f32[16,32,128]{2,1,0:T(8,128)S(1)}, u32[]{:S(2)}, u32[]{:S(2)}) collective-permute-start(f32[16,32,128]{2,1,0:T(8,128)S(1)} %add.36), channel_id=1, source_target_pairs={{1,2},{5,6},{9,10},{13,14},{17,18},{21,22},{25,26},{29,30}} | collective-permute-start | bytes 786440 | tf_op jit(solution)/shard_map/ppermute | solution.py:412
  226.6 24.4 %collective-permute-start.63 = (f32[16,32,128]{2,1,0:T(8,128)S(1)}, f32[16,32,128]{2,1,0:T(8,128)S(1)}, u32[]{:S(2)}, u32[]{:S(2)}) collective-permute-start(f32[16,32,128]{2,1,0:T(8,128)S(1)} %add.34), channel_id=1, source_target_pairs={{1,2},{5,6},{9,10},{13,14},{17,18},{21,22},{25,26},{29,30}} | collective-permute-start | bytes 786440 | tf_op jit(solution)/shard_map/ppermute | solution.py:412
  227.2 8.9 %collective-permute-start.44 = (f32[16,24,128]{2,1,0:T(8,128)S(1)}, f32[16,24,128]{2,1,0:T(8,128)S(1)}, u32[]{:S(2)}, u32[]{:S(2)}) collective-permute-start(f32[16,24,128]{2,1,0:T(8,128)S(1)} %get-tuple-element.164), channel_id=1, source_target_pairs={{0,1},{1,2},{2,3},{3,0},{4,5},{5,6},{6,7},{7,4},{8,9},{9,10},{10,1... | collective-permute-start | bytes 589832 | tf_op jit(solution)/shard_map/ppermute | solution.py:358
  230.4 7.8 %collective-permute-start.45 = (f32[16,24,128]{2,1,0:T(8,128)S(1)}, f32[16,24,128]{2,1,0:T(8,128)S(1)}, u32[]{:S(2)}, u32[]{:S(2)}) collective-permute-start(f32[16,24,128]{2,1,0:T(8,128)S(1)} %get-tuple-element.165.refs_9_), channel_id=1, source_target_pairs={{1,0},{2,1},{3,2},{0,3},{5,4},{6,5},{7,6},{4,7},{9,8},{10,9},{11,1... | collective-permute-start | bytes 589832 | tf_op jit(solution)/shard_map/ppermute | solution.py:359
  231.2 23.3 %collective-permute-start.70 = (f32[16,40,128]{2,1,0:T(8,128)S(1)}, f32[16,40,128]{2,1,0:T(8,128)S(1)}, u32[]{:S(2)}, u32[]{:S(2)}) collective-permute-start(f32[16,40,128]{2,1,0:T(8,128)S(1)} %add.39), channel_id=1, source_target_pairs={{2,3},{6,7},{10,11},{14,15},{18,19},{22,23},{26,27},{30,31}} | collective-permute-start | bytes 983048 | tf_op jit(solution)/shard_map/ppermute | solution.py:412
  240.3 11.4 %collective-permute-start.56 = (f32[8,24,128]{2,1,0:T(8,128)S(1)}, f32[8,24,128]{2,1,0:T(8,128)S(1)}, u32[]{:S(2)}, u32[]{:S(2)}) collective-permute-start(f32[8,24,128]{2,1,0:T(8,128)S(1)} %get-tuple-element.179), channel_id=1, source_target_pairs={{0,1},{4,5},{8,9},{12,13},{16,17},{20,21},{24,25},{28,29}} | collective-permute-start | bytes 294920 | tf_op jit(solution)/shard_map/ppermute | solution.py:412
  250.3 6.4 %collective-permute-start.67 = (f32[16,32,128]{2,1,0:T(8,128)S(1)}, f32[16,32,128]{2,1,0:T(8,128)S(1)}, u32[]{:S(2)}, u32[]{:S(2)}) collective-permute-start(f32[16,32,128]{2,1,0:T(8,128)S(1)} %add.37), channel_id=1, source_target_pairs={{2,3},{6,7},{10,11},{14,15},{18,19},{22,23},{26,27},{30,31}} | collective-permute-start | bytes 786440 | tf_op jit(solution)/shard_map/ppermute | solution.py:412
  251.0 7.4 %collective-permute-start.64 = (f32[16,32,128]{2,1,0:T(8,128)S(1)}, f32[16,32,128]{2,1,0:T(8,128)S(1)}, u32[]{:S(2)}, u32[]{:S(2)}) collective-permute-start(f32[16,32,128]{2,1,0:T(8,128)S(1)} %add.35), channel_id=1, source_target_pairs={{2,3},{6,7},{10,11},{14,15},{18,19},{22,23},{26,27},{30,31}} | collective-permute-start | bytes 786440 | tf_op jit(solution)/shard_map/ppermute | solution.py:412
  253.1 7.1 %collective-permute-start.58 = (f32[8,24,128]{2,1,0:T(8,128)S(1)}, f32[8,24,128]{2,1,0:T(8,128)S(1)}, u32[]{:S(2)}, u32[]{:S(2)}) collective-permute-start(f32[8,24,128]{2,1,0:T(8,128)S(1)} %add.31), channel_id=1, source_target_pairs={{2,3},{6,7},{10,11},{14,15},{18,19},{22,23},{26,27},{30,31}} | collective-permute-start | bytes 294920 | tf_op jit(solution)/shard_map/ppermute | solution.py:412
  253.9 6.4 %collective-permute-start.61 = (f32[8,24,128]{2,1,0:T(8,128)S(1)}, f32[8,24,128]{2,1,0:T(8,128)S(1)}, u32[]{:S(2)}, u32[]{:S(2)}) collective-permute-start(f32[8,24,128]{2,1,0:T(8,128)S(1)} %add.33), channel_id=1, source_target_pairs={{2,3},{6,7},{10,11},{14,15},{18,19},{22,23},{26,27},{30,31}} | collective-permute-start | bytes 294920 | tf_op jit(solution)/shard_map/ppermute | solution.py:412
  (7 other events, 21.2 us)
